TPU v7x, 32 devices: a whole 2x2x4 slice. The times are simulated.
32 devices in a mesh: pool: 8 (over z, y), band: 4 (over x, core).
Axes of the slice: x: 2, y: 2, z: 4, core: 2. Of those that a mesh axis runs over, the one named last changes fastest.
Arguments:
- orbitals: bfloat16 [8, 4, 2, 46656], P('pool', 'band'), may hold values from -6 to 6
- occupation: int32 [8, 4], P('pool', 'band'), may hold values from 1 to 2
- kernel: float32 [46656], replicated, may hold values from 0.02 to 2
Outputs:
- exchanged: bfloat16 [8, 4, 2, 46656], P('pool', 'band')
- gram_matrix: float32 [8, 2, 4, 4], P('pool', None, None, 'band')
All inputs are finite; a program needn't handle non-finite values.
Results may differ from a plain program's by a relative error of at most 0.013.
Values may be sent and summed in bfloat16 or wider, within the bound.
No kernel may reach another device: no remote copies, remote signals or barrier semaphores. Data moves between devices by JAX's collectives and lax.ppermute only.
A program may use at most 64 MiB of HBM per device.

v0:
```python
import math

import jax
import jax.numpy as jnp
from jax import lax
from jax.sharding import PartitionSpec as P

NG = 36
GRID = 46656


def shifted(array, axis, by):
    length = lax.axis_size(axis)
    return lax.ppermute(array, axis, [(i, (i + by) % length) for i in range(length)])


def dft_matrix(direction):
    points = jnp.arange(NG, dtype=jnp.int32)
    phases = points[:, None] * points[None, :] % NG
    angles = 2.0 * math.pi / NG * phases.astype(jnp.float32)
    cosine = jnp.cos(angles)
    sine = direction * jnp.sin(angles)
    blocks = jnp.stack([jnp.stack([cosine, sine]), jnp.stack([-sine, cosine])])
    return jnp.transpose(blocks, (0, 2, 1, 3)).astype(jnp.bfloat16)


def transform(values, matrix, keep_float):
    count = values.shape[0]
    current = values.reshape(count, 2, NG, NG * NG)
    product = jnp.einsum("uavb,pvbc->puac", matrix, current, preferred_element_type=jnp.float32)
    current = product.astype(jnp.bfloat16).reshape(count, 2, NG, NG, NG)
    product = jnp.einsum("uavb,pvxbz->puxaz", matrix, current, preferred_element_type=jnp.float32)
    current = product.astype(jnp.bfloat16)
    product = jnp.einsum("uavb,pvxyb->puxya", matrix, current, preferred_element_type=jnp.float32)
    if not keep_float:
        product = product.astype(jnp.bfloat16)
    return product.reshape(count, 2, NG * NG * NG)


def add_block(
    accum_real,
    accum_imag,
    local_bands,
    visiting,
    visiting_occ,
    kernel,
    forward_matrix,
    inverse_matrix,
):
    c = local_bands[:, 0].astype(jnp.float32)[None]
    d = local_bands[:, 1].astype(jnp.float32)[None]
    a = visiting[:, 0].astype(jnp.float32)[:, None]
    b = visiting[:, 1].astype(jnp.float32)[:, None]
    visits = visiting.shape[0]
    owned = local_bands.shape[0]
    density = jnp.stack([a * c + b * d, a * d - b * c], axis=2).astype(jnp.bfloat16)
    density = density.reshape(visits * owned, 2, density.shape[3])
    spectrum = transform(density, forward_matrix, False)
    screened = (spectrum.astype(jnp.float32) * (kernel / GRID)).astype(jnp.bfloat16)
    potential = transform(screened, inverse_matrix, True)
    potential = potential.reshape(visits, owned, 2, potential.shape[2])
    weight = (-0.5 * visiting_occ.astype(jnp.float32))[:, None, None]
    e = potential[:, :, 0]
    f = potential[:, :, 1]
    accum_real = accum_real + jnp.sum(weight * (a * e - b * f), axis=0)
    accum_imag = accum_imag + jnp.sum(weight * (a * f + b * e), axis=0)
    return (accum_real, accum_imag)


def contract(x, y):
    return jnp.einsum("ig,jg->ij", x, y, preferred_element_type=jnp.float32)


def gram_block(bra_rows, ket_rows):
    c = bra_rows[:, 0]
    d = bra_rows[:, 1]
    e = ket_rows[:, 0]
    f = ket_rows[:, 1]
    real_part = contract(c, e) + contract(d, f)
    imag_part = contract(c, f) - contract(d, e)
    return jnp.stack([real_part, imag_part])


def shards(orbitals, occupation, kernel):
    local_bands = orbitals[0]
    own_occupation = occupation[0]
    forward_matrix = dft_matrix(1.0)
    inverse_matrix = dft_matrix(-1.0)
    zeros_grid = jnp.zeros((local_bands.shape[0], local_bands.shape[2]), jnp.float32)
    first_block, first_occ = shifted((local_bands, own_occupation), "pool", 1)
    accum_real, accum_imag = add_block(
        zeros_grid,
        zeros_grid,
        local_bands,
        first_block,
        first_occ,
        kernel,
        forward_matrix,
        inverse_matrix,
    )
    second_block, second_occ = shifted((first_block, first_occ), "band", 1)
    accum_real, accum_imag = add_block(
        accum_real,
        accum_imag,
        local_bands,
        second_block,
        second_occ,
        kernel,
        forward_matrix,
        inverse_matrix,
    )
    exchanged = jnp.stack([accum_real, accum_imag], axis=1).astype(jnp.bfloat16)
    norm_factor = 1.0 / math.sqrt(GRID)
    part = (
        gram_block(lax.all_gather(local_bands, "band", axis=0, tiled=True), exchanged) * norm_factor
    )
    return (exchanged[None], part[None])


def solution(mesh):
    return jax.shard_map(
        shards,
        mesh=mesh,
        in_specs=(P("pool", "band", None, None), P("pool", "band"), P()),
        out_specs=(P("pool", "band", None, None), P("pool", None, None, "band")),
        check_vma=False,
    )
```

profile of v0, /device:TPU:0, one launch (start us, length us, event | category | flops | bytes accessed | tf_op | source)
XLA Modules:
  0.0 45.1 jit_solution(17190550461648578065)
XLA Ops:
  0.6 3.0 %collective-permute-start.1 = (bf16[1,2,46656]{2,1,0:T(2,128)(2,1)}, bf16[1,2,46656]{2,1,0:T(2,128)(2,1)S(1)}, u32[]{:S(2)}, u32[]{:S(2)}) collective-permute-start(bf16[1,2,46656]{2,1,0:T(2,128)(2,1)} %bitcast.302), channel_id=1, source_target_pairs={{0,4},{4,8},{8,12},{12,16},{16,20},{20,24},{24,28},{28,0},{1,5},{5... | collective-permute-start | bytes 559880 | tf_op jit(solution)/shard_map/ppermute | solution.py:14
  3.7 1.5 %collective-permute-start = (s32[1]{0:T(128)}, s32[1]{0:T(128)}, u32[]{:S(2)}, u32[]{:S(2)}) collective-permute-start(s32[1]{0:T(128)} %bitcast), channel_id=1, source_target_pairs={{0,4},{4,8},{8,12},{12,16},{16,20},{20,24},{24,28},{28,0},{1,5},{5... | collective-permute-start | bytes 20 | tf_op jit(solution)/shard_map/ppermute | solution.py:14
  5.2 8.6 %all-gather = bf16[4,1,2,46656]{3,2,1,0:T(2,128)(2,1)S(1)} all-gather(bf16[1,1,2,46656]{3,2,1,0:T(2,128)(2,1)} %param.3), channel_id=2, replica_groups=mesh['pool'=8,'band'=4] {'band'}, dimensions={0}, use_global_device_ids=true | all-gather | bytes 933120 | tf_op jit(solution)/shard_map/all_gather | solution.py:115
  13.8 0.9 %broadcast_multiply_fusion = f32[46656]{0:T(1024)S(1)} fusion(f32[46656]{0:T(1024)} %param.5), kind=kLoop, calls=%fused_computation.75 | loop fusion | flops 46656 | bytes 373248 | tf_op jit(solution)/shard_map/div | solution.py:59
  14.9 2.2 %fusion.65 = (bf16[4,1,46656]{2,1,0:T(2,128)(2,1)}, bf16[4,1,46656]{2,1,0:T(2,128)(2,1)}) fusion(bf16[4,2,46656]{2,1,0:T(2,128)(2,1)S(1)} %bitcast.301), kind=kLoop, calls=%fused_computation.111 | loop fusion | bytes 1492992 | tf_op jit(solution)/shard_map/slice | solution.py:75
  17.3 0.4 collective-permute-start.3
  18.5 0.5 %collective-permute-start.2 = (s32[1]{0:T(128)}, s32[1]{0:T(128)}, u32[]{:S(2)}, u32[]{:S(2)}) collective-permute-start(s32[1]{0:T(128)} %collective-permute-done), channel_id=1, source_target_pairs={{0,1},{1,2},{2,3},{3,0},{4,5},{5,6},{6,7},{7,4},{8,9},{9,10},{10,1... | collective-permute-start | bytes 20 | tf_op jit(solution)/shard_map/ppermute | solution.py:14
  19.0 3.4 %collective-permute-done.2 = s32[1]{0:T(128)} collective-permute-done((s32[1]{0:T(128)}, s32[1]{0:T(128)}, u32[]{:S(2)}, u32[]{:S(2)}) %collective-permute-start.2) | collective-permute-done | bytes 36 | tf_op jit(solution)/shard_map/ppermute | solution.py:14
  23.1 2.7 %convert_reduce_fusion.1 = (bf16[46656]{0:T(1024)(128)(2,1)S(1)}, bf16[46656]{0:T(1024)(128)(2,1)S(1)}, bf16[46656]{0:T(1024)(128)(2,1)S(1)}, bf16[46656]{0:T(1024)(128)(2,1)S(1)}) fusion(bf16[1,2,46656]{2,1,0:T(2,128)(2,1)S(1)} %bitcast.303, bf16[1,2,46656]{2,1,0:T(2,128)(2,1)S(1)} %collective-permute-done.3, bf16[1,2,46656]{2,1,0:T(2,128)(2,1)S(1)} %collective-permute-done.1), kind=kLoop, calls=%fused_computation.72 | loop fusion | flops 1026432 | bytes 933120 | tf_op jit(solution)/shard_map/convert.15
  26.5 0.6 %reshape.535 = bf16[2,36,36,36]{3,2,1,0:T(8,128)(2,1)S(1)} reshape(bf16[1,2,36,1296]{3,2,1,0:T(8,128)(2,1)S(1)} %fusion.7) | data formatting | bytes 373248 | tf_op jit(solution)/shard_map/reshape.3
  27.1 0.9 %convert_bitcast_fusion.1 = f32[1,2,36,36,36]{4,3,1,2,0:T(8,128)S(1)} fusion(bf16[1,2,36,36]{3,2,1,0:T(8,128)(2,1)S(1)} %get-tuple-element.16, bf16[1,2,36,36]{3,2,1,0:T(8,128)(2,1)S(1)} %get-tuple-element.17, bf16[2,36,36,36]{3,2,1,0:T(8,128)(2,1)S(1)} %reshape.535), kind=kOutput, calls=%fused_computation.13 | convolution fusion | flops 27195264 | bytes 570240 | tf_op jit(solution)/shard_map/uavb,pvxyb->puxya/dot_general | solution.py:34
  28.0 1.1 %reshape.496 = f32[2,36,1296]{2,0,1:T(2,128)S(1)} reshape(f32[1,2,36,36,36]{4,3,1,2,0:T(8,128)S(1)} %convert_bitcast_fusion.1) | data formatting | bytes 746496 | tf_op jit(solution)/shard_map/convert_element_type | solution.py:59
  29.4 0.3 fusion.5
  29.7 0.6 %reshape.537 = bf16[2,36,36,36]{3,2,1,0:T(8,128)(2,1)S(1)} reshape(bf16[1,2,36,1296]{3,2,1,0:T(8,128)(2,1)S(1)} %fusion.5) | data formatting | bytes 373248 | tf_op jit(solution)/shard_map/reshape.28
  30.3 0.9 %convert_bitcast_fusion = f32[1,2,36,36,36]{4,3,1,2,0:T(8,128)S(1)} fusion(bf16[1,2,36,36]{3,2,1,0:T(8,128)(2,1)S(1)} %get-tuple-element.16, bf16[1,2,36,36]{3,2,1,0:T(8,128)(2,1)S(1)} %get-tuple-element.17, bf16[2,36,36,36]{3,2,1,0:T(8,128)(2,1)S(1)} %reshape.537), kind=kOutput, calls=%fused_computation.12 | convolution fusion | flops 27195264 | bytes 570240 | tf_op jit(solution)/shard_map/uavb,pvxyb->puxya/dot_general | solution.py:34
  31.2 1.1 %reshape.497 = f32[2,36,1296]{2,0,1:T(2,128)S(1)} reshape(f32[1,2,36,36,36]{4,3,1,2,0:T(8,128)S(1)} %convert_bitcast_fusion) | data formatting | bytes 746496 | tf_op jit(solution)/shard_map/convert_element_type | solution.py:59
  32.2 1.0 %multiply_convert_fusion = (bf16[2,36,1296]{2,0,1:T(2,128)(2,1)S(1)}, bf16[2,36,1296]{2,0,1:T(2,128)(2,1)}) fusion(f32[2,36,1296]{2,0,1:T(2,128)S(1)} %reshape.497, f32[36,1296]{1,0:T(8,128)S(1)} %mul.318, f32[2,36,1296]{2,0,1:T(2,128)S(1)} %reshape.496), kind=kLoop, calls=%fused_computation.40 | loop fusion | flops 373248 | bytes 1306368 | tf_op jit(solution)/shard_map/convert_element_type | solution.py:59
  33.3 0.3 fusion.4
  33.5 0.6 %reshape.538 = bf16[2,36,36,36]{3,2,1,0:T(8,128)(2,1)S(1)} reshape(bf16[1,2,36,1296]{3,2,1,0:T(8,128)(2,1)S(1)} %fusion.4) | data formatting | bytes 373248 | tf_op jit(solution)/shard_map/reshape.35
  34.2 0.9 %convolution_bitcast_fusion.4 = f32[1,2,36,36,36]{4,3,1,2,0:T(8,128)S(1)} fusion(bf16[1,2,36,36]{3,2,1,0:T(8,128)(2,1)S(1)} %get-tuple-element.15, bf16[1,2,36,36]{3,2,1,0:T(8,128)(2,1)S(1)} %get-tuple-element.14, bf16[2,36,36,36]{3,2,1,0:T(8,128)(2,1)S(1)} %reshape.538), kind=kOutput, calls=%fused_computation.20 | convolution fusion | flops 27008640 | bytes 570240 | tf_op jit(solution)/shard_map/uavb,pvxyb->puxya/dot_general | solution.py:34
  35.2 1.7 %reshape_reshape.9 = f32[1,1,2,46656]{3,2,1,0:T(2,128)} reshape(f32[1,2,36,36,36]{4,3,2,1,0:T(8,128)S(1)} %copy.46) | data formatting | bytes 746496 | tf_op jit(solution)/shard_map/reshape;reshape | solution.py:61
  36.9 0.3 fusion.6
  37.1 0.8 %reshape.536 = bf16[2,36,36,36]{3,2,1,0:T(8,128)(2,1)S(1)} reshape(bf16[1,2,36,1296]{3,2,1,0:T(8,128)(2,1)S(1)} %fusion.6) | data formatting | bytes 373248 | tf_op jit(solution)/shard_map/reshape.20
  38.0 0.9 %convolution_bitcast_fusion.5 = f32[1,2,36,36,36]{4,3,1,2,0:T(8,128)S(1)} fusion(bf16[1,2,36,36]{3,2,1,0:T(8,128)(2,1)S(1)} %get-tuple-element.15, bf16[1,2,36,36]{3,2,1,0:T(8,128)(2,1)S(1)} %get-tuple-element.14, bf16[2,36,36,36]{3,2,1,0:T(8,128)(2,1)S(1)} %reshape.536), kind=kOutput, calls=%fused_computation.21 | convolution fusion | flops 27008640 | bytes 570240 | tf_op jit(solution)/shard_map/uavb,pvxyb->puxya/dot_general | solution.py:34
  39.0 1.0 %reshape_reshape.8 = f32[1,1,2,46656]{3,2,1,0:T(2,128)S(1)} reshape(f32[1,2,36,36,36]{4,3,2,1,0:T(8,128)S(1)} %copy.38) | data formatting | bytes 746496 | tf_op jit(solution)/shard_map/reshape;reshape | solution.py:61
  40.0 1.5 %multiply_add_fusion.1 = (bf16[1,1,46656]{2,1,0:T(2,128)(2,1)S(1)}, bf16[1,1,46656]{2,1,0:T(2,128)(2,1)S(1)}) fusion(f32[1,1,2,46656]{3,2,1,0:T(2,128)S(1)} %reshape_reshape.8, f32[1,1,2,46656]{3,2,1,0:T(2,128)S(1)} %copy-done.1, f32[]{:T(128)} %bitcast.45, f32[]{:T(128)} %bitcast.1, bf16[1,2,46656]{2,1,0:T(2,128)(2,1)S(1)} %collective-permute-done.1, ...), kind=kLoop, calls=%fused_computation.70 | loop fusion | flops 1119744 | bytes 1306376 | tf_op jit(solution)/shard_map/add | solution.py:65
  41.4 0.5 %convolution_bitcast_fusion.8 = f32[4]{0:T(128)S(1)} fusion(bf16[1,1,46656]{2,1,0:T(2,128)(2,1)S(1)} %get-tuple-element.9, bf16[4,1,46656]{2,1,0:T(2,128)(2,1)S(1)} %copy-done.4), kind=kOutput, calls=%fused_computation.30 | convolution fusion | flops 373248 | bytes 466576 | tf_op jit(solution)/shard_map/ig,jg->ij/dot_general | solution.py:71
  41.9 0.5 %convolution_bitcast_fusion.6 = f32[4]{0:T(128)S(1)} fusion(bf16[1,1,46656]{2,1,0:T(2,128)(2,1)S(1)} %get-tuple-element.8, bf16[4,1,46656]{2,1,0:T(2,128)(2,1)S(1)} %copy-done.4), kind=kOutput, calls=%fused_computation.28 | convolution fusion | flops 373248 | bytes 466576 | tf_op jit(solution)/shard_map/ig,jg->ij/dot_general | solution.py:71
  42.6 0.4 fusion.15
  42.9 0.5 %fusion.17 = f32[1,1,4,1]{2,3,1,0:T(1,128)S(1)} fusion(f32[4]{0:T(128)S(1)} %convolution_bitcast_fusion.6, bf16[1,1,46656]{2,1,0:T(2,128)(2,1)S(1)} %get-tuple-element.9, bf16[4,1,46656]{2,1,0:T(2,128)(2,1)S(1)} %copy-done.3), kind=kOutput, calls=%fused_computation.35 | convolution fusion | flops 373252 | bytes 466592 | tf_op jit(solution)/shard_map/ig,jg->ij/dot_general | solution.py:71
  43.4 0.6 %maximum_multiply_fusion = f32[1,2,4,1]{2,3,1,0:T(1,128)} fusion(f32[1,1,4,1]{2,3,1,0:T(1,128)S(1)} %fusion.17, f32[1,1,4,1]{2,3,1,0:T(1,128)S(1)} %fusion.15), kind=kLoop, calls=%fused_computation.108 | loop fusion | flops 16 | bytes 64 | tf_op jit(solution)/shard_map/mul | solution.py:115
  44.0 1.1 %pad_maximum_fusion = bf16[1,1,2,46656]{3,2,1,0:T(2,128)(2,1)} fusion(bf16[1,1,1,46656]{3,2,1,0:T(2,128)(2,1)S(1)} %bitcast.305, bf16[1,1,1,46656]{3,2,1,0:T(2,128)(2,1)S(1)} %bitcast.304), kind=kLoop, calls=%fused_computation.64 | loop fusion | flops 373248 | bytes 373248 | tf_op jit(solution)/shard_map/stack | solution.py:112
  (25 shorter events, 1.8 us)
Async XLA Ops:
  0.6 16.7 %collective-permute-start.1 = (bf16[1,2,46656]{2,1,0:T(2,128)(2,1)}, bf16[1,2,46656]{2,1,0:T(2,128)(2,1)S(1)}, u32[]{:S(2)}, u32[]{:S(2)}) collective-permute-start(bf16[1,2,46656]{2,1,0:T(2,128)(2,1)} %bitcast.302), channel_id=1, source_target_pairs={{0,4},{4,8},{8,12},{12,16},{16,20},{20,24},{24,28},{28,0},{1,5},{5... | collective-permute-start | bytes 559880 | tf_op jit(solution)/shard_map/ppermute | solution.py:14
  3.7 14.2 %collective-permute-start = (s32[1]{0:T(128)}, s32[1]{0:T(128)}, u32[]{:S(2)}, u32[]{:S(2)}) collective-permute-start(s32[1]{0:T(128)} %bitcast), channel_id=1, source_target_pairs={{0,4},{4,8},{8,12},{12,16},{16,20},{20,24},{24,28},{28,0},{1,5},{5... | collective-permute-start | bytes 20 | tf_op jit(solution)/shard_map/ppermute | solution.py:14
  14.9 8.2 %copy-start = (bf16[1,1,2,46656]{3,2,1,0:T(2,128)(2,1)S(1)}, bf16[1,1,2,46656]{3,2,1,0:T(2,128)(2,1)}, u32[]{:S(2)}) copy-start(bf16[1,1,2,46656]{3,2,1,0:T(2,128)(2,1)} %param.3) | copy-start | bytes 559876
  17.3 5.8 %collective-permute-start.3 = (bf16[1,2,46656]{2,1,0:T(2,128)(2,1)S(1)}, bf16[1,2,46656]{2,1,0:T(2,128)(2,1)S(1)}, u32[]{:S(2)}, u32[]{:S(2)}) collective-permute-start(bf16[1,2,46656]{2,1,0:T(2,128)(2,1)S(1)} %collective-permute-done.1), channel_id=1, source_target_pairs={{0,1},{1,2},{2,3},{3,0},{4,5},{5,6},{6,7},{7,4},{8,9},{9,10},{10,1... | collective-permute-start | bytes 559880 | tf_op jit(solution)/shard_map/ppermute | solution.py:14
  18.5 4.0 %collective-permute-start.2 = (s32[1]{0:T(128)}, s32[1]{0:T(128)}, u32[]{:S(2)}, u32[]{:S(2)}) collective-permute-start(s32[1]{0:T(128)} %collective-permute-done), channel_id=1, source_target_pairs={{0,1},{1,2},{2,3},{3,0},{4,5},{5,6},{6,7},{7,4},{8,9},{9,10},{10,1... | collective-permute-start | bytes 20 | tf_op jit(solution)/shard_map/ppermute | solution.py:14
  35.1 1.7 %copy-start.2 = (bf16[2,36,1296]{2,0,1:T(2,128)(2,1)S(1)}, bf16[2,36,1296]{2,0,1:T(2,128)(2,1)}, u32[]{:S(2)}) copy-start(bf16[2,36,1296]{2,0,1:T(2,128)(2,1)} %get-tuple-element.13) | copy-start | bytes 559876
  39.0 1.0 %copy-start.1 = (f32[1,1,2,46656]{3,2,1,0:T(2,128)S(1)}, f32[1,1,2,46656]{3,2,1,0:T(2,128)}, u32[]{:S(2)}) copy-start(f32[1,1,2,46656]{3,2,1,0:T(2,128)} %reshape_reshape.9) | copy-start | bytes 1119748
  39.9 1.5 %copy-start.4 = (bf16[4,1,46656]{2,1,0:T(2,128)(2,1)S(1)}, bf16[4,1,46656]{2,1,0:T(2,128)(2,1)}, u32[]{:S(2)}) copy-start(bf16[4,1,46656]{2,1,0:T(2,128)(2,1)} %get-tuple-element.11) | copy-start | bytes 1119748
  41.4 1.1 %copy-start.3 = (bf16[4,1,46656]{2,1,0:T(2,128)(2,1)S(1)}, bf16[4,1,46656]{2,1,0:T(2,128)(2,1)}, u32[]{:S(2)}) copy-start(bf16[4,1,46656]{2,1,0:T(2,128)(2,1)} %get-tuple-element.10) | copy-start | bytes 1119748
where the time goes:
time: 45.3 us; the launch traced here: 45.1 us
  local copies, waits for them, and re-layouts  10.8 us (24%)
  blocking collectives  8.58 us (19%)
  other arithmetic  8.18 us (18%)
  matrix products  6.45 us (14%)
  starting transfers between devices  5.5 us (12%)
  waiting for transfers between devices  3.45 us (8%)
  between operations  2.15 us (5%)
    all_gather x1, blocking collectives, shards(): lax.all_gather(local_bands, 'band', axis=0, tiled=True)  8.58 us
    ppermute x4, starting transfers between devices, shifted(): lax.ppermute(array, axis, [(i, (i + by) % length) for i in range(length)])  5.5 us
    dot_general x4, matrix products, transform(): jnp.einsum('uavb,pvxyb->puxya', matrix, current, preferred_element_type=j...  3.56 us
    ppermute x4, waiting for transfers between devices, shifted(): lax.ppermute(array, axis, [(i, (i + by) % length) for i in range(length)])  3.45 us
    another operation x4, other arithmetic  3.02 us
    another operation x2, local copies, waits for them, and re-layouts, add_block(): potential = potential.reshape(visits, owned, 2, potential.shape[2])  2.68 us
    another operation x4, local copies, waits for them, and re-layouts  2.67 us
    slice x1, local copies, waits for them, and re-layouts, gram_block(): c = bra_rows[:, 0]  2.17 us
  transfers between devices with their start and end apart: 4, of which 1 were waited for; matrix products, arithmetic and copies ran while one was open for 8% of the time, Pallas kernels for 0%

commit v1 on v0

v1 whole, which is shorter than its diff:
```python
import math

import jax
import jax.numpy as jnp
import numpy as np
from jax import lax
from jax.experimental import pallas as pl
from jax.experimental.pallas import tpu as pltpu
from jax.sharding import PartitionSpec as P

LANES = 128
F32 = jnp.float32
BF16 = jnp.bfloat16
VMEM = pl.BlockSpec(memory_space=pltpu.VMEM)
SMEM = pl.BlockSpec(memory_space=pltpu.SMEM)


class Plan:
    def __init__(self, grid):
        ng = round(grid ** (1.0 / 3.0))
        self.grid = grid
        self.ng = ng
        self.split = max(b for b in range(1, ng + 1) if ng % b == 0 and b * ng <= LANES)
        self.coarse = ng // self.split
        self.width = self.split * ng
        self.rows = grid // self.width
        self.tiles = grid // LANES + 1
        self.tail = grid % LANES
        common = math.lcm(self.width, LANES)
        self.row_period = common // self.width
        self.tile_period = common // LANES
        self.padded_rows = (self.rows // self.row_period + 1) * self.row_period + 8
        self.padded_tiles = (self.tiles // self.tile_period + 1) * self.tile_period + 8


def roots(ng, phases):
    angles = 2.0 * np.pi / ng * (phases % ng)
    return np.cos(angles), np.sin(angles)


def constants(plan):
    ng, split, coarse, width = plan.ng, plan.split, plan.coarse, plan.width
    x, a = np.divmod(np.arange(plan.rows), coarse)
    b, z = np.divmod(np.arange(width), ng)
    cosine, sine = roots(ng, np.outer(x, x) + split * np.outer(a, a))
    left = np.concatenate([cosine, sine], axis=1)
    cosine, sine = roots(ng, coarse * np.outer(b, b) + np.outer(z, z))
    right = np.zeros((2, 2, LANES, 2, LANES))
    for way, sign in enumerate((1.0, -1.0)):
        right[way, 0, :width, 0, :width] = cosine
        right[way, 1, :width, 1, :width] = cosine
        right[way, 1, :width, 0, :width] = sign * sine
        right[way, 0, :width, 1, :width] = -sign * sine
    twiddle = np.zeros((2, plan.rows, LANES))
    twiddle[0, :, :width], twiddle[1, :, :width] = roots(ng, np.outer(a, b))
    return (
        jnp.asarray(left, BF16),
        jnp.asarray(right.reshape(2, 2 * LANES, 2 * LANES), BF16),
        jnp.asarray(twiddle, F32),
    )


def pack(plan):
    def body(orbital, occupation, out):
        last = plan.tiles - 1
        for q in range(last):
            out[2 * q : 2 * q + 2, :] = orbital[:, LANES * q : LANES * (q + 1)]
        if plan.tail:
            out[2 * last :, : plan.tail] = orbital[:, LANES * last :]
        fill = jnp.full((2, LANES - plan.tail), occupation[0], jnp.int32)
        out[2 * last :, plan.tail :] = fill.astype(F32).astype(BF16)

    return pl.pallas_call(
        body,
        out_shape=jax.ShapeDtypeStruct((2 * plan.tiles, LANES), BF16),
        in_specs=[VMEM, SMEM],
        out_specs=VMEM,
        name="pack",
    )


def to_matrix(plan, tiles, store):
    for j in range(plan.row_period):
        q, shift = divmod(plan.width * j, LANES)
        count = -(-(plan.rows - j) // plan.row_period)
        stride = 2 * plan.tile_period
        for part in range(2):
            block = tiles[pl.ds(2 * q + part, count, stride=stride), :]
            if shift + plan.width > LANES:
                after = tiles[pl.ds(2 * q + 2 + part, count, stride=stride), :]
                lane = lax.broadcasted_iota(jnp.int32, block.shape, 1)
                block = jnp.where(lane >= shift, block, after)
            if shift:
                block = pltpu.roll(block, LANES - shift, axis=1)
            store(part, j, count, block)


def from_matrix(plan, matrix, tiles):
    width = plan.width
    for i in range(plan.tile_period):
        row, offset = divmod(LANES * i, width)
        count = -(-(plan.tiles - i) // plan.tile_period)
        for part in range(2):
            block = None
            start = -offset
            while start < LANES:
                rows = matrix[part, pl.ds(row, count, stride=plan.row_period), :]
                if start % LANES:
                    rows = pltpu.roll(rows, start % LANES, axis=1)
                if block is None:
                    block = rows
                else:
                    lane = lax.broadcasted_iota(jnp.int32, rows.shape, 1)
                    block = jnp.where(lane < start, block, rows)
                start += width
                row += 1
            row -= -(-(LANES + offset) // width)
            tiles[pl.ds(2 * i + part, count, stride=2 * plan.tile_period), :] = block


def exchange(plan, own, tiles, near, fourier, kernel, left, right, twiddle):
    rows = plan.rows

    def keep(part, first, count, block):
        near[part, pl.ds(first, count, stride=plan.row_period), :] = block

    to_matrix(plan, tiles, keep)
    c = own[0, :rows, :]
    d = own[1, :rows, :]
    a = near[0, :rows, :]
    b = near[1, :rows, :]

    def put(real, imag, sign):
        real = real.astype(BF16)
        imag = imag.astype(BF16)
        fourier[:rows, :LANES] = real
        fourier[:rows, LANES:] = imag
        fourier[rows:, :LANES] = imag if sign > 0 else -imag
        fourier[rows:, LANES:] = -real if sign > 0 else real

    def dot(x, y):
        return jnp.dot(x, y, preferred_element_type=F32)

    put(a * c + b * d, a * d - b * c, 1)
    half = dot(left[...], fourier[...])
    real, imag = half[:, :LANES], half[:, LANES:]
    cosine = twiddle[0]
    sine = twiddle[1]
    turned = jnp.concatenate(
        [real * cosine + imag * sine, imag * cosine - real * sine], axis=1
    ).astype(BF16)
    spectrum = dot(turned, right[0])
    factor = kernel[...]
    screened = jnp.concatenate(
        [spectrum[:, :LANES] * factor, spectrum[:, LANES:] * factor], axis=1
    ).astype(BF16)
    half = dot(screened, right[1])
    real, imag = half[:, :LANES], half[:, LANES:]
    put(real * cosine - imag * sine, imag * cosine + real * sine, -1)
    potential = dot(left[...], fourier[...])
    e = potential[:, :LANES]
    f = potential[:, LANES:]
    last = 2 * plan.tiles - 2
    weight = -0.5 * tiles[last : last + 1, plan.tail : plan.tail + 1]
    a = near[0, :rows, :]
    b = near[1, :rows, :]
    return weight * (a * e - b * f), weight * (a * f + b * e)


def first_pair(plan, others):
    def body(*refs):
        own_in, near_in, kernel, left, right, twiddle = refs[:6]
        band_in = refs[6 : 6 + others]
        own, accum, bands, tiles, near, fourier = refs[6 + others :]
        size = 2 * plan.tiles

        def keep_own(part, first, count, block):
            own[part, pl.ds(first, count, stride=plan.row_period), :] = block

        tiles[:size, :] = own_in[...].astype(F32)
        to_matrix(plan, tiles, keep_own)
        tiles[:size, :] = near_in[...].astype(F32)
        real, imag = exchange(plan, own, tiles, near, fourier, kernel, left, right, twiddle)
        accum[0] = real
        accum[1] = imag
        for index in range(others):

            def keep_band(part, first, count, block):
                bands[index, part, pl.ds(first, count, stride=plan.row_period), :] = block

            tiles[:size, :] = band_in[index][...].astype(F32)
            to_matrix(plan, tiles, keep_band)

    rows = plan.rows
    return pl.pallas_call(
        body,
        out_shape=[
            jax.ShapeDtypeStruct((2, rows, LANES), F32),
            jax.ShapeDtypeStruct((2, rows, LANES), F32),
            jax.ShapeDtypeStruct((others, 2, rows, LANES), F32),
        ],
        in_specs=[VMEM] * (6 + others),
        out_specs=[VMEM] * 3,
        scratch_shapes=[
            pltpu.VMEM((2 * plan.padded_tiles, LANES), F32),
            pltpu.VMEM((2, plan.padded_rows, LANES), F32),
            pltpu.VMEM((2 * rows, 2 * LANES), BF16),
        ],
        name="first_pair",
    )


def second_pair(plan, others):
    count = others + 1

    def body(place, own, accum, bands, far_in, near_in, kernel, left, right, twiddle, out, gram, *scratch):
        tiles, near, fourier, total = scratch
        size = 2 * plan.tiles
        odd = place[0] % 2 == 1
        tiles[:size, :] = jnp.where(odd, near_in[...].astype(F32), far_in[...].astype(F32))
        real, imag = exchange(plan, own, tiles, near, fourier, kernel, left, right, twiddle)
        e = (accum[0] + real).astype(BF16).astype(F32)
        f = (accum[1] + imag).astype(BF16).astype(F32)
        total[0, : plan.rows, :] = e
        total[1, : plan.rows, :] = f
        lane = lax.broadcasted_iota(jnp.int32, (1, count), 1)
        sums = [jnp.zeros((1, count), F32)] * 2
        norm = 1.0 / math.sqrt(plan.grid)
        for index in range(count):
            c = own[0] if index == 0 else bands[index - 1, 0]
            d = own[1] if index == 0 else bands[index - 1, 1]
            parts = (c * e + d * f, c * f - d * e)
            for part in range(2):
                value = jnp.sum(jnp.sum(parts[part], axis=0, keepdims=True), axis=1, keepdims=True)
                sums[part] = jnp.where(lane == place[index], value * norm, sums[part])
        for part in range(2):
            gram[part] = sums[part]
        from_matrix(plan, total, tiles)
        last = plan.tiles - 1
        for q in range(last):
            out[:, LANES * q : LANES * (q + 1)] = tiles[2 * q : 2 * q + 2, :].astype(BF16)
        if plan.tail:
            out[:, LANES * last :] = tiles[2 * last : 2 * last + 2, : plan.tail].astype(BF16)

    rows = plan.rows
    return pl.pallas_call(
        body,
        out_shape=[
            jax.ShapeDtypeStruct((2, plan.grid), BF16),
            jax.ShapeDtypeStruct((2, 1, count), F32),
        ],
        in_specs=[SMEM] + [VMEM] * 9,
        out_specs=[VMEM] * 2,
        scratch_shapes=[
            pltpu.VMEM((2 * plan.padded_tiles, LANES), F32),
            pltpu.VMEM((2, plan.padded_rows, LANES), F32),
            pltpu.VMEM((2 * rows, 2 * LANES), BF16),
            pltpu.VMEM((2, plan.padded_rows, LANES), F32),
        ],
        name="second_pair",
    )


def shards(orbitals, occupation, kernel):
    plan = Plan(orbitals.shape[3])
    pools = lax.axis_size("pool")
    groups = lax.axis_size("band")

    def move(array, target):
        pairs = [
            (p * groups + g, q * groups + h)
            for p in range(pools)
            for g in range(groups)
            for q, h in [target(p, g)]
        ]
        return lax.ppermute(array, ("pool", "band"), pairs)

    own = pack(plan)(orbitals[0, 0], occupation[0])
    near = move(own, lambda p, g: ((p + 1) % pools, g))
    far = move(
        own,
        lambda p, g: ((p + 1) % pools, (g + 1) % groups) if g % 2 else (p, g + 1),
    )
    partner = lambda p, g: (p, g ^ 1)
    bands = [move(own, partner)]
    for step in range(1, groups // 2):
        shifted = move(own, lambda p, g: (p, (g + 2 * step) % groups))
        bands += [shifted, move(shifted, partner)]
    swapped = move(near, partner)
    here = lax.axis_index("band")
    places = [here, here ^ 1]
    for step in range(1, groups // 2):
        places += [(here - 2 * step) % groups, ((here ^ 1) - 2 * step) % groups]
    place = jnp.stack(places).astype(jnp.int32)

    factor = kernel.reshape(plan.ng, plan.split, plan.coarse, plan.ng).transpose(0, 2, 1, 3)
    factor = factor.reshape(plan.rows, plan.width) * (1.0 / plan.grid)
    factor = jnp.pad(factor, ((0, 0), (0, LANES - plan.width)))
    left, right, twiddle = constants(plan)
    others = groups - 1
    mine, accum, stack = first_pair(plan, others)(own, near, factor, left, right, twiddle, *bands)
    exchanged, gram = second_pair(plan, others)(
        place, mine, accum, stack, far, swapped, factor, left, right, twiddle
    )
    return exchanged[None, None], jnp.swapaxes(gram, 1, 2)[None]


def solution(mesh):
    return jax.shard_map(
        shards,
        mesh=mesh,
        in_specs=(P("pool", "band", None, None), P("pool", "band"), P()),
        out_specs=(P("pool", "band", None, None), P("pool", None, None, "band")),
        check_vma=False,
    )
```

time: 45.3 us -> 33.9 us (0.75)
  Pallas kernels: 0 us -> 13 us
  blocking collectives: 8.58 us -> 0 us
  local copies, waits for them, and re-layouts: 10.8 us -> 3.94 us
  other arithmetic: 8.18 us -> 1.68 us
  matrix products: 6.45 us -> 0 us
  waiting for transfers between devices: 3.45 us -> 8.68 us
  between operations: 2.15 us -> 1.4 us
  starting transfers between devices: 5.5 us -> 5 us
    pallas_call x0 -> x3, Pallas kernels: none -> 13 us  [the longest x1 5.74 us: shards(): first_pair(plan, others)(own, near, factor, left, right, twiddle, *bands)]
    all_gather x1 -> x0, blocking collectives: 8.58 us -> none  [shards(): lax.all_gather(local_bands, 'band', axis=0, tiled=True)]
    dot_general x12 -> x0, matrix products: 6.45 us -> none  [the longest x4 3.56 us: transform(): jnp.einsum('uavb,pvxyb->puxya', matrix, current, preferred_element_type=j...]
    another operation x10 -> x0, local copies, waits for them, and re-layouts: 6.05 us -> none  [the longest x2 2.68 us: add_block(): potential = potential.reshape(visits, owned, 2, potential.shape[2])]
    ppermute x4 -> x6, waiting for transfers between devices: 3.45 us -> 8.68 us  [move(): return lax.ppermute(array, ('pool', 'band'), pairs)]
    another operation x6 -> x1, other arithmetic: 4.14 us -> 0.67 us  [shards(): place = jnp.stack(places).astype(jnp.int32)]
    slice x1 -> x0, local copies, waits for them, and re-layouts: 2.17 us -> none  [gram_block(): c = bra_rows[:, 0]]
    convert_element_type x2 -> x0, local copies, waits for them, and re-layouts: 2.1 us -> none  [add_block(): spectrum.astype(jnp.float32) * (kernel / GRID)]
  transfers between devices with their start and end apart: 4 -> 6, of which waited for: 1 -> 2; matrix products, arithmetic and copies ran while one was open for 8% -> 11% of each run, Pallas kernels for 0% -> 17%
where the time goes in v1:
time: 33.9 us; the launch traced here: 33.7 us
  Pallas kernels  13 us (38%)
  waiting for transfers between devices  8.68 us (26%)
  starting transfers between devices  5 us (15%)
  local copies, waits for them, and re-layouts  3.94 us (12%)
  other arithmetic  1.68 us (5%)
  between operations  1.4 us (4%)
    ppermute x6, waiting for transfers between devices, move(): return lax.ppermute(array, ('pool', 'band'), pairs)  8.68 us
    pallas_call x1, Pallas kernels, shards(): first_pair(plan, others)(own, near, factor, left, right, twiddle, *bands)  5.74 us
    pallas_call x1, Pallas kernels, shards(): second_pair(plan, others)  5.38 us
    ppermute x6, starting transfers between devices, move(): return lax.ppermute(array, ('pool', 'band'), pairs)  5 us
    unnamed x12, local copies, waits for them, and re-layouts  2.07 us
    pallas_call x1, Pallas kernels, shards(): own = pack(plan)(orbitals[0, 0], occupation[0])  1.84 us
    mul x3, local copies, waits for them, and re-layouts, shards(): factor = factor.reshape(plan.rows, plan.width) * (1.0 / plan.grid)  1.17 us
    mul x1, other arithmetic, shards(): factor = factor.reshape(plan.rows, plan.width) * (1.0 / plan.grid)  1.01 us
  transfers between devices with their start and end apart: 6, of which 2 were waited for; matrix products, arithmetic and copies ran while one was open for 11% of the time, Pallas kernels for 17%

profile of v1, /device:TPU:0, one launch (start us, length us, event | category | flops | bytes accessed | tf_op | source)
XLA Modules:
  0.0 33.7 jit_solution(15754954660663645149)
XLA Ops:
  1.3 1.8 %pack.1.refs_0_ = bf16[730,128]{1,0:T(8,128)(2,1)} custom-call(bf16[2,46656]{1,0:T(2,128)(2,1)} %bitcast.13, s32[1]{0:T(128)} %bitcast.11.occupation), custom_call_target="tpu_custom_call" | custom-call | tf_op jit(solution)/shard_map/pack/pallas_call | solution.py:278
  3.1 3.0 %collective-permute-start.2 = (bf16[730,128]{1,0:T(8,128)(2,1)}, bf16[730,128]{1,0:T(8,128)(2,1)S(1)}, u32[]{:S(2)}, u32[]{:S(2)}) collective-permute-start(bf16[730,128]{1,0:T(8,128)(2,1)} %pack.1.refs_0_), channel_id=1, source_target_pairs={{0,2},{1,3},{2,0},{3,1},{4,6},{5,7},{6,4},{7,5},{8,10},{9,11},{10,... | collective-permute-start | bytes 560648 | tf_op jit(solution)/shard_map/ppermute | solution.py:276
  6.1 1.5 %collective-permute-start = (bf16[730,128]{1,0:T(8,128)(2,1)}, bf16[730,128]{1,0:T(8,128)(2,1)S(1)}, u32[]{:S(2)}, u32[]{:S(2)}) collective-permute-start(bf16[730,128]{1,0:T(8,128)(2,1)} %pack.1.refs_0_), channel_id=1, source_target_pairs={{0,4},{1,5},{2,6},{3,7},{4,8},{5,9},{6,10},{7,11},{8,12},{9,13},{1... | collective-permute-start | bytes 560648 | tf_op jit(solution)/shard_map/ppermute | solution.py:276
  7.6 0.0 collective-permute-start.1
  7.6 0.5 %collective-permute-start.4 = (bf16[730,128]{1,0:T(8,128)(2,1)}, bf16[730,128]{1,0:T(8,128)(2,1)S(1)}, u32[]{:S(2)}, u32[]{:S(2)}) collective-permute-start(bf16[730,128]{1,0:T(8,128)(2,1)} %pack.1.refs_0_), channel_id=1, source_target_pairs={{0,1},{1,6},{2,3},{3,4},{4,5},{5,10},{6,7},{7,8},{8,9},{9,14},{10,... | collective-permute-start | bytes 560648 | tf_op jit(solution)/shard_map/ppermute | solution.py:276
  8.1 2.9 %collective-permute-done.2.refs_7_ = bf16[730,128]{1,0:T(8,128)(2,1)S(1)} collective-permute-done((bf16[730,128]{1,0:T(8,128)(2,1)}, bf16[730,128]{1,0:T(8,128)(2,1)S(1)}, u32[]{:S(2)}, u32[]{:S(2)}) %collective-permute-start.2) | collective-permute-done | bytes 186912 | tf_op jit(solution)/shard_map/ppermute | solution.py:276
  11.0 0.0 copy-start.1
  11.0 0.0 collective-permute-start.3
  11.0 5.8 %collective-permute-done.refs_1_ = bf16[730,128]{1,0:T(8,128)(2,1)S(1)} collective-permute-done((bf16[730,128]{1,0:T(8,128)(2,1)}, bf16[730,128]{1,0:T(8,128)(2,1)S(1)}, u32[]{:S(2)}, u32[]{:S(2)}) %collective-permute-start) | collective-permute-done | bytes 186912 | tf_op jit(solution)/shard_map/ppermute | solution.py:276
  16.8 0.0 collective-permute-start.5
  16.8 1.0 %broadcast_multiply_fusion = f32[46656]{0:T(1024)S(1)} fusion(f32[46656]{0:T(1024)} %param.8), kind=kLoop, calls=%fused_computation | loop fusion | flops 46656 | bytes 373248 | tf_op jit(solution)/shard_map/mul | solution.py:297
  17.8 0.5 %mul.17 = f32[36,3,12,36]{3,2,1,0:T(8,128)S(1)} reshape(f32[46656]{0:T(1024)S(1)} %broadcast_multiply_fusion) | data formatting | bytes 373248 | tf_op jit(solution)/shard_map/mul | solution.py:297
  18.3 0.4 %copy.9 = f32[36,12,3,36]{3,2,1,0:T(4,128)S(1)} copy(f32[36,12,3,36]{3,1,2,0:T(8,128)S(1)} %bitcast.12) | data formatting | bytes 373248 | tf_op jit(solution)/shard_map/mul | solution.py:297
  18.7 0.0 copy-done.1
  18.7 0.0 copy-done
  18.7 0.3 %mul.19 = f32[432,108]{1,0:T(8,128)S(1)} reshape(f32[36,12,3,36]{3,2,1,0:T(4,128)S(1)} %copy.9) | data formatting | bytes 373248 | tf_op jit(solution)/shard_map/mul | solution.py:297
  19.1 0.7 %pad.4.refs_2_.kernel = f32[432,128]{1,0:T(8,128)} pad(f32[432,108]{1,0:T(8,128)S(1)} %mul.19, f32[]{:T(128)} %constant.37.clone.1), padding=0_0x0_20 | pad | bytes 407812 | tf_op jit(solution)/shard_map/jit(_pad)/pad | solution.py:298
  19.8 0.7 %pad_add_fusion.place = s32[4]{0:T(128)} fusion(s32[1]{0:T(128)} %bitcast.3, s32[1]{0:T(128)} %bitcast.2, s32[1]{0:T(128)} %bitcast.1, s32[1]{0:T(128)} %bitcast), kind=kLoop, calls=%fused_computation.1 | loop fusion | flops 12 | bytes 32 | tf_op jit(solution)/shard_map/stack | solution.py:294
  20.4 0.0 collective-permute-done.1.refs_6_
  20.4 0.0 copy-start.2
  20.4 0.0 collective-permute-done.3.refs_8_
  20.5 0.7 %copy-done.2 = bf16[730,128]{1,0:T(8,128)(2,1)} copy-done((bf16[730,128]{1,0:T(8,128)(2,1)}, bf16[730,128]{1,0:T(8,128)(2,1)S(1)}, u32[]{:S(2)}) %copy-start.2) | copy-done | bytes 186904
  21.1 0.0 copy-start.3
  21.1 0.7 %copy-done.3 = bf16[730,128]{1,0:T(8,128)(2,1)} copy-done((bf16[730,128]{1,0:T(8,128)(2,1)}, bf16[730,128]{1,0:T(8,128)(2,1)S(1)}, u32[]{:S(2)}) %copy-start.3) | copy-done | bytes 186904
  21.8 5.7 %first_pair.1 = (f32[2,432,128]{2,1,0:T(8,128)}, f32[2,432,128]{2,1,0:T(8,128)}, f32[3,2,432,128]{3,2,1,0:T(8,128)}) custom-call(bf16[730,128]{1,0:T(8,128)(2,1)} %pack.1.refs_0_, bf16[730,128]{1,0:T(8,128)(2,1)} %copy-done, f32[432,128]{1,0:T(8,128)} %pad.4.refs_2_.kernel, bf16[432,864]{1,0:T(8,128)(2,1)} %constant.38.clone.refs_3_.left, ...), custom_call_target="tpu_custom_call" | custom-call | tf_op jit(solution)/shard_map/first_pair/pallas_call | solution.py:301
  27.5 0.0 collective-permute-done.4.far_in
  27.5 0.0 copy-start.4
  27.5 0.0 collective-permute-done.5.near_in
  27.6 0.0 copy-start.5
  27.6 0.7 %copy-done.4 = bf16[730,128]{1,0:T(8,128)(2,1)} copy-done((bf16[730,128]{1,0:T(8,128)(2,1)}, bf16[730,128]{1,0:T(8,128)(2,1)S(1)}, u32[]{:S(2)}) %copy-start.4) | copy-done | bytes 186904
  28.2 0.1 copy-done.5
  28.3 5.4 %second_pair.1 = (bf16[2,46656]{1,0:T(2,128)(2,1)}, f32[2,1,4]{2,1,0:T(1,128)}) custom-call(s32[4]{0:T(128)} %pad_add_fusion.place, f32[2,432,128]{2,1,0:T(8,128)} %get-tuple-element.7.own, f32[2,432,128]{2,1,0:T(8,128)} %get-tuple-element.8.accum, f32[3,2,432,128]{3,2,1,0:T(8,128)} %get-tuple-element.9.bands, bf16[730,128]{1,0:T(8,128)(2,1)} %copy-done.4, ...), custom_call_target="tpu_custom_call" | custom-call | tf_op jit(solution)/shard_map/second_pair/pallas_call | solution.py:302
  (1 shorter events, 0.0 us)
Async XLA Ops:
  3.1 7.9 %collective-permute-start.2 = (bf16[730,128]{1,0:T(8,128)(2,1)}, bf16[730,128]{1,0:T(8,128)(2,1)S(1)}, u32[]{:S(2)}, u32[]{:S(2)}) collective-permute-start(bf16[730,128]{1,0:T(8,128)(2,1)} %pack.1.refs_0_), channel_id=1, source_target_pairs={{0,2},{1,3},{2,0},{3,1},{4,6},{5,7},{6,4},{7,5},{8,10},{9,11},{10,... | collective-permute-start | bytes 560648 | tf_op jit(solution)/shard_map/ppermute | solution.py:276
  6.1 10.7 %collective-permute-start = (bf16[730,128]{1,0:T(8,128)(2,1)}, bf16[730,128]{1,0:T(8,128)(2,1)S(1)}, u32[]{:S(2)}, u32[]{:S(2)}) collective-permute-start(bf16[730,128]{1,0:T(8,128)(2,1)} %pack.1.refs_0_), channel_id=1, source_target_pairs={{0,4},{1,5},{2,6},{3,7},{4,8},{5,9},{6,10},{7,11},{8,12},{9,13},{1... | collective-permute-start | bytes 560648 | tf_op jit(solution)/shard_map/ppermute | solution.py:276
  7.6 12.8 %collective-permute-start.1 = (bf16[730,128]{1,0:T(8,128)(2,1)}, bf16[730,128]{1,0:T(8,128)(2,1)S(1)}, u32[]{:S(2)}, u32[]{:S(2)}) collective-permute-start(bf16[730,128]{1,0:T(8,128)(2,1)} %pack.1.refs_0_), channel_id=1, source_target_pairs={{0,1},{1,0},{2,3},{3,2},{4,5},{5,4},{6,7},{7,6},{8,9},{9,8},{10,11... | collective-permute-start | bytes 560648 | tf_op jit(solution)/shard_map/ppermute | solution.py:276
  7.6 19.9 %collective-permute-start.4 = (bf16[730,128]{1,0:T(8,128)(2,1)}, bf16[730,128]{1,0:T(8,128)(2,1)S(1)}, u32[]{:S(2)}, u32[]{:S(2)}) collective-permute-start(bf16[730,128]{1,0:T(8,128)(2,1)} %pack.1.refs_0_), channel_id=1, source_target_pairs={{0,1},{1,6},{2,3},{3,4},{4,5},{5,10},{6,7},{7,8},{8,9},{9,14},{10,... | collective-permute-start | bytes 560648 | tf_op jit(solution)/shard_map/ppermute | solution.py:276
  11.0 7.7 %copy-start.1 = (bf16[730,128]{1,0:T(8,128)(2,1)}, bf16[730,128]{1,0:T(8,128)(2,1)S(1)}, u32[]{:S(2)}) copy-start(bf16[730,128]{1,0:T(8,128)(2,1)S(1)} %collective-permute-done.2.refs_7_) | copy-start | bytes 560644
  11.0 9.4 %collective-permute-start.3 = (bf16[730,128]{1,0:T(8,128)(2,1)S(1)}, bf16[730,128]{1,0:T(8,128)(2,1)S(1)}, u32[]{:S(2)}, u32[]{:S(2)}) collective-permute-start(bf16[730,128]{1,0:T(8,128)(2,1)S(1)} %collective-permute-done.2.refs_7_), channel_id=1, source_target_pairs={{0,1},{1,0},{2,3},{3,2},{4,5},{5,4},{6,7},{7,6},{8,9},{9,8},{10,11... | collective-permute-start | bytes 560648 | tf_op jit(solution)/shard_map/ppermute | solution.py:276
  16.8 1.9 %copy-start = (bf16[730,128]{1,0:T(8,128)(2,1)}, bf16[730,128]{1,0:T(8,128)(2,1)S(1)}, u32[]{:S(2)}) copy-start(bf16[730,128]{1,0:T(8,128)(2,1)S(1)} %collective-permute-done.refs_1_) | copy-start | bytes 560644
  16.8 10.8 %collective-permute-start.5 = (bf16[730,128]{1,0:T(8,128)(2,1)S(1)}, bf16[730,128]{1,0:T(8,128)(2,1)S(1)}, u32[]{:S(2)}, u32[]{:S(2)}) collective-permute-start(bf16[730,128]{1,0:T(8,128)(2,1)S(1)} %collective-permute-done.refs_1_), channel_id=1, source_target_pairs={{0,1},{1,0},{2,3},{3,2},{4,5},{5,4},{6,7},{7,6},{8,9},{9,8},{10,11... | collective-permute-start | bytes 560648 | tf_op jit(solution)/shard_map/ppermute | solution.py:276
  20.4 0.7 %copy-start.2 = (bf16[730,128]{1,0:T(8,128)(2,1)}, bf16[730,128]{1,0:T(8,128)(2,1)S(1)}, u32[]{:S(2)}) copy-start(bf16[730,128]{1,0:T(8,128)(2,1)S(1)} %collective-permute-done.1.refs_6_) | copy-start | bytes 560644
  21.1 0.7 %copy-start.3 = (bf16[730,128]{1,0:T(8,128)(2,1)}, bf16[730,128]{1,0:T(8,128)(2,1)S(1)}, u32[]{:S(2)}) copy-start(bf16[730,128]{1,0:T(8,128)(2,1)S(1)} %collective-permute-done.3.refs_8_) | copy-start | bytes 560644
  27.5 0.7 %copy-start.4 = (bf16[730,128]{1,0:T(8,128)(2,1)}, bf16[730,128]{1,0:T(8,128)(2,1)S(1)}, u32[]{:S(2)}) copy-start(bf16[730,128]{1,0:T(8,128)(2,1)S(1)} %collective-permute-done.4.far_in) | copy-start | bytes 560644
  27.6 0.7 %copy-start.5 = (bf16[730,128]{1,0:T(8,128)(2,1)}, bf16[730,128]{1,0:T(8,128)(2,1)S(1)}, u32[]{:S(2)}) copy-start(bf16[730,128]{1,0:T(8,128)(2,1)S(1)} %collective-permute-done.5.near_in) | copy-start | bytes 560644

commit v2 on v1

v2 whole, which is shorter than its diff:
```python
import math

import jax
import jax.numpy as jnp
import numpy as np
from jax import lax
from jax.experimental import pallas as pl
from jax.experimental.pallas import tpu as pltpu
from jax.sharding import PartitionSpec as P


LANES = 128
F32 = jnp.float32
BF16 = jnp.bfloat16
VMEM = pl.BlockSpec(memory_space=pltpu.VMEM)
SMEM = pl.BlockSpec(memory_space=pltpu.SMEM)
HBM = pl.BlockSpec(memory_space=pl.ANY)


class Plan:
    def __init__(self, grid):
        ng = round(grid ** (1.0 / 3.0))
        self.grid = grid
        self.ng = ng
        self.split = max(b for b in range(1, ng + 1) if ng % b == 0 and b * ng <= LANES)
        self.coarse = ng // self.split
        self.width = self.split * ng
        self.rows = grid // self.width
        self.tiles = grid // LANES + 1
        self.tail = grid % LANES
        common = math.lcm(self.width, LANES)
        self.row_period = common // self.width
        self.tile_period = common // LANES
        self.blocks = -(-self.rows // self.row_period)
        self.kept = self.blocks * self.row_period
        self.padded_tiles = (self.blocks * self.tile_period + 15) // 8 * 8


def roots(ng, phases):
    angles = 2.0 * np.pi / ng * (phases % ng)
    return np.cos(angles), np.sin(angles)


def constants(plan):
    ng, split, coarse, width = plan.ng, plan.split, plan.coarse, plan.width
    j, block = np.divmod(np.arange(plan.kept), plan.blocks)
    row = block * plan.row_period + j
    real_row = row < plan.rows
    x, a = np.divmod(row, coarse)
    b, z = np.divmod(np.arange(width), ng)
    mask = np.outer(real_row, real_row)
    cosine, sine = roots(ng, np.outer(x, x) + split * np.outer(a, a))
    left = np.concatenate([cosine * mask, sine * mask], axis=1)
    cosine, sine = roots(ng, coarse * np.outer(b, b) + np.outer(z, z))
    right = np.zeros((2, 2, LANES, 2, LANES))
    for way, sign in enumerate((1.0, -1.0)):
        right[way, 0, :width, 0, :width] = cosine
        right[way, 1, :width, 1, :width] = cosine
        right[way, 1, :width, 0, :width] = sign * sine
        right[way, 0, :width, 1, :width] = -sign * sine
    twiddle = np.zeros((2, plan.kept, LANES))
    twiddle[0, :, :width], twiddle[1, :, :width] = roots(ng, np.outer(a, b))
    return (
        jnp.asarray(left, BF16),
        jnp.asarray(right.reshape(2, 2 * LANES, 2 * LANES), BF16),
        jnp.asarray(twiddle, F32),
    )


def pack(plan):
    def body(orbital, occupation, out):
        last = plan.tiles - 1
        for q in range(last):
            out[2 * q : 2 * q + 2, :] = orbital[:, LANES * q : LANES * (q + 1)]
        if plan.tail:
            out[2 * last :, : plan.tail] = orbital[:, LANES * last :]
        fill = jnp.full((2, LANES - plan.tail), occupation[0], jnp.int32)
        out[2 * last :, plan.tail :] = fill.astype(F32).astype(BF16)

    return pl.pallas_call(
        body,
        out_shape=jax.ShapeDtypeStruct((2 * plan.tiles, LANES), BF16),
        in_specs=[VMEM, SMEM],
        out_specs=VMEM,
        compiler_params=pltpu.CompilerParams(vmem_limit_bytes=4 * 1024 * 1024),
        name="pack",
    )


def shifted_rows(plan, tiles, first, step, j):
    q, shift = divmod(plan.width * j, LANES)
    stride = step * plan.tile_period
    rows = tiles[pl.ds(step * q + first, plan.blocks, stride=stride), :]
    if shift + plan.width > LANES:
        after = tiles[pl.ds(step * (q + 1) + first, plan.blocks, stride=stride), :]
        lane = lax.broadcasted_iota(jnp.int32, rows.shape, 1)
        rows = jnp.where(lane >= shift, rows, after)
    return pltpu.roll(rows, LANES - shift, axis=1) if shift else rows


def to_matrix(plan, packed, tiles, matrix):
    size = 2 * plan.tiles
    tiles[:size, :] = packed.astype(F32)
    tiles[size:, :] = jnp.zeros((2 * plan.padded_tiles - size, LANES), F32)
    for j in range(plan.row_period):
        for part in range(2):
            rows = shifted_rows(plan, tiles, part, 2, j)
            matrix[part, plan.blocks * j : plan.blocks * (j + 1), :] = rows


def from_matrix(plan, matrix, tiles):
    width, blocks = plan.width, plan.blocks
    for i in range(plan.tile_period):
        for part in range(2):
            row, offset = divmod(LANES * i, width)
            flat = None
            start = -offset
            while start < LANES:
                turn, j = divmod(row, plan.row_period)
                rows = matrix[part, blocks * j + turn : blocks * (j + 1) + turn, :]
                if start % LANES:
                    rows = pltpu.roll(rows, start % LANES, axis=1)
                if flat is None:
                    flat = rows
                else:
                    lane = lax.broadcasted_iota(jnp.int32, rows.shape, 1)
                    flat = jnp.where(lane < start, flat, rows)
                start += width
                row += 1
            tiles[blocks * (2 * i + part) : blocks * (2 * i + part + 1), :] = flat


def prepare(plan):
    split, coarse, ng = plan.split, plan.coarse, plan.ng

    def body(own_in, kernel_in, left, right, twiddle, own, factor, left_out, right_out, twiddle_out, tiles, plain, ordered, arrived):
        copies = [
            pltpu.make_async_copy(source, target, arrived.at[index])
            for index, (source, target) in enumerate(
                ((left, left_out), (right, right_out), (twiddle, twiddle_out))
            )
        ]
        for copy in copies:
            copy.start()
        to_matrix(plan, own_in[...], tiles, own)
        for j in range(plan.row_period):
            rows = shifted_rows(plan, kernel_in, 0, 1, j)
            plain[pl.ds(j, plan.blocks, stride=plan.row_period), :] = rows * (1.0 / plan.grid)
        lane = lax.broadcasted_iota(jnp.int32, (ng, LANES), 1)
        for a in range(coarse):
            rows = None
            for b in range(split):
                row, column = divmod(a + coarse * b, split)
                piece = plain[pl.ds(row, ng, stride=coarse), :]
                shift = (ng * (b - column)) % LANES
                if shift:
                    piece = pltpu.roll(piece, shift, axis=1)
                rows = piece if rows is None else jnp.where(lane < ng * b, rows, piece)
            ordered[pl.ds(a, ng, stride=coarse), :] = rows
        ordered[plan.rows :, :] = jnp.zeros((plan.kept - plan.rows, LANES), F32)
        for j in range(plan.row_period):
            rows = ordered[pl.ds(j, plan.blocks, stride=plan.row_period), :]
            factor[plan.blocks * j : plan.blocks * (j + 1), :] = rows
        for copy in copies:
            copy.wait()

    return pl.pallas_call(
        body,
        out_shape=[
            jax.ShapeDtypeStruct((2, plan.kept, LANES), F32),
            jax.ShapeDtypeStruct((plan.kept, LANES), F32),
            jax.ShapeDtypeStruct((plan.kept, 2 * plan.kept), BF16),
            jax.ShapeDtypeStruct((2, 2 * LANES, 2 * LANES), BF16),
            jax.ShapeDtypeStruct((2, plan.kept, LANES), F32),
        ],
        in_specs=[VMEM] * 2 + [HBM] * 3,
        out_specs=[VMEM] * 5,
        scratch_shapes=[
            pltpu.VMEM((2 * plan.padded_tiles, LANES), F32),
            pltpu.VMEM((plan.kept, LANES), F32),
            pltpu.VMEM((plan.kept, LANES), F32),
            pltpu.SemaphoreType.DMA((3,)),
        ],
        compiler_params=pltpu.CompilerParams(vmem_limit_bytes=4 * 1024 * 1024),
        name="prepare",
    )


def exchange(plan, own, packed, tiles, near, fourier, kernel, left, right, twiddle):
    rows = plan.kept
    to_matrix(plan, packed, tiles, near)
    c = own[0]
    d = own[1]
    a = near[0]
    b = near[1]

    def put(real, imag, sign):
        real = real.astype(BF16)
        imag = imag.astype(BF16)
        fourier[:rows, :LANES] = real
        fourier[:rows, LANES:] = imag
        fourier[rows:, :LANES] = imag if sign > 0 else -imag
        fourier[rows:, LANES:] = -real if sign > 0 else real

    def dot(x, y):
        return jnp.dot(x, y, preferred_element_type=F32)

    put(a * c + b * d, a * d - b * c, 1)
    half = dot(left[...], fourier[...])
    real, imag = half[:, :LANES], half[:, LANES:]
    cosine = twiddle[0]
    sine = twiddle[1]
    turned = jnp.concatenate(
        [real * cosine + imag * sine, imag * cosine - real * sine], axis=1
    ).astype(BF16)
    spectrum = dot(turned, right[0])
    factor = kernel[...]
    screened = jnp.concatenate(
        [spectrum[:, :LANES] * factor, spectrum[:, LANES:] * factor], axis=1
    ).astype(BF16)
    half = dot(screened, right[1])
    real, imag = half[:, :LANES], half[:, LANES:]
    put(real * cosine - imag * sine, imag * cosine + real * sine, -1)
    potential = dot(left[...], fourier[...])
    e = potential[:, :LANES]
    f = potential[:, LANES:]
    last = 2 * plan.tiles - 2
    weight = -0.5 * tiles[last : last + 1, plan.tail : plan.tail + 1]
    a = near[0]
    b = near[1]
    return weight * (a * e - b * f), weight * (a * f + b * e)


def scratch_of(plan):
    return [
        pltpu.VMEM((2 * plan.padded_tiles, LANES), F32),
        pltpu.VMEM((2, plan.kept, LANES), F32),
        pltpu.VMEM((2 * plan.kept, 2 * LANES), BF16),
    ]


def first_pair(plan):
    def body(own, near_in, kernel, left, right, twiddle, pair_in, accum, pair, tiles, near, fourier):
        real, imag = exchange(plan, own, near_in[...], tiles, near, fourier, kernel, left, right, twiddle)
        accum[0] = real
        accum[1] = imag
        to_matrix(plan, pair_in[...], tiles, pair)

    matrix = jax.ShapeDtypeStruct((2, plan.kept, LANES), F32)
    return pl.pallas_call(
        body,
        out_shape=[matrix, matrix],
        in_specs=[VMEM] * 7,
        out_specs=[VMEM] * 2,
        scratch_shapes=scratch_of(plan),
        compiler_params=pltpu.CompilerParams(vmem_limit_bytes=16 * 1024 * 1024),
        name="first_pair",
    )


def second_pair(plan):
    def body(place, own, accum, far_in, near_in, kernel, left, right, twiddle, total, tiles, near, fourier):
        packed = jnp.where(place[0] % 2 == 1, near_in[...], far_in[...])
        real, imag = exchange(plan, own, packed, tiles, near, fourier, kernel, left, right, twiddle)
        total[0] = (accum[0] + real).astype(BF16).astype(F32)
        total[1] = (accum[1] + imag).astype(BF16).astype(F32)

    return pl.pallas_call(
        body,
        out_shape=jax.ShapeDtypeStruct((2, plan.kept, LANES), F32),
        in_specs=[SMEM] + [VMEM] * 8,
        out_specs=VMEM,
        scratch_shapes=scratch_of(plan),
        compiler_params=pltpu.CompilerParams(vmem_limit_bytes=16 * 1024 * 1024),
        name="second_pair",
    )


def finish(plan, others):
    count = others + 1

    def body(*refs):
        place, total, own, pair = refs[:4]
        bands = refs[4 : 3 + others]
        out, gram, tiles, matrix, flat, sent = refs[3 + others :]
        from_matrix(plan, total, tiles)
        for q in range(plan.tiles):
            turn, i = divmod(q, plan.tile_period)
            pair_rows = tiles[pl.ds(2 * plan.blocks * i + turn, 2, stride=plan.blocks), :].astype(BF16)
            used = min(LANES, plan.grid - LANES * q)
            if used:
                flat[:, LANES * q : LANES * q + used] = pair_rows[:, :used]
        copy = pltpu.make_async_copy(flat, out, sent)
        copy.start()
        lane = lax.broadcasted_iota(jnp.int32, (1, count), 1)
        sums = [jnp.zeros((1, count), F32)] * 2
        norm = 1.0 / math.sqrt(plan.grid)
        e = total[0]
        f = total[1]
        for index in range(count):
            if index < 2:
                band = (own, pair)[index]
                c, d = band[0], band[1]
            else:
                to_matrix(plan, bands[index - 2][...], tiles, matrix)
                c, d = matrix[0], matrix[1]
            parts = (c * e + d * f, c * f - d * e)
            for part in range(2):
                value = jnp.sum(jnp.sum(parts[part], axis=0, keepdims=True), axis=1, keepdims=True)
                sums[part] = jnp.where(lane == place[index], value * norm, sums[part])
        for part in range(2):
            gram[part] = sums[part]
        copy.wait()

    return pl.pallas_call(
        body,
        out_shape=[
            jax.ShapeDtypeStruct((2, plan.grid), BF16),
            jax.ShapeDtypeStruct((2, 1, count), F32),
        ],
        in_specs=[SMEM] + [VMEM] * (2 + others),
        out_specs=[HBM, VMEM],
        scratch_shapes=[
            pltpu.VMEM((2 * plan.padded_tiles, LANES), F32),
            pltpu.VMEM((2, plan.kept, LANES), F32),
            pltpu.VMEM((2, plan.grid), BF16),
            pltpu.SemaphoreType.DMA,
        ],
        compiler_params=pltpu.CompilerParams(vmem_limit_bytes=16 * 1024 * 1024),
        name="finish",
    )


def shards(orbitals, occupation, kernel):
    plan = Plan(orbitals.shape[3])
    pools = lax.axis_size("pool")
    groups = lax.axis_size("band")
    others = groups - 1

    def move(array, target):
        pairs = [
            (p * groups + g, q * groups + h)
            for p in range(pools)
            for g in range(groups)
            for q, h in [target(p, g)]
        ]
        return lax.ppermute(array, ("pool", "band"), pairs)

    here = lax.axis_index("band")
    places = [here, here ^ 1]
    for step in range(1, groups // 2):
        places += [(here - 2 * step) % groups, ((here ^ 1) - 2 * step) % groups]
    place = jnp.stack(places).astype(jnp.int32)
    own = pack(plan)(orbitals[0, 0], occupation[0])
    near = move(own, lambda p, g: ((p + 1) % pools, g))
    far = move(own, lambda p, g: ((p + 1) % pools, (g + 1) % groups) if g % 2 else (p, g + 1))
    partner = lambda p, g: (p, g ^ 1)
    bands = [move(own, partner)]
    for step in range(1, groups // 2):
        shifted = move(own, lambda p, g: (p, (g + 2 * step) % groups))
        bands += [shifted, move(shifted, partner)]
    swapped = move(near, partner)
    padded = jnp.pad(kernel, (0, plan.padded_tiles * LANES - plan.grid))
    mine, factor, left, right, twiddle = prepare(plan)(
        own, padded.reshape(-1, LANES), *constants(plan)
    )
    accum, pair = first_pair(plan)(mine, near, factor, left, right, twiddle, bands[0])
    total = second_pair(plan)(place, mine, accum, far, swapped, factor, left, right, twiddle)
    exchanged, gram = finish(plan, others)(place, total, mine, pair, *bands[1:])
    return exchanged[None, None], jnp.swapaxes(gram, 1, 2)[None]


def solution(mesh):
    return jax.shard_map(
        shards,
        mesh=mesh,
        in_specs=(P("pool", "band", None, None), P("pool", "band"), P()),
        out_specs=(P("pool", "band", None, None), P("pool", None, None, "band")),
        check_vma=False,
    )
```

time: 33.9 us -> 25.3 us (0.75)
  Pallas kernels: 13 us -> 7.81 us
  waiting for transfers between devices: 8.68 us -> 6.38 us
  other arithmetic: 1.68 us -> 0.08 us
  starting transfers between devices: 5 us -> 5.56 us
    pallas_call x2 -> x4, Pallas kernels: 11.1 us -> 7.57 us  [the longest x1 2.71 us: shards(): exchanged, gram = finish(plan, others)(place, total, mine, pair, *bands[1:])]
    ppermute x6, waiting for transfers between devices: 8.68 us -> 6.38 us  [move(): return lax.ppermute(array, ('pool', 'band'), pairs)]
    pallas_call x1, Pallas kernels: 1.84 us -> 0.24 us  [shards(): own = pack(plan)(orbitals[0, 0], occupation[0])]
    mul x3 -> x0, local copies, waits for them, and re-layouts: 1.17 us -> none  [shards(): factor = factor.reshape(plan.rows, plan.width) * (1.0 / plan.grid)]
    mul x1 -> x0, other arithmetic: 1.01 us -> none  [shards(): factor = factor.reshape(plan.rows, plan.width) * (1.0 / plan.grid)]
    reshape x0 -> x1, local copies, waits for them, and re-layouts: none -> 0.94 us  [shards(): padded.reshape(-1, LANES)]
    unnamed x12 -> x8, local copies, waits for them, and re-layouts: 2.07 us -> 2.89 us
    pad x1 -> x0, local copies, waits for them, and re-layouts: 0.7 us -> none  [shards(): factor = jnp.pad(factor, ((0, 0), (0, LANES - plan.width)))]
  transfers between devices with their start and end apart: 6 -> 6, of which waited for: 2 -> 1; matrix products, arithmetic and copies ran while one was open for 11% -> 4% of each run, Pallas kernels for 17% -> 19%
where the time goes in v2:
time: 25.3 us; the launch traced here: 25.1 us
  Pallas kernels  7.81 us (31%)
  waiting for transfers between devices  6.38 us (25%)
  starting transfers between devices  5.56 us (22%)
  local copies, waits for them, and re-layouts  3.82 us (15%)
  between operations  1.44 us (6%)
    ppermute x6, waiting for transfers between devices, move(): return lax.ppermute(array, ('pool', 'band'), pairs)  6.38 us
    ppermute x6, starting transfers between devices, move(): return lax.ppermute(array, ('pool', 'band'), pairs)  5.56 us
    unnamed x8, local copies, waits for them, and re-layouts  2.89 us
    pallas_call x1, Pallas kernels, shards(): exchanged, gram = finish(plan, others)(place, total, mine, pair, *bands[1:])  2.71 us
    pallas_call x1, Pallas kernels, shards(): second_pair(plan)  2.18 us
    pallas_call x1, Pallas kernels, shards(): first_pair(plan)(mine, near, factor, left, right, twiddle, bands[0])  1.65 us
    pallas_call x1, Pallas kernels, shards(): prepare(plan)(own, padded.reshape(-1, LANES), *constants(plan))  1.03 us
    reshape x1, local copies, waits for them, and re-layouts, shards(): padded.reshape(-1, LANES)  0.94 us
  transfers between devices with their start and end apart: 6, of which 1 were waited for; matrix products, arithmetic and copies ran while one was open for 4% of the time, Pallas kernels for 19%

profile of v2, /device:TPU:0, one launch (start us, length us, event | category | flops | bytes accessed | tf_op | source)
XLA Modules:
  0.0 25.1 jit_solution(8138209552095713123)
XLA Ops:
  0.6 0.0 copy-start
  1.4 0.0 copy-start.3
  1.4 0.9 %copy-done.3 = bf16[1,1,2,46656]{3,2,1,0:T(2,128)(2,1)S(1)} copy-done((bf16[1,1,2,46656]{3,2,1,0:T(2,128)(2,1)S(1)}, bf16[1,1,2,46656]{3,2,1,0:T(2,128)(2,1)}, u32[]{:S(2)}) %copy-start.3) | copy-done | bytes 186648
  2.3 0.2 pack.1.own_in
  2.5 3.0 %collective-permute-start = (bf16[730,128]{1,0:T(8,128)(2,1)S(1)}, bf16[730,128]{1,0:T(8,128)(2,1)S(1)}, u32[]{:S(2)}, u32[]{:S(2)}) collective-permute-start(bf16[730,128]{1,0:T(8,128)(2,1)S(1)} %pack.1.own_in), channel_id=1, source_target_pairs={{0,4},{1,5},{2,6},{3,7},{4,8},{5,9},{6,10},{7,11},{8,12},{9,13},{1... | collective-permute-start | bytes 560648 | tf_op jit(solution)/shard_map/ppermute | solution.py:347
  5.6 1.5 %collective-permute-start.4 = (bf16[730,128]{1,0:T(8,128)(2,1)S(1)}, bf16[730,128]{1,0:T(8,128)(2,1)S(1)}, u32[]{:S(2)}, u32[]{:S(2)}) collective-permute-start(bf16[730,128]{1,0:T(8,128)(2,1)S(1)} %pack.1.own_in), channel_id=1, source_target_pairs={{0,2},{1,3},{2,0},{3,1},{4,6},{5,7},{6,4},{7,5},{8,10},{9,11},{10,... | collective-permute-start | bytes 560648 | tf_op jit(solution)/shard_map/ppermute | solution.py:347
  7.1 0.0 collective-permute-start.1
  7.1 0.5 %collective-permute-start.2 = (bf16[730,128]{1,0:T(8,128)(2,1)S(1)}, bf16[730,128]{1,0:T(8,128)(2,1)S(1)}, u32[]{:S(2)}, u32[]{:S(2)}) collective-permute-start(bf16[730,128]{1,0:T(8,128)(2,1)S(1)} %pack.1.own_in), channel_id=1, source_target_pairs={{0,1},{1,6},{2,3},{3,4},{4,5},{5,10},{6,7},{7,8},{8,9},{9,14},{10,... | collective-permute-start | bytes 560648 | tf_op jit(solution)/shard_map/ppermute | solution.py:347
  7.6 6.4 %collective-permute-done.near_in = bf16[730,128]{1,0:T(8,128)(2,1)S(1)} collective-permute-done((bf16[730,128]{1,0:T(8,128)(2,1)S(1)}, bf16[730,128]{1,0:T(8,128)(2,1)S(1)}, u32[]{:S(2)}, u32[]{:S(2)}) %collective-permute-start) | collective-permute-done | bytes 186912 | tf_op jit(solution)/shard_map/ppermute | solution.py:347
  14.0 0.0 collective-permute-start.3
  14.0 0.0 collective-permute-done.4.refs_4_
  14.0 0.5 %collective-permute-start.5 = (bf16[730,128]{1,0:T(8,128)(2,1)S(1)}, bf16[730,128]{1,0:T(8,128)(2,1)S(1)}, u32[]{:S(2)}, u32[]{:S(2)}) collective-permute-start(bf16[730,128]{1,0:T(8,128)(2,1)S(1)} %collective-permute-done.4.refs_4_), channel_id=1, source_target_pairs={{0,1},{1,0},{2,3},{3,2},{4,5},{5,4},{6,7},{7,6},{8,9},{9,8},{10,11... | collective-permute-start | bytes 560648 | tf_op jit(solution)/shard_map/ppermute | solution.py:347
  14.5 0.9 %pad_bitcast_fusion.kernel_in = f32[392,128]{1,0:T(8,128)S(1)} fusion(f32[46656]{0:T(1024)} %param.8), kind=kLoop, calls=%fused_computation | loop fusion | bytes 387328 | tf_op jit(solution)/shard_map/reshape | solution.py:365
  15.4 0.0 copy-done
  15.4 0.0 copy-start.1
  15.4 1.0 %copy-done.1 = f32[2,448,128]{2,1,0:T(8,128)S(1)} copy-done((f32[2,448,128]{2,1,0:T(8,128)S(1)}, f32[2,448,128]{2,1,0:T(8,128)}, u32[]{:S(2)}) %copy-start.1) | copy-done | bytes 458776
  16.4 0.0 copy-start.2
  16.4 0.9 %copy-done.2 = bf16[2,256,256]{2,1,0:T(8,128)(2,1)S(1)} copy-done((bf16[2,256,256]{2,1,0:T(8,128)(2,1)S(1)}, bf16[2,256,256]{2,1,0:T(8,128)(2,1)}, u32[]{:S(2)}) %copy-start.2) | copy-done | bytes 262168
  17.4 1.0 %prepare.1 = (f32[2,448,128]{2,1,0:T(8,128)S(1)}, f32[448,128]{1,0:T(8,128)S(1)}, bf16[448,896]{1,0:T(8,128)(2,1)S(1)}, bf16[2,256,256]{2,1,0:T(8,128)(2,1)S(1)}, f32[2,448,128]{2,1,0:T(8,128)S(1)}) custom-call(bf16[730,128]{1,0:T(8,128)(2,1)S(1)} %pack.1.own_in, f32[392,128]{1,0:T(8,128)S(1)} %pad_bitcast_fusion.kernel_in, bf16[448,896]{1,0:T(8,128)(2,1)S(1)} %copy-done, ...), custom_call_target="tpu_custom_call" | custom-call | tf_op jit(solution)/shard_map/prepare/pallas_call | solution.py:364
  18.4 0.1 pad_add_fusion.place.refs_0_
  18.5 0.0 collective-permute-done.1.pair_in
  18.5 1.6 %first_pair.1 = (f32[2,448,128]{2,1,0:T(8,128)S(1)}, f32[2,448,128]{2,1,0:T(8,128)S(1)}) custom-call(f32[2,448,128]{2,1,0:T(8,128)S(1)} %get-tuple-element.11.own.refs_2_, bf16[730,128]{1,0:T(8,128)(2,1)S(1)} %collective-permute-done.near_in, f32[448,128]{1,0:T(8,128)S(1)} %get-tuple-element.12.kernel, bf16[448,896]{1,0:T(8,128)(2,1)S(1)} %get-tuple-element.13.left, ...), custom_call_target="tpu_custom_call" | custom-call | tf_op jit(solution)/shard_map/first_pair/pallas_call | solution.py:367
  20.2 0.0 collective-permute-done.2.far_in
  20.2 0.0 collective-permute-done.3.near_in
  20.2 2.2 %second_pair.1.refs_1_ = f32[2,448,128]{2,1,0:T(8,128)S(1)} custom-call(s32[4]{0:T(128)S(1)} %pad_add_fusion.place.refs_0_, f32[2,448,128]{2,1,0:T(8,128)S(1)} %get-tuple-element.11.own.refs_2_, f32[2,448,128]{2,1,0:T(8,128)S(1)} %get-tuple-element.16.accum, bf16[730,128]{1,0:T(8,128)(2,1)S(1)} %collective-permute-done.2.far_in, ...), custom_call_target="tpu_custom_call" | custom-call | tf_op jit(solution)/shard_map/second_pair/pallas_call | solution.py:368
  22.4 0.0 collective-permute-done.5.refs_5_
  22.4 2.7 %finish.1 = (bf16[2,46656]{1,0:T(2,128)(2,1)}, f32[2,1,4]{2,1,0:T(1,128)}) custom-call(s32[4]{0:T(128)S(1)} %pad_add_fusion.place.refs_0_, f32[2,448,128]{2,1,0:T(8,128)S(1)} %second_pair.1.refs_1_, f32[2,448,128]{2,1,0:T(8,128)S(1)} %get-tuple-element.11.own.refs_2_, f32[2,448,128]{2,1,0:T(8,128)S(1)} %get-tuple-element.17.refs_3_, ...), custom_call_target="tpu_custom_call" | custom-call | tf_op jit(solution)/shard_map/finish/pallas_call | solution.py:369
Async XLA Ops:
  0.6 14.8 %copy-start = (bf16[448,896]{1,0:T(8,128)(2,1)S(1)}, bf16[448,896]{1,0:T(8,128)(2,1)}, u32[]{:S(2)}) copy-start(bf16[448,896]{1,0:T(8,128)(2,1)} %constant.36.clone.left) | copy-start | bytes 2408452
  1.4 0.9 %copy-start.3 = (bf16[1,1,2,46656]{3,2,1,0:T(2,128)(2,1)S(1)}, bf16[1,1,2,46656]{3,2,1,0:T(2,128)(2,1)}, u32[]{:S(2)}) copy-start(bf16[1,1,2,46656]{3,2,1,0:T(2,128)(2,1)} %param.6) | copy-start | bytes 559876
  2.5 11.4 %collective-permute-start = (bf16[730,128]{1,0:T(8,128)(2,1)S(1)}, bf16[730,128]{1,0:T(8,128)(2,1)S(1)}, u32[]{:S(2)}, u32[]{:S(2)}) collective-permute-start(bf16[730,128]{1,0:T(8,128)(2,1)S(1)} %pack.1.own_in), channel_id=1, source_target_pairs={{0,4},{1,5},{2,6},{3,7},{4,8},{5,9},{6,10},{7,11},{8,12},{9,13},{1... | collective-permute-start | bytes 560648 | tf_op jit(solution)/shard_map/ppermute | solution.py:347
  5.6 8.4 %collective-permute-start.4 = (bf16[730,128]{1,0:T(8,128)(2,1)S(1)}, bf16[730,128]{1,0:T(8,128)(2,1)S(1)}, u32[]{:S(2)}, u32[]{:S(2)}) collective-permute-start(bf16[730,128]{1,0:T(8,128)(2,1)S(1)} %pack.1.own_in), channel_id=1, source_target_pairs={{0,2},{1,3},{2,0},{3,1},{4,6},{5,7},{6,4},{7,5},{8,10},{9,11},{10,... | collective-permute-start | bytes 560648 | tf_op jit(solution)/shard_map/ppermute | solution.py:347
  7.1 11.4 %collective-permute-start.1 = (bf16[730,128]{1,0:T(8,128)(2,1)S(1)}, bf16[730,128]{1,0:T(8,128)(2,1)S(1)}, u32[]{:S(2)}, u32[]{:S(2)}) collective-permute-start(bf16[730,128]{1,0:T(8,128)(2,1)S(1)} %pack.1.own_in), channel_id=1, source_target_pairs={{0,1},{1,0},{2,3},{3,2},{4,5},{5,4},{6,7},{7,6},{8,9},{9,8},{10,11... | collective-permute-start | bytes 560648 | tf_op jit(solution)/shard_map/ppermute | solution.py:347
  7.1 13.1 %collective-permute-start.2 = (bf16[730,128]{1,0:T(8,128)(2,1)S(1)}, bf16[730,128]{1,0:T(8,128)(2,1)S(1)}, u32[]{:S(2)}, u32[]{:S(2)}) collective-permute-start(bf16[730,128]{1,0:T(8,128)(2,1)S(1)} %pack.1.own_in), channel_id=1, source_target_pairs={{0,1},{1,6},{2,3},{3,4},{4,5},{5,10},{6,7},{7,8},{8,9},{9,14},{10,... | collective-permute-start | bytes 560648 | tf_op jit(solution)/shard_map/ppermute | solution.py:347
  14.0 6.2 %collective-permute-start.3 = (bf16[730,128]{1,0:T(8,128)(2,1)S(1)}, bf16[730,128]{1,0:T(8,128)(2,1)S(1)}, u32[]{:S(2)}, u32[]{:S(2)}) collective-permute-start(bf16[730,128]{1,0:T(8,128)(2,1)S(1)} %collective-permute-done.near_in), channel_id=1, source_target_pairs={{0,1},{1,0},{2,3},{3,2},{4,5},{5,4},{6,7},{7,6},{8,9},{9,8},{10,11... | collective-permute-start | bytes 560648 | tf_op jit(solution)/shard_map/ppermute | solution.py:347
  14.0 8.4 %collective-permute-start.5 = (bf16[730,128]{1,0:T(8,128)(2,1)S(1)}, bf16[730,128]{1,0:T(8,128)(2,1)S(1)}, u32[]{:S(2)}, u32[]{:S(2)}) collective-permute-start(bf16[730,128]{1,0:T(8,128)(2,1)S(1)} %collective-permute-done.4.refs_4_), channel_id=1, source_target_pairs={{0,1},{1,0},{2,3},{3,2},{4,5},{5,4},{6,7},{7,6},{8,9},{9,8},{10,11... | collective-permute-start | bytes 560648 | tf_op jit(solution)/shard_map/ppermute | solution.py:347
  15.4 1.0 %copy-start.1 = (f32[2,448,128]{2,1,0:T(8,128)S(1)}, f32[2,448,128]{2,1,0:T(8,128)}, u32[]{:S(2)}) copy-start(f32[2,448,128]{2,1,0:T(8,128)} %constant.38.clone.twiddle) | copy-start | bytes 1376260
  16.4 0.9 %copy-start.2 = (bf16[2,256,256]{2,1,0:T(8,128)(2,1)S(1)}, bf16[2,256,256]{2,1,0:T(8,128)(2,1)}, u32[]{:S(2)}) copy-start(bf16[2,256,256]{2,1,0:T(8,128)(2,1)} %constant.37.clone.right) | copy-start | bytes 786436

commit v3 on v2

--- a/solution.py
+++ b/solution.py
@@ -10,11 +10,12 @@
 
 
 LANES = 128
+PARTS = 2
 F32 = jnp.float32
 BF16 = jnp.bfloat16
 VMEM = pl.BlockSpec(memory_space=pltpu.VMEM)
 SMEM = pl.BlockSpec(memory_space=pltpu.SMEM)
-HBM = pl.BlockSpec(memory_space=pl.ANY)
+ANYWHERE = pl.BlockSpec(memory_space=pl.ANY)
 
 
 class Plan:
@@ -133,18 +134,19 @@
 def prepare(plan):
     split, coarse, ng = plan.split, plan.coarse, plan.ng
 
-    def body(own_in, kernel_in, left, right, twiddle, own, factor, left_out, right_out, twiddle_out, tiles, plain, ordered, arrived):
-        copies = [
-            pltpu.make_async_copy(source, target, arrived.at[index])
-            for index, (source, target) in enumerate(
-                ((left, left_out), (right, right_out), (twiddle, twiddle_out))
-            )
-        ]
-        for copy in copies:
-            copy.start()
+    def body(own_in, kernel_in, left, right, twiddle, own, factor, tiles, plain, ordered):
+        del left, right, twiddle
         to_matrix(plan, own_in[...], tiles, own)
+        eight = 8 * LANES
+        for q in range(0, plan.grid // eight):
+            tiles[8 * q : 8 * q + 8, :] = kernel_in[eight * q : eight * (q + 1)].reshape(8, LANES)
+        for q in range(plan.grid // eight * 8, plan.grid // LANES):
+            tiles[q : q + 1, :] = kernel_in[LANES * q : LANES * (q + 1)].reshape(1, LANES)
+        if plan.tail:
+            q = plan.grid // LANES
+            tiles[q : q + 1, : plan.tail] = kernel_in[LANES * q :].reshape(1, plan.tail)
         for j in range(plan.row_period):
-            rows = shifted_rows(plan, kernel_in, 0, 1, j)
+            rows = shifted_rows(plan, tiles, 0, 1, j)
             plain[pl.ds(j, plan.blocks, stride=plan.row_period), :] = rows * (1.0 / plan.grid)
         lane = lax.broadcasted_iota(jnp.int32, (ng, LANES), 1)
         for a in range(coarse):
@@ -161,25 +163,19 @@
         for j in range(plan.row_period):
             rows = ordered[pl.ds(j, plan.blocks, stride=plan.row_period), :]
             factor[plan.blocks * j : plan.blocks * (j + 1), :] = rows
-        for copy in copies:
-            copy.wait()
 
     return pl.pallas_call(
         body,
         out_shape=[
             jax.ShapeDtypeStruct((2, plan.kept, LANES), F32),
             jax.ShapeDtypeStruct((plan.kept, LANES), F32),
-            jax.ShapeDtypeStruct((plan.kept, 2 * plan.kept), BF16),
-            jax.ShapeDtypeStruct((2, 2 * LANES, 2 * LANES), BF16),
-            jax.ShapeDtypeStruct((2, plan.kept, LANES), F32),
         ],
-        in_specs=[VMEM] * 2 + [HBM] * 3,
-        out_specs=[VMEM] * 5,
+        in_specs=[VMEM] * 2 + [ANYWHERE] * 3,
+        out_specs=[VMEM] * 2,
         scratch_shapes=[
             pltpu.VMEM((2 * plan.padded_tiles, LANES), F32),
             pltpu.VMEM((plan.kept, LANES), F32),
             pltpu.VMEM((plan.kept, LANES), F32),
-            pltpu.SemaphoreType.DMA((3,)),
         ],
         compiler_params=pltpu.CompilerParams(vmem_limit_bytes=4 * 1024 * 1024),
         name="prepare",
@@ -194,41 +190,53 @@
     a = near[0]
     b = near[1]
 
-    def put(real, imag, sign):
+    step = rows // PARTS
+    parts = [slice(step * index, step * (index + 1)) for index in range(PARTS)]
+
+    def put(part, real, imag, sign):
         real = real.astype(BF16)
         imag = imag.astype(BF16)
-        fourier[:rows, :LANES] = real
-        fourier[:rows, LANES:] = imag
-        fourier[rows:, :LANES] = imag if sign > 0 else -imag
-        fourier[rows:, LANES:] = -real if sign > 0 else real
+        below = slice(rows + part.start, rows + part.stop)
+        fourier[part, :LANES] = real
+        fourier[part, LANES:] = imag
+        fourier[below, :LANES] = imag if sign > 0 else -imag
+        fourier[below, LANES:] = -real if sign > 0 else real
 
     def dot(x, y):
         return jnp.dot(x, y, preferred_element_type=F32)
 
-    put(a * c + b * d, a * d - b * c, 1)
-    half = dot(left[...], fourier[...])
-    real, imag = half[:, :LANES], half[:, LANES:]
-    cosine = twiddle[0]
-    sine = twiddle[1]
-    turned = jnp.concatenate(
-        [real * cosine + imag * sine, imag * cosine - real * sine], axis=1
-    ).astype(BF16)
-    spectrum = dot(turned, right[0])
-    factor = kernel[...]
-    screened = jnp.concatenate(
-        [spectrum[:, :LANES] * factor, spectrum[:, LANES:] * factor], axis=1
-    ).astype(BF16)
-    half = dot(screened, right[1])
-    real, imag = half[:, :LANES], half[:, LANES:]
-    put(real * cosine - imag * sine, imag * cosine + real * sine, -1)
-    potential = dot(left[...], fourier[...])
-    e = potential[:, :LANES]
-    f = potential[:, LANES:]
+    def split(value):
+        return value[:, :LANES], value[:, LANES:]
+
+    for part in parts:
+        a, b, c, d = near[0, part, :], near[1, part, :], own[0, part, :], own[1, part, :]
+        put(part, a * c + b * d, a * d - b * c, 1)
+    halves = [dot(left[part, :], fourier[...]) for part in parts]
+    for index, part in enumerate(parts):
+        real, imag = split(halves[index])
+        cosine, sine = twiddle[0, part, :], twiddle[1, part, :]
+        halves[index] = jnp.concatenate(
+            [real * cosine + imag * sine, imag * cosine - real * sine], axis=1
+        ).astype(BF16)
+    halves = [dot(value, right[0]) for value in halves]
+    for index, part in enumerate(parts):
+        real, imag = split(halves[index])
+        factor = kernel[part, :]
+        halves[index] = jnp.concatenate([real * factor, imag * factor], axis=1).astype(BF16)
+    halves = [dot(value, right[1]) for value in halves]
+    for index, part in enumerate(parts):
+        real, imag = split(halves[index])
+        cosine, sine = twiddle[0, part, :], twiddle[1, part, :]
+        put(part, real * cosine - imag * sine, imag * cosine + real * sine, -1)
+    potential = [dot(left[part, :], fourier[...]) for part in parts]
+    results = []
     last = 2 * plan.tiles - 2
     weight = -0.5 * tiles[last : last + 1, plan.tail : plan.tail + 1]
-    a = near[0]
-    b = near[1]
-    return weight * (a * e - b * f), weight * (a * f + b * e)
+    for index, part in enumerate(parts):
+        e, f = split(potential[index])
+        a, b = near[0, part, :], near[1, part, :]
+        results.append((part, weight * (a * e - b * f), weight * (a * f + b * e)))
+    return results
 
 
 def scratch_of(plan):
@@ -241,9 +249,10 @@
 
 def first_pair(plan):
     def body(own, near_in, kernel, left, right, twiddle, pair_in, accum, pair, tiles, near, fourier):
-        real, imag = exchange(plan, own, near_in[...], tiles, near, fourier, kernel, left, right, twiddle)
-        accum[0] = real
-        accum[1] = imag
+        results = exchange(plan, own, near_in[...], tiles, near, fourier, kernel, left, right, twiddle)
+        for part, real, imag in results:
+            accum[0, part, :] = real
+            accum[1, part, :] = imag
         to_matrix(plan, pair_in[...], tiles, pair)
 
     matrix = jax.ShapeDtypeStruct((2, plan.kept, LANES), F32)
@@ -261,15 +270,17 @@
 def second_pair(plan):
     def body(place, own, accum, far_in, near_in, kernel, left, right, twiddle, total, tiles, near, fourier):
         packed = jnp.where(place[0] % 2 == 1, near_in[...], far_in[...])
-        real, imag = exchange(plan, own, packed, tiles, near, fourier, kernel, left, right, twiddle)
-        total[0] = (accum[0] + real).astype(BF16).astype(F32)
-        total[1] = (accum[1] + imag).astype(BF16).astype(F32)
+        results = exchange(plan, own, packed, tiles, near, fourier, kernel, left, right, twiddle)
+        for part, real, imag in results:
+            total[0, part, :] = (accum[0, part, :] + real).astype(BF16).astype(F32)
+            total[1, part, :] = (accum[1, part, :] + imag).astype(BF16).astype(F32)
 
     return pl.pallas_call(
         body,
         out_shape=jax.ShapeDtypeStruct((2, plan.kept, LANES), F32),
         in_specs=[SMEM] + [VMEM] * 8,
         out_specs=VMEM,
+        input_output_aliases={2: 0},
         scratch_shapes=scratch_of(plan),
         compiler_params=pltpu.CompilerParams(vmem_limit_bytes=16 * 1024 * 1024),
         name="second_pair",
@@ -292,24 +303,34 @@
                 flat[:, LANES * q : LANES * q + used] = pair_rows[:, :used]
         copy = pltpu.make_async_copy(flat, out, sent)
         copy.start()
-        lane = lax.broadcasted_iota(jnp.int32, (1, count), 1)
-        sums = [jnp.zeros((1, count), F32)] * 2
-        norm = 1.0 / math.sqrt(plan.grid)
-        e = total[0]
-        f = total[1]
-        for index in range(count):
-            if index < 2:
-                band = (own, pair)[index]
-                c, d = band[0], band[1]
-            else:
-                to_matrix(plan, bands[index - 2][...], tiles, matrix)
-                c, d = matrix[0], matrix[1]
-            parts = (c * e + d * f, c * f - d * e)
+        here = place[0]
+
+        @pl.when(here >= 0)
+        def _():
+            lane = lax.broadcasted_iota(jnp.int32, (1, count), 1)
+            where = [here, here ^ 1]
+            for step in range(1, count // 2):
+                for start in (here, here ^ 1):
+                    source = start - 2 * step
+                    where.append(jnp.where(source < 0, source + count, source))
+            sums = [jnp.zeros((1, count), F32)] * 2
+            norm = 1.0 / math.sqrt(plan.grid)
+            e = total[0]
+            f = total[1]
+            for index in range(count):
+                if index < 2:
+                    band = (own, pair)[index]
+                    c, d = band[0], band[1]
+                else:
+                    to_matrix(plan, bands[index - 2][...], tiles, matrix)
+                    c, d = matrix[0], matrix[1]
+                parts = (c * e + d * f, c * f - d * e)
+                for part in range(2):
+                    value = jnp.sum(jnp.sum(parts[part], axis=0, keepdims=True), axis=1, keepdims=True)
+                    sums[part] = jnp.where(lane == where[index], value * norm, sums[part])
             for part in range(2):
-                value = jnp.sum(jnp.sum(parts[part], axis=0, keepdims=True), axis=1, keepdims=True)
-                sums[part] = jnp.where(lane == place[index], value * norm, sums[part])
-        for part in range(2):
-            gram[part] = sums[part]
+                gram[part] = sums[part]
+
         copy.wait()
 
     return pl.pallas_call(
@@ -319,7 +340,7 @@
             jax.ShapeDtypeStruct((2, 1, count), F32),
         ],
         in_specs=[SMEM] + [VMEM] * (2 + others),
-        out_specs=[HBM, VMEM],
+        out_specs=[ANYWHERE, VMEM],
         scratch_shapes=[
             pltpu.VMEM((2 * plan.padded_tiles, LANES), F32),
             pltpu.VMEM((2, plan.kept, LANES), F32),
@@ -347,10 +368,7 @@
         return lax.ppermute(array, ("pool", "band"), pairs)
 
     here = lax.axis_index("band")
-    places = [here, here ^ 1]
-    for step in range(1, groups // 2):
-        places += [(here - 2 * step) % groups, ((here ^ 1) - 2 * step) % groups]
-    place = jnp.stack(places).astype(jnp.int32)
+    place = lax.broadcast(here.astype(jnp.int32), (1,))
     own = pack(plan)(orbitals[0, 0], occupation[0])
     near = move(own, lambda p, g: ((p + 1) % pools, g))
     far = move(own, lambda p, g: ((p + 1) % pools, (g + 1) % groups) if g % 2 else (p, g + 1))
@@ -358,14 +376,15 @@
     bands = [move(own, partner)]
     for step in range(1, groups // 2):
         shifted = move(own, lambda p, g: (p, (g + 2 * step) % groups))
-        bands += [shifted, move(shifted, partner)]
+        crossed = move(shifted, partner)
+        bands += [shifted, crossed]
     swapped = move(near, partner)
-    padded = jnp.pad(kernel, (0, plan.padded_tiles * LANES - plan.grid))
-    mine, factor, left, right, twiddle = prepare(plan)(
-        own, padded.reshape(-1, LANES), *constants(plan)
-    )
-    accum, pair = first_pair(plan)(mine, near, factor, left, right, twiddle, bands[0])
-    total = second_pair(plan)(place, mine, accum, far, swapped, factor, left, right, twiddle)
+    tables = constants(plan)
+    mine, factor = prepare(plan)(own, kernel, *tables)
+    accum, pair = first_pair(plan)(mine, near, factor, *tables, bands[0])
+    total = second_pair(plan)(
+        place, mine, accum, far, swapped, factor, *tables
+    )
     exchanged, gram = finish(plan, others)(place, total, mine, pair, *bands[1:])
     return exchanged[None, None], jnp.swapaxes(gram, 1, 2)[None]
 

time: 25.3 us -> 23.3 us (0.921)
  Pallas kernels: 7.81 us -> 5.06 us
  local copies, waits for them, and re-layouts: 3.82 us -> 4.63 us
    unnamed x8 -> x14, local copies, waits for them, and re-layouts: 2.89 us -> 4.63 us
    pallas_call x3, Pallas kernels: 4.86 us -> 3.21 us  [the longest x1 1.32 us: shards(): total = second_pair(plan)(place, mine, accum, far, swapped, factor, *tables)]
    pallas_call x1, Pallas kernels: 2.71 us -> 1.61 us  [shards(): exchanged, gram = finish(plan, others)(place, total, mine, pair, *bands[1:])]
    reshape x1 -> x0, local copies, waits for them, and re-layouts: 0.94 us -> none  [shards(): padded.reshape(-1, LANES)]
  transfers between devices with their start and end apart: 6 -> 6, of which waited for: 1 -> 1; matrix products, arithmetic and copies ran while one was open for 4% -> 0% of each run, Pallas kernels for 19% -> 14%
where the time goes in v3:
time: 23.3 us; the launch traced here: 23 us
  waiting for transfers between devices  6.38 us (27%)
  starting transfers between devices  5.56 us (24%)
  Pallas kernels  5.06 us (22%)
  local copies, waits for them, and re-layouts  4.63 us (20%)
  between operations  1.4 us (6%)
    ppermute x6, waiting for transfers between devices, move(): return lax.ppermute(array, ('pool', 'band'), pairs)  6.38 us
    ppermute x6, starting transfers between devices, move(): return lax.ppermute(array, ('pool', 'band'), pairs)  5.56 us
    unnamed x14, local copies, waits for them, and re-layouts  4.63 us
    pallas_call x1, Pallas kernels, shards(): exchanged, gram = finish(plan, others)(place, total, mine, pair, *bands[1:])  1.61 us
    pallas_call x1, Pallas kernels, shards(): total = second_pair(plan)(place, mine, accum, far, swapped, factor, *tables)  1.32 us
    pallas_call x1, Pallas kernels, shards(): accum, pair = first_pair(plan)(mine, near, factor, *tables, bands[0])  1.27 us
    pallas_call x1, Pallas kernels, shards(): mine, factor = prepare(plan)(own, kernel, *tables)  0.61 us
  transfers between devices with their start and end apart: 6, of which 1 were waited for; matrix products, arithmetic and copies ran while one was open for 0% of the time, Pallas kernels for 14%

profile of v3, /device:TPU:0, one launch (start us, length us, event | category | flops | bytes accessed | tf_op | source)
XLA Modules:
  0.0 23.0 jit_solution(3424375511900700736)
XLA Ops:
  0.6 0.0 copy-start.4
  1.3 0.0 copy-start.6
  1.3 0.9 %copy-done.6 = bf16[1,1,2,46656]{3,2,1,0:T(2,128)(2,1)S(1)} copy-done((bf16[1,1,2,46656]{3,2,1,0:T(2,128)(2,1)S(1)}, bf16[1,1,2,46656]{3,2,1,0:T(2,128)(2,1)}, u32[]{:S(2)}) %copy-start.6) | copy-done | bytes 186648
  2.3 0.2 %pack.1.own_in = bf16[730,128]{1,0:T(8,128)(2,1)S(1)} custom-call(bf16[2,46656]{1,0:T(2,128)(2,1)S(1)} %bitcast.8, s32[1]{0:T(128)} %bitcast.7.occupation), custom_call_target="tpu_custom_call" | custom-call | tf_op jit(solution)/shard_map/pack/pallas_call | solution.py:372
  2.5 3.0 %collective-permute-start = (bf16[730,128]{1,0:T(8,128)(2,1)S(1)}, bf16[730,128]{1,0:T(8,128)(2,1)S(1)}, u32[]{:S(2)}, u32[]{:S(2)}) collective-permute-start(bf16[730,128]{1,0:T(8,128)(2,1)S(1)} %pack.1.own_in), channel_id=1, source_target_pairs={{0,4},{1,5},{2,6},{3,7},{4,8},{5,9},{6,10},{7,11},{8,12},{9,13},{1... | collective-permute-start | bytes 560648 | tf_op jit(solution)/shard_map/ppermute | solution.py:368
  5.5 1.5 %collective-permute-start.4 = (bf16[730,128]{1,0:T(8,128)(2,1)S(1)}, bf16[730,128]{1,0:T(8,128)(2,1)S(1)}, u32[]{:S(2)}, u32[]{:S(2)}) collective-permute-start(bf16[730,128]{1,0:T(8,128)(2,1)S(1)} %pack.1.own_in), channel_id=1, source_target_pairs={{0,2},{1,3},{2,0},{3,1},{4,6},{5,7},{6,4},{7,5},{8,10},{9,11},{10,... | collective-permute-start | bytes 560648 | tf_op jit(solution)/shard_map/ppermute | solution.py:368
  7.0 0.0 collective-permute-start.1
  7.0 0.5 %collective-permute-start.2 = (bf16[730,128]{1,0:T(8,128)(2,1)S(1)}, bf16[730,128]{1,0:T(8,128)(2,1)S(1)}, u32[]{:S(2)}, u32[]{:S(2)}) collective-permute-start(bf16[730,128]{1,0:T(8,128)(2,1)S(1)} %pack.1.own_in), channel_id=1, source_target_pairs={{0,1},{1,6},{2,3},{3,4},{4,5},{5,10},{6,7},{7,8},{8,9},{9,14},{10,... | collective-permute-start | bytes 560648 | tf_op jit(solution)/shard_map/ppermute | solution.py:368
  7.6 6.4 %collective-permute-done.near_in = bf16[730,128]{1,0:T(8,128)(2,1)S(1)} collective-permute-done((bf16[730,128]{1,0:T(8,128)(2,1)S(1)}, bf16[730,128]{1,0:T(8,128)(2,1)S(1)}, u32[]{:S(2)}, u32[]{:S(2)}) %collective-permute-start) | collective-permute-done | bytes 186912 | tf_op jit(solution)/shard_map/ppermute | solution.py:368
  13.9 0.0 collective-permute-start.3
  13.9 0.0 collective-permute-done.4.refs_4_
  13.9 0.5 %collective-permute-start.5 = (bf16[730,128]{1,0:T(8,128)(2,1)S(1)}, bf16[730,128]{1,0:T(8,128)(2,1)S(1)}, u32[]{:S(2)}, u32[]{:S(2)}) collective-permute-start(bf16[730,128]{1,0:T(8,128)(2,1)S(1)} %collective-permute-done.4.refs_4_), channel_id=1, source_target_pairs={{0,1},{1,0},{2,3},{3,2},{4,5},{5,4},{6,7},{7,6},{8,9},{9,8},{10,11... | collective-permute-start | bytes 560648 | tf_op jit(solution)/shard_map/ppermute | solution.py:368
  14.4 0.0 copy-done.4
  14.4 0.0 copy-start
  14.4 1.1 %copy-done = bf16[448,896]{1,0:T(8,128)(2,1)S(1)} copy-done((bf16[448,896]{1,0:T(8,128)(2,1)S(1)}, bf16[448,896]{1,0:T(8,128)(2,1)}, u32[]{:S(2)}) %copy-start) | copy-done | bytes 802840
  15.6 0.0 copy-start.2
  15.6 1.0 %copy-done.2 = f32[2,448,128]{2,1,0:T(8,128)S(1)} copy-done((f32[2,448,128]{2,1,0:T(8,128)S(1)}, f32[2,448,128]{2,1,0:T(8,128)}, u32[]{:S(2)}) %copy-start.2) | copy-done | bytes 458776
  16.6 0.0 copy-start.5
  16.6 0.9 %copy-done.5 = f32[46656]{0:T(1024)S(1)} copy-done((f32[46656]{0:T(1024)S(1)}, f32[46656]{0:T(1024)}, u32[]{:S(2)}) %copy-start.5) | copy-done | bytes 186648
  17.5 0.0 copy-start.1
  17.5 0.0 copy-start.3
  17.5 0.6 %prepare.1 = (f32[2,448,128]{2,1,0:T(8,128)S(1)}, f32[448,128]{1,0:T(8,128)S(1)}) custom-call(bf16[730,128]{1,0:T(8,128)(2,1)S(1)} %pack.1.own_in, f32[46656]{0:T(1024)S(1)} %copy-done.5, bf16[448,896]{1,0:T(8,128)(2,1)S(1)} %copy-done, bf16[2,256,256]{2,1,0:T(8,128)(2,1)S(1)} %copy-done.4, f32[2,448,128]{2,1,0:T(8,128)S(1)} %copy-done.2), custom_call_target="tpu_custom_call" | custom-call | tf_op jit(solution)/shard_map/prepare/pallas_call | solution.py:383
  18.1 0.0 collective-permute-done.1.pair_in
  18.2 0.5 %copy-done.1 = bf16[448,896]{1,0:T(8,128)(2,1)S(1)} copy-done((bf16[448,896]{1,0:T(8,128)(2,1)S(1)}, bf16[448,896]{1,0:T(8,128)(2,1)}, u32[]{:S(2)}) %copy-start.1) | copy-done | bytes 802840
  18.7 0.1 copy-done.3
  18.8 1.3 %first_pair.1 = (f32[2,448,128]{2,1,0:T(8,128)S(1)}, f32[2,448,128]{2,1,0:T(8,128)S(1)}) custom-call(f32[2,448,128]{2,1,0:T(8,128)S(1)} %get-tuple-element.8.own.refs_2_, bf16[730,128]{1,0:T(8,128)(2,1)S(1)} %collective-permute-done.near_in, f32[448,128]{1,0:T(8,128)S(1)} %get-tuple-element.9.kernel, bf16[448,896]{1,0:T(8,128)(2,1)S(1)} %copy-done.1, ...), custom_call_target="tpu_custom_call" | custom-call | tf_op jit(solution)/shard_map/first_pair/pallas_call | solution.py:384
  20.1 0.0 collective-permute-done.2.far_in
  20.1 0.0 collective-permute-done.3.near_in
  20.1 1.3 %second_pair.1.refs_1_ = f32[2,448,128]{2,1,0:T(8,128)S(1)} custom-call(s32[1]{0:T(128)} %bitcast.place.refs_0_, f32[2,448,128]{2,1,0:T(8,128)S(1)} %get-tuple-element.8.own.refs_2_, f32[2,448,128]{2,1,0:T(8,128)S(1)} %get-tuple-element.10.accum, bf16[730,128]{1,0:T(8,128)(2,1)S(1)} %collective-permute-done.2.far_in, ...), custom_call_target="tpu_custom_call", output_to_operand_aliasing={{}: (2, {})} | custom-call | tf_op jit(solution)/shard_map/second_pair/pallas_call | solution.py:385
  21.4 0.0 collective-permute-done.5.refs_5_
  21.4 1.6 %finish.1 = (bf16[2,46656]{1,0:T(2,128)(2,1)}, f32[2,1,4]{2,1,0:T(1,128)}) custom-call(s32[1]{0:T(128)} %bitcast.place.refs_0_, f32[2,448,128]{2,1,0:T(8,128)S(1)} %second_pair.1.refs_1_, f32[2,448,128]{2,1,0:T(8,128)S(1)} %get-tuple-element.8.own.refs_2_, f32[2,448,128]{2,1,0:T(8,128)S(1)} %get-tuple-element.11.refs_3_, ...), custom_call_target="tpu_custom_call" | custom-call | tf_op jit(solution)/shard_map/finish/pallas_call | solution.py:388
Async XLA Ops:
  0.6 13.8 %copy-start.4 = (bf16[2,256,256]{2,1,0:T(8,128)(2,1)S(1)}, bf16[2,256,256]{2,1,0:T(8,128)(2,1)}, u32[]{:S(2)}) copy-start(bf16[2,256,256]{2,1,0:T(8,128)(2,1)} %constant.11.clone.right) | copy-start | bytes 786436
  1.3 0.9 %copy-start.6 = (bf16[1,1,2,46656]{3,2,1,0:T(2,128)(2,1)S(1)}, bf16[1,1,2,46656]{3,2,1,0:T(2,128)(2,1)}, u32[]{:S(2)}) copy-start(bf16[1,1,2,46656]{3,2,1,0:T(2,128)(2,1)} %param.6) | copy-start | bytes 559876
  2.5 11.4 %collective-permute-start = (bf16[730,128]{1,0:T(8,128)(2,1)S(1)}, bf16[730,128]{1,0:T(8,128)(2,1)S(1)}, u32[]{:S(2)}, u32[]{:S(2)}) collective-permute-start(bf16[730,128]{1,0:T(8,128)(2,1)S(1)} %pack.1.own_in), channel_id=1, source_target_pairs={{0,4},{1,5},{2,6},{3,7},{4,8},{5,9},{6,10},{7,11},{8,12},{9,13},{1... | collective-permute-start | bytes 560648 | tf_op jit(solution)/shard_map/ppermute | solution.py:368
  5.5 8.4 %collective-permute-start.4 = (bf16[730,128]{1,0:T(8,128)(2,1)S(1)}, bf16[730,128]{1,0:T(8,128)(2,1)S(1)}, u32[]{:S(2)}, u32[]{:S(2)}) collective-permute-start(bf16[730,128]{1,0:T(8,128)(2,1)S(1)} %pack.1.own_in), channel_id=1, source_target_pairs={{0,2},{1,3},{2,0},{3,1},{4,6},{5,7},{6,4},{7,5},{8,10},{9,11},{10,... | collective-permute-start | bytes 560648 | tf_op jit(solution)/shard_map/ppermute | solution.py:368
  7.0 11.1 %collective-permute-start.1 = (bf16[730,128]{1,0:T(8,128)(2,1)S(1)}, bf16[730,128]{1,0:T(8,128)(2,1)S(1)}, u32[]{:S(2)}, u32[]{:S(2)}) collective-permute-start(bf16[730,128]{1,0:T(8,128)(2,1)S(1)} %pack.1.own_in), channel_id=1, source_target_pairs={{0,1},{1,0},{2,3},{3,2},{4,5},{5,4},{6,7},{7,6},{8,9},{9,8},{10,11... | collective-permute-start | bytes 560648 | tf_op jit(solution)/shard_map/ppermute | solution.py:368
  7.0 13.0 %collective-permute-start.2 = (bf16[730,128]{1,0:T(8,128)(2,1)S(1)}, bf16[730,128]{1,0:T(8,128)(2,1)S(1)}, u32[]{:S(2)}, u32[]{:S(2)}) collective-permute-start(bf16[730,128]{1,0:T(8,128)(2,1)S(1)} %pack.1.own_in), channel_id=1, source_target_pairs={{0,1},{1,6},{2,3},{3,4},{4,5},{5,10},{6,7},{7,8},{8,9},{9,14},{10,... | collective-permute-start | bytes 560648 | tf_op jit(solution)/shard_map/ppermute | solution.py:368
  13.9 6.2 %collective-permute-start.3 = (bf16[730,128]{1,0:T(8,128)(2,1)S(1)}, bf16[730,128]{1,0:T(8,128)(2,1)S(1)}, u32[]{:S(2)}, u32[]{:S(2)}) collective-permute-start(bf16[730,128]{1,0:T(8,128)(2,1)S(1)} %collective-permute-done.near_in), channel_id=1, source_target_pairs={{0,1},{1,0},{2,3},{3,2},{4,5},{5,4},{6,7},{7,6},{8,9},{9,8},{10,11... | collective-permute-start | bytes 560648 | tf_op jit(solution)/shard_map/ppermute | solution.py:368
  13.9 7.5 %collective-permute-start.5 = (bf16[730,128]{1,0:T(8,128)(2,1)S(1)}, bf16[730,128]{1,0:T(8,128)(2,1)S(1)}, u32[]{:S(2)}, u32[]{:S(2)}) collective-permute-start(bf16[730,128]{1,0:T(8,128)(2,1)S(1)} %collective-permute-done.4.refs_4_), channel_id=1, source_target_pairs={{0,1},{1,0},{2,3},{3,2},{4,5},{5,4},{6,7},{7,6},{8,9},{9,8},{10,11... | collective-permute-start | bytes 560648 | tf_op jit(solution)/shard_map/ppermute | solution.py:368
  14.4 1.1 %copy-start = (bf16[448,896]{1,0:T(8,128)(2,1)S(1)}, bf16[448,896]{1,0:T(8,128)(2,1)}, u32[]{:S(2)}) copy-start(bf16[448,896]{1,0:T(8,128)(2,1)} %constant.10.clone.left) | copy-start | bytes 2408452
  15.6 1.0 %copy-start.2 = (f32[2,448,128]{2,1,0:T(8,128)S(1)}, f32[2,448,128]{2,1,0:T(8,128)}, u32[]{:S(2)}) copy-start(f32[2,448,128]{2,1,0:T(8,128)} %constant.12.clone.twiddle) | copy-start | bytes 1376260
  16.6 0.9 %copy-start.5 = (f32[46656]{0:T(1024)S(1)}, f32[46656]{0:T(1024)}, u32[]{:S(2)}) copy-start(f32[46656]{0:T(1024)} %kernel_in.1) | copy-start | bytes 559876
  17.5 1.1 %copy-start.1 = (bf16[448,896]{1,0:T(8,128)(2,1)S(1)}, bf16[448,896]{1,0:T(8,128)(2,1)}, u32[]{:S(2)}) copy-start(bf16[448,896]{1,0:T(8,128)(2,1)} %constant.10.clone.left) | copy-start | bytes 2408452
  17.5 1.3 %copy-start.3 = (f32[2,448,128]{2,1,0:T(8,128)S(1)}, f32[2,448,128]{2,1,0:T(8,128)}, u32[]{:S(2)}) copy-start(f32[2,448,128]{2,1,0:T(8,128)} %constant.12.clone.twiddle) | copy-start | bytes 1376260

commit v4 on v3

--- a/solution.py
+++ b/solution.py
@@ -268,8 +268,8 @@
 
 
 def second_pair(plan):
-    def body(place, own, accum, far_in, near_in, kernel, left, right, twiddle, total, tiles, near, fourier):
-        packed = jnp.where(place[0] % 2 == 1, near_in[...], far_in[...])
+    def body(own, accum, far_in, near_in, kernel, left, right, twiddle, total, tiles, near, fourier):
+        packed = jnp.where(lax.axis_index("band") % 2 == 1, near_in[...], far_in[...])
         results = exchange(plan, own, packed, tiles, near, fourier, kernel, left, right, twiddle)
         for part, real, imag in results:
             total[0, part, :] = (accum[0, part, :] + real).astype(BF16).astype(F32)
@@ -278,9 +278,9 @@
     return pl.pallas_call(
         body,
         out_shape=jax.ShapeDtypeStruct((2, plan.kept, LANES), F32),
-        in_specs=[SMEM] + [VMEM] * 8,
+        in_specs=[VMEM] * 8,
         out_specs=VMEM,
-        input_output_aliases={2: 0},
+        input_output_aliases={1: 0},
         scratch_shapes=scratch_of(plan),
         compiler_params=pltpu.CompilerParams(vmem_limit_bytes=16 * 1024 * 1024),
         name="second_pair",
@@ -291,9 +291,9 @@
     count = others + 1
 
     def body(*refs):
-        place, total, own, pair = refs[:4]
-        bands = refs[4 : 3 + others]
-        out, gram, tiles, matrix, flat, sent = refs[3 + others :]
+        total, own, pair = refs[:3]
+        bands = refs[3 : 2 + others]
+        out, gram, tiles, matrix, flat, sent = refs[2 + others :]
         from_matrix(plan, total, tiles)
         for q in range(plan.tiles):
             turn, i = divmod(q, plan.tile_period)
@@ -303,7 +303,7 @@
                 flat[:, LANES * q : LANES * q + used] = pair_rows[:, :used]
         copy = pltpu.make_async_copy(flat, out, sent)
         copy.start()
-        here = place[0]
+        here = lax.axis_index("band")
 
         @pl.when(here >= 0)
         def _():
@@ -339,7 +339,7 @@
             jax.ShapeDtypeStruct((2, plan.grid), BF16),
             jax.ShapeDtypeStruct((2, 1, count), F32),
         ],
-        in_specs=[SMEM] + [VMEM] * (2 + others),
+        in_specs=[VMEM] * (2 + others),
         out_specs=[ANYWHERE, VMEM],
         scratch_shapes=[
             pltpu.VMEM((2 * plan.padded_tiles, LANES), F32),
@@ -367,8 +367,6 @@
         ]
         return lax.ppermute(array, ("pool", "band"), pairs)
 
-    here = lax.axis_index("band")
-    place = lax.broadcast(here.astype(jnp.int32), (1,))
     own = pack(plan)(orbitals[0, 0], occupation[0])
     near = move(own, lambda p, g: ((p + 1) % pools, g))
     far = move(own, lambda p, g: ((p + 1) % pools, (g + 1) % groups) if g % 2 else (p, g + 1))
@@ -383,9 +381,9 @@
     mine, factor = prepare(plan)(own, kernel, *tables)
     accum, pair = first_pair(plan)(mine, near, factor, *tables, bands[0])
     total = second_pair(plan)(
-        place, mine, accum, far, swapped, factor, *tables
-    )
-    exchanged, gram = finish(plan, others)(place, total, mine, pair, *bands[1:])
+        mine, accum, far, swapped, factor, *tables
+    )
+    exchanged, gram = finish(plan, others)(total, mine, pair, *bands[1:])
     return exchanged[None, None], jnp.swapaxes(gram, 1, 2)[None]
 
 

time: 23.3 us -> 23.3 us (level)
  no operation moved by 1% of the time
where the time goes in v4:
time: 23.3 us; the launch traced here: 23 us
  waiting for transfers between devices  6.38 us (27%)
  starting transfers between devices  5.56 us (24%)
  Pallas kernels  5.06 us (22%)
  local copies, waits for them, and re-layouts  4.63 us (20%)
  between operations  1.4 us (6%)
    ppermute x6, waiting for transfers between devices, move(): return lax.ppermute(array, ('pool', 'band'), pairs)  6.38 us
    ppermute x6, starting transfers between devices, move(): return lax.ppermute(array, ('pool', 'band'), pairs)  5.56 us
    unnamed x14, local copies, waits for them, and re-layouts  4.63 us
    pallas_call x1, Pallas kernels, shards(): exchanged, gram = finish(plan, others)(total, mine, pair, *bands[1:])  1.61 us
    pallas_call x1, Pallas kernels, shards(): total = second_pair(plan)(mine, accum, far, swapped, factor, *tables)  1.33 us
    pallas_call x1, Pallas kernels, shards(): accum, pair = first_pair(plan)(mine, near, factor, *tables, bands[0])  1.27 us
    pallas_call x1, Pallas kernels, shards(): mine, factor = prepare(plan)(own, kernel, *tables)  0.61 us
  transfers between devices with their start and end apart: 6, of which 1 were waited for; matrix products, arithmetic and copies ran while one was open for 0% of the time, Pallas kernels for 14%

profile of v4, /device:TPU:0, one launch (start us, length us, event | category | flops | bytes accessed | tf_op | source)
XLA Modules:
  0.0 23.0 jit_solution(14217315735288048504)
XLA Ops:
  0.6 0.0 copy-start.4
  1.3 0.0 copy-start.6
  1.3 0.9 %copy-done.6 = bf16[1,1,2,46656]{3,2,1,0:T(2,128)(2,1)S(1)} copy-done((bf16[1,1,2,46656]{3,2,1,0:T(2,128)(2,1)S(1)}, bf16[1,1,2,46656]{3,2,1,0:T(2,128)(2,1)}, u32[]{:S(2)}) %copy-start.6) | copy-done | bytes 186648
  2.3 0.2 %pack.1.own_in = bf16[730,128]{1,0:T(8,128)(2,1)S(1)} custom-call(bf16[2,46656]{1,0:T(2,128)(2,1)S(1)} %bitcast.7, s32[1]{0:T(128)} %bitcast.6.occupation), custom_call_target="tpu_custom_call" | custom-call | tf_op jit(solution)/shard_map/pack/pallas_call | solution.py:370
  2.5 3.0 %collective-permute-start = (bf16[730,128]{1,0:T(8,128)(2,1)S(1)}, bf16[730,128]{1,0:T(8,128)(2,1)S(1)}, u32[]{:S(2)}, u32[]{:S(2)}) collective-permute-start(bf16[730,128]{1,0:T(8,128)(2,1)S(1)} %pack.1.own_in), channel_id=1, source_target_pairs={{0,4},{1,5},{2,6},{3,7},{4,8},{5,9},{6,10},{7,11},{8,12},{9,13},{1... | collective-permute-start | bytes 560648 | tf_op jit(solution)/shard_map/ppermute | solution.py:368
  5.5 1.5 %collective-permute-start.4 = (bf16[730,128]{1,0:T(8,128)(2,1)S(1)}, bf16[730,128]{1,0:T(8,128)(2,1)S(1)}, u32[]{:S(2)}, u32[]{:S(2)}) collective-permute-start(bf16[730,128]{1,0:T(8,128)(2,1)S(1)} %pack.1.own_in), channel_id=1, source_target_pairs={{0,2},{1,3},{2,0},{3,1},{4,6},{5,7},{6,4},{7,5},{8,10},{9,11},{10,... | collective-permute-start | bytes 560648 | tf_op jit(solution)/shard_map/ppermute | solution.py:368
  7.0 0.0 collective-permute-start.1
  7.0 0.5 %collective-permute-start.2 = (bf16[730,128]{1,0:T(8,128)(2,1)S(1)}, bf16[730,128]{1,0:T(8,128)(2,1)S(1)}, u32[]{:S(2)}, u32[]{:S(2)}) collective-permute-start(bf16[730,128]{1,0:T(8,128)(2,1)S(1)} %pack.1.own_in), channel_id=1, source_target_pairs={{0,1},{1,6},{2,3},{3,4},{4,5},{5,10},{6,7},{7,8},{8,9},{9,14},{10,... | collective-permute-start | bytes 560648 | tf_op jit(solution)/shard_map/ppermute | solution.py:368
  7.6 6.4 %collective-permute-done.near_in = bf16[730,128]{1,0:T(8,128)(2,1)S(1)} collective-permute-done((bf16[730,128]{1,0:T(8,128)(2,1)S(1)}, bf16[730,128]{1,0:T(8,128)(2,1)S(1)}, u32[]{:S(2)}, u32[]{:S(2)}) %collective-permute-start) | collective-permute-done | bytes 186912 | tf_op jit(solution)/shard_map/ppermute | solution.py:368
  13.9 0.0 collective-permute-start.3
  13.9 0.0 collective-permute-done.4.refs_3_
  13.9 0.5 %collective-permute-start.5 = (bf16[730,128]{1,0:T(8,128)(2,1)S(1)}, bf16[730,128]{1,0:T(8,128)(2,1)S(1)}, u32[]{:S(2)}, u32[]{:S(2)}) collective-permute-start(bf16[730,128]{1,0:T(8,128)(2,1)S(1)} %collective-permute-done.4.refs_3_), channel_id=1, source_target_pairs={{0,1},{1,0},{2,3},{3,2},{4,5},{5,4},{6,7},{7,6},{8,9},{9,8},{10,11... | collective-permute-start | bytes 560648 | tf_op jit(solution)/shard_map/ppermute | solution.py:368
  14.4 0.0 copy-done.4
  14.4 0.0 copy-start
  14.4 1.1 %copy-done = bf16[448,896]{1,0:T(8,128)(2,1)S(1)} copy-done((bf16[448,896]{1,0:T(8,128)(2,1)S(1)}, bf16[448,896]{1,0:T(8,128)(2,1)}, u32[]{:S(2)}) %copy-start) | copy-done | bytes 802840
  15.6 0.0 copy-start.2
  15.6 1.0 %copy-done.2 = f32[2,448,128]{2,1,0:T(8,128)S(1)} copy-done((f32[2,448,128]{2,1,0:T(8,128)S(1)}, f32[2,448,128]{2,1,0:T(8,128)}, u32[]{:S(2)}) %copy-start.2) | copy-done | bytes 458776
  16.6 0.0 copy-start.5
  16.6 0.9 %copy-done.5 = f32[46656]{0:T(1024)S(1)} copy-done((f32[46656]{0:T(1024)S(1)}, f32[46656]{0:T(1024)}, u32[]{:S(2)}) %copy-start.5) | copy-done | bytes 186648
  17.5 0.0 copy-start.1
  17.5 0.0 copy-start.3
  17.5 0.6 %prepare.1 = (f32[2,448,128]{2,1,0:T(8,128)S(1)}, f32[448,128]{1,0:T(8,128)S(1)}) custom-call(bf16[730,128]{1,0:T(8,128)(2,1)S(1)} %pack.1.own_in, f32[46656]{0:T(1024)S(1)} %copy-done.5, bf16[448,896]{1,0:T(8,128)(2,1)S(1)} %copy-done, bf16[2,256,256]{2,1,0:T(8,128)(2,1)S(1)} %copy-done.4, f32[2,448,128]{2,1,0:T(8,128)S(1)} %copy-done.2), custom_call_target="tpu_custom_call" | custom-call | tf_op jit(solution)/shard_map/prepare/pallas_call | solution.py:381
  18.1 0.0 collective-permute-done.1.pair_in
  18.2 0.5 %copy-done.1 = bf16[448,896]{1,0:T(8,128)(2,1)S(1)} copy-done((bf16[448,896]{1,0:T(8,128)(2,1)S(1)}, bf16[448,896]{1,0:T(8,128)(2,1)}, u32[]{:S(2)}) %copy-start.1) | copy-done | bytes 802840
  18.7 0.1 copy-done.3
  18.8 1.3 %first_pair.1 = (f32[2,448,128]{2,1,0:T(8,128)S(1)}, f32[2,448,128]{2,1,0:T(8,128)S(1)}) custom-call(f32[2,448,128]{2,1,0:T(8,128)S(1)} %get-tuple-element.8.own.refs_1_, bf16[730,128]{1,0:T(8,128)(2,1)S(1)} %collective-permute-done.near_in, f32[448,128]{1,0:T(8,128)S(1)} %get-tuple-element.9.kernel, bf16[448,896]{1,0:T(8,128)(2,1)S(1)} %copy-done.1, ...), custom_call_target="tpu_custom_call" | custom-call | tf_op jit(solution)/shard_map/first_pair/pallas_call | solution.py:382
  20.1 0.0 collective-permute-done.2.far_in
  20.1 0.0 collective-permute-done.3.near_in
  20.1 1.3 %second_pair.1.refs_0_ = f32[2,448,128]{2,1,0:T(8,128)S(1)} custom-call(f32[2,448,128]{2,1,0:T(8,128)S(1)} %get-tuple-element.8.own.refs_1_, f32[2,448,128]{2,1,0:T(8,128)S(1)} %get-tuple-element.10.accum, bf16[730,128]{1,0:T(8,128)(2,1)S(1)} %collective-permute-done.2.far_in, ...), custom_call_target="tpu_custom_call", output_to_operand_aliasing={{}: (1, {})} | custom-call | tf_op jit(solution)/shard_map/second_pair/pallas_call | solution.py:383
  21.4 0.0 collective-permute-done.5.refs_4_
  21.4 1.6 %finish.1 = (bf16[2,46656]{1,0:T(2,128)(2,1)}, f32[2,1,4]{2,1,0:T(1,128)}) custom-call(f32[2,448,128]{2,1,0:T(8,128)S(1)} %second_pair.1.refs_0_, f32[2,448,128]{2,1,0:T(8,128)S(1)} %get-tuple-element.8.own.refs_1_, f32[2,448,128]{2,1,0:T(8,128)S(1)} %get-tuple-element.11.refs_2_, bf16[730,128]{1,0:T(8,128)(2,1)S(1)} %collective-permute-done.4.refs_3_, ...), custom_call_target="tpu_custom_call" | custom-call | tf_op jit(solution)/shard_map/finish/pallas_call | solution.py:386
Async XLA Ops:
  0.6 13.8 %copy-start.4 = (bf16[2,256,256]{2,1,0:T(8,128)(2,1)S(1)}, bf16[2,256,256]{2,1,0:T(8,128)(2,1)}, u32[]{:S(2)}) copy-start(bf16[2,256,256]{2,1,0:T(8,128)(2,1)} %constant.7.clone.right) | copy-start | bytes 786436
  1.3 0.9 %copy-start.6 = (bf16[1,1,2,46656]{3,2,1,0:T(2,128)(2,1)S(1)}, bf16[1,1,2,46656]{3,2,1,0:T(2,128)(2,1)}, u32[]{:S(2)}) copy-start(bf16[1,1,2,46656]{3,2,1,0:T(2,128)(2,1)} %param.6) | copy-start | bytes 559876
  2.5 11.4 %collective-permute-start = (bf16[730,128]{1,0:T(8,128)(2,1)S(1)}, bf16[730,128]{1,0:T(8,128)(2,1)S(1)}, u32[]{:S(2)}, u32[]{:S(2)}) collective-permute-start(bf16[730,128]{1,0:T(8,128)(2,1)S(1)} %pack.1.own_in), channel_id=1, source_target_pairs={{0,4},{1,5},{2,6},{3,7},{4,8},{5,9},{6,10},{7,11},{8,12},{9,13},{1... | collective-permute-start | bytes 560648 | tf_op jit(solution)/shard_map/ppermute | solution.py:368
  5.5 8.4 %collective-permute-start.4 = (bf16[730,128]{1,0:T(8,128)(2,1)S(1)}, bf16[730,128]{1,0:T(8,128)(2,1)S(1)}, u32[]{:S(2)}, u32[]{:S(2)}) collective-permute-start(bf16[730,128]{1,0:T(8,128)(2,1)S(1)} %pack.1.own_in), channel_id=1, source_target_pairs={{0,2},{1,3},{2,0},{3,1},{4,6},{5,7},{6,4},{7,5},{8,10},{9,11},{10,... | collective-permute-start | bytes 560648 | tf_op jit(solution)/shard_map/ppermute | solution.py:368
  7.0 11.1 %collective-permute-start.1 = (bf16[730,128]{1,0:T(8,128)(2,1)S(1)}, bf16[730,128]{1,0:T(8,128)(2,1)S(1)}, u32[]{:S(2)}, u32[]{:S(2)}) collective-permute-start(bf16[730,128]{1,0:T(8,128)(2,1)S(1)} %pack.1.own_in), channel_id=1, source_target_pairs={{0,1},{1,0},{2,3},{3,2},{4,5},{5,4},{6,7},{7,6},{8,9},{9,8},{10,11... | collective-permute-start | bytes 560648 | tf_op jit(solution)/shard_map/ppermute | solution.py:368
  7.0 13.0 %collective-permute-start.2 = (bf16[730,128]{1,0:T(8,128)(2,1)S(1)}, bf16[730,128]{1,0:T(8,128)(2,1)S(1)}, u32[]{:S(2)}, u32[]{:S(2)}) collective-permute-start(bf16[730,128]{1,0:T(8,128)(2,1)S(1)} %pack.1.own_in), channel_id=1, source_target_pairs={{0,1},{1,6},{2,3},{3,4},{4,5},{5,10},{6,7},{7,8},{8,9},{9,14},{10,... | collective-permute-start | bytes 560648 | tf_op jit(solution)/shard_map/ppermute | solution.py:368
  13.9 6.2 %collective-permute-start.3 = (bf16[730,128]{1,0:T(8,128)(2,1)S(1)}, bf16[730,128]{1,0:T(8,128)(2,1)S(1)}, u32[]{:S(2)}, u32[]{:S(2)}) collective-permute-start(bf16[730,128]{1,0:T(8,128)(2,1)S(1)} %collective-permute-done.near_in), channel_id=1, source_target_pairs={{0,1},{1,0},{2,3},{3,2},{4,5},{5,4},{6,7},{7,6},{8,9},{9,8},{10,11... | collective-permute-start | bytes 560648 | tf_op jit(solution)/shard_map/ppermute | solution.py:368
  13.9 7.5 %collective-permute-start.5 = (bf16[730,128]{1,0:T(8,128)(2,1)S(1)}, bf16[730,128]{1,0:T(8,128)(2,1)S(1)}, u32[]{:S(2)}, u32[]{:S(2)}) collective-permute-start(bf16[730,128]{1,0:T(8,128)(2,1)S(1)} %collective-permute-done.4.refs_3_), channel_id=1, source_target_pairs={{0,1},{1,0},{2,3},{3,2},{4,5},{5,4},{6,7},{7,6},{8,9},{9,8},{10,11... | collective-permute-start | bytes 560648 | tf_op jit(solution)/shard_map/ppermute | solution.py:368
  14.4 1.1 %copy-start = (bf16[448,896]{1,0:T(8,128)(2,1)S(1)}, bf16[448,896]{1,0:T(8,128)(2,1)}, u32[]{:S(2)}) copy-start(bf16[448,896]{1,0:T(8,128)(2,1)} %constant.6.clone.left) | copy-start | bytes 2408452
  15.6 1.0 %copy-start.2 = (f32[2,448,128]{2,1,0:T(8,128)S(1)}, f32[2,448,128]{2,1,0:T(8,128)}, u32[]{:S(2)}) copy-start(f32[2,448,128]{2,1,0:T(8,128)} %constant.8.clone.twiddle) | copy-start | bytes 1376260
  16.6 0.9 %copy-start.5 = (f32[46656]{0:T(1024)S(1)}, f32[46656]{0:T(1024)}, u32[]{:S(2)}) copy-start(f32[46656]{0:T(1024)} %kernel_in.1) | copy-start | bytes 559876
  17.5 1.1 %copy-start.1 = (bf16[448,896]{1,0:T(8,128)(2,1)S(1)}, bf16[448,896]{1,0:T(8,128)(2,1)}, u32[]{:S(2)}) copy-start(bf16[448,896]{1,0:T(8,128)(2,1)} %constant.6.clone.left) | copy-start | bytes 2408452
  17.5 1.3 %copy-start.3 = (f32[2,448,128]{2,1,0:T(8,128)S(1)}, f32[2,448,128]{2,1,0:T(8,128)}, u32[]{:S(2)}) copy-start(f32[2,448,128]{2,1,0:T(8,128)} %constant.8.clone.twiddle) | copy-start | bytes 1376260

commit v5 on v4

v5 whole, which is shorter than its diff:
```python
import math

import jax
import jax.numpy as jnp
import numpy as np
from jax import lax
from jax.experimental import pallas as pl
from jax.experimental.pallas import tpu as pltpu
from jax.sharding import PartitionSpec as P


LANES = 128
F32 = jnp.float32
BF16 = jnp.bfloat16
VMEM = pl.BlockSpec(memory_space=pltpu.VMEM)
SMEM = pl.BlockSpec(memory_space=pltpu.SMEM)
ANYWHERE = pl.BlockSpec(memory_space=pl.ANY)


class Plan:
    def __init__(self, grid):
        ng = round(grid ** (1.0 / 3.0))
        self.grid = grid
        self.ng = ng
        self.split = max(b for b in range(1, ng + 1) if ng % b == 0 and b * ng <= LANES)
        self.coarse = ng // self.split
        self.width = self.split * ng
        self.rows = grid // self.width
        self.tiles = grid // LANES + 1
        self.tail = grid % LANES
        common = math.lcm(self.width, LANES)
        self.row_period = common // self.width
        self.tile_period = common // LANES
        self.blocks = -(-self.rows // self.row_period)
        self.half = self.rows // 2
        self.half_blocks = -(-self.half // self.row_period)
        self.half_kept = self.half_blocks * self.row_period
        self.kept = 2 * self.half_kept
        self.padded_tiles = (self.blocks * self.tile_period + 15) // 8 * 8


def roots(ng, phases):
    angles = 2.0 * np.pi / ng * (phases % ng)
    return np.cos(angles), np.sin(angles)


def constants(plan):
    ng, split, coarse, width = plan.ng, plan.split, plan.coarse, plan.width
    j, block = np.divmod(np.arange(plan.half_kept), plan.half_blocks)
    row = block * plan.row_period + j
    real_row = row < plan.half
    x, a = np.divmod(row, coarse)
    b, z = np.divmod(np.arange(width), ng)
    mask = np.outer(real_row, real_row)
    left = []
    for first, second in ((2 * x, x), (2 * x + 1, x), (x, 2 * x + 1)):
        cosine, sine = roots(ng, np.outer(first, second) + split * np.outer(a, a))
        left.append(np.concatenate([cosine * mask, sine * mask], axis=1))
    left = np.stack(left)
    cosine, sine = roots(ng, coarse * np.outer(b, b) + np.outer(z, z))
    right = np.zeros((2, 2, LANES, 2, LANES))
    for way, sign in enumerate((1.0, -1.0)):
        right[way, 0, :width, 0, :width] = cosine
        right[way, 1, :width, 1, :width] = cosine
        right[way, 1, :width, 0, :width] = sign * sine
        right[way, 0, :width, 1, :width] = -sign * sine
    twiddle = np.zeros((2, plan.half_kept, LANES))
    twiddle[0, :, :width], twiddle[1, :, :width] = roots(ng, np.outer(a, b))
    return (
        jnp.asarray(left, BF16),
        jnp.asarray(right.reshape(2, 2 * LANES, 2 * LANES), BF16),
        jnp.asarray(twiddle, F32),
    )


def pack(plan):
    def body(orbital, occupation, out):
        last = plan.tiles - 1
        for q in range(last):
            out[2 * q : 2 * q + 2, :] = orbital[:, LANES * q : LANES * (q + 1)]
        if plan.tail:
            out[2 * last :, : plan.tail] = orbital[:, LANES * last :]
        fill = jnp.full((2, LANES - plan.tail), occupation[0], jnp.int32)
        out[2 * last :, plan.tail :] = fill.astype(F32).astype(BF16)

    return pl.pallas_call(
        body,
        out_shape=jax.ShapeDtypeStruct((2 * plan.tiles, LANES), BF16),
        in_specs=[VMEM, SMEM],
        out_specs=VMEM,
        compiler_params=pltpu.CompilerParams(vmem_limit_bytes=4 * 1024 * 1024),
        name="pack",
    )


def shifted_rows(plan, tiles, first, step, row, count):
    q, shift = divmod(plan.width * row, LANES)
    stride = step * plan.tile_period
    rows = tiles[pl.ds(step * q + first, count, stride=stride), :]
    if shift + plan.width > LANES:
        after = tiles[pl.ds(step * (q + 1) + first, count, stride=stride), :]
        lane = lax.broadcasted_iota(jnp.int32, rows.shape, 1)
        rows = jnp.where(lane >= shift, rows, after)
    return pltpu.roll(rows, LANES - shift, axis=1) if shift else rows


def to_matrix(plan, packed, tiles, matrix):
    size = 2 * plan.tiles
    tiles[:size, :] = packed.astype(F32)
    tiles[size:, :] = jnp.zeros((2 * plan.padded_tiles - size, LANES), F32)
    count = plan.half_blocks
    for upper in range(2):
        for j in range(plan.row_period):
            first = plan.half_kept * upper + count * j
            for part in range(2):
                rows = shifted_rows(plan, tiles, part, 2, j + plan.half * upper, count)
                matrix[part, first : first + count, :] = rows


def join_halves(plan, matrix, whole):
    for upper in range(2):
        for j in range(plan.row_period):
            count = -(-(plan.half - j) // plan.row_period)
            source = plan.half_kept * upper + plan.half_blocks * j
            turn, place = divmod(j + plan.half * upper, plan.row_period)
            target = plan.blocks * place + turn
            for part in range(2):
                whole[part, target : target + count, :] = matrix[part, source : source + count, :]


def from_matrix(plan, matrix, tiles):
    width, blocks = plan.width, plan.blocks
    for i in range(plan.tile_period):
        for part in range(2):
            row, offset = divmod(LANES * i, width)
            flat = None
            start = -offset
            while start < LANES:
                turn, j = divmod(row, plan.row_period)
                rows = matrix[part, blocks * j + turn : blocks * (j + 1) + turn, :]
                if start % LANES:
                    rows = pltpu.roll(rows, start % LANES, axis=1)
                if flat is None:
                    flat = rows
                else:
                    lane = lax.broadcasted_iota(jnp.int32, rows.shape, 1)
                    flat = jnp.where(lane < start, flat, rows)
                start += width
                row += 1
            tiles[blocks * (2 * i + part) : blocks * (2 * i + part + 1), :] = flat


def prepare(plan):
    split, coarse, ng = plan.split, plan.coarse, plan.ng

    def body(own_in, pair_in, kernel_in, left, right, twiddle, own, pair, factor, tiles, plain, ordered):
        del left, right, twiddle
        to_matrix(plan, own_in[...], tiles, own)
        to_matrix(plan, pair_in[...], tiles, pair)
        eight = 8 * LANES
        for q in range(0, plan.grid // eight):
            tiles[8 * q : 8 * q + 8, :] = kernel_in[eight * q : eight * (q + 1)].reshape(8, LANES)
        for q in range(plan.grid // eight * 8, plan.grid // LANES):
            tiles[q : q + 1, :] = kernel_in[LANES * q : LANES * (q + 1)].reshape(1, LANES)
        if plan.tail:
            q = plan.grid // LANES
            tiles[q : q + 1, : plan.tail] = kernel_in[LANES * q :].reshape(1, plan.tail)
        for j in range(plan.row_period):
            rows = shifted_rows(plan, tiles, 0, 1, j, plan.blocks)
            plain[pl.ds(j, plan.blocks, stride=plan.row_period), :] = rows * (1.0 / plan.grid)
        count = ng // 2
        lane = lax.broadcasted_iota(jnp.int32, (count, LANES), 1)
        for odd in range(2):
            base = plan.half_kept * odd
            for a in range(coarse):
                rows = None
                for b in range(split):
                    row, column = divmod(a + coarse * b, split)
                    piece = plain[pl.ds(coarse * odd + row, count, stride=2 * coarse), :]
                    shift = (ng * (b - column)) % LANES
                    if shift:
                        piece = pltpu.roll(piece, shift, axis=1)
                    rows = piece if rows is None else jnp.where(lane < ng * b, rows, piece)
                ordered[pl.ds(base + a, count, stride=coarse), :] = rows
            spare = plan.half_kept - plan.half
            if spare:
                ordered[base + plan.half : base + plan.half_kept, :] = jnp.zeros((spare, LANES), F32)
            for j in range(plan.row_period):
                rows = ordered[pl.ds(base + j, plan.half_blocks, stride=plan.row_period), :]
                first = base + plan.half_blocks * j
                factor[first : first + plan.half_blocks, :] = rows

    return pl.pallas_call(
        body,
        out_shape=[
            jax.ShapeDtypeStruct((2, plan.kept, LANES), F32),
            jax.ShapeDtypeStruct((2, plan.kept, LANES), F32),
            jax.ShapeDtypeStruct((plan.kept, LANES), F32),
        ],
        in_specs=[VMEM] * 3 + [ANYWHERE] * 3,
        out_specs=[VMEM] * 3,
        scratch_shapes=[
            pltpu.VMEM((2 * plan.padded_tiles, LANES), F32),
            pltpu.VMEM((plan.blocks * plan.row_period, LANES), F32),
            pltpu.VMEM((plan.kept, LANES), F32),
        ],
        compiler_params=pltpu.CompilerParams(vmem_limit_bytes=4 * 1024 * 1024),
        name="prepare",
    )


def exchange(plan, own, packed, tiles, near, fourier, kernel, left, right, twiddle):
    to_matrix(plan, packed, tiles, near)
    size = plan.half_kept
    parts = [slice(0, size), slice(size, 2 * size)]

    def put(index, real, imag, sign):
        real = real.astype(BF16)
        imag = imag.astype(BF16)
        above = slice(2 * size * index, 2 * size * index + size)
        below = slice(2 * size * index + size, 2 * size * (index + 1))
        fourier[above, :LANES] = real
        fourier[above, LANES:] = imag
        fourier[below, :LANES] = imag if sign > 0 else -imag
        fourier[below, LANES:] = -real if sign > 0 else real

    def dot(x, y):
        return jnp.dot(x, y, preferred_element_type=F32)

    def both(tables):
        return [
            dot(left[table], fourier[2 * size * index : 2 * size * (index + 1), :])
            for index, table in enumerate(tables)
        ]

    def halve(value):
        return value[:, :LANES], value[:, LANES:]

    density = []
    for part in parts:
        a, b, c, d = near[0, part, :], near[1, part, :], own[0, part, :], own[1, part, :]
        density.append((a * c + b * d, a * d - b * c))
    (low_real, low_imag), (high_real, high_imag) = density
    put(0, low_real + high_real, low_imag + high_imag, 1)
    put(1, low_real - high_real, low_imag - high_imag, 1)
    values = both((0, 1))
    cosine, sine = twiddle[0], twiddle[1]
    for index in range(2):
        real, imag = halve(values[index])
        values[index] = jnp.concatenate(
            [real * cosine + imag * sine, imag * cosine - real * sine], axis=1
        ).astype(BF16)
    values = [dot(value, right[0]) for value in values]
    for index, part in enumerate(parts):
        real, imag = halve(values[index])
        factor = kernel[part, :]
        values[index] = jnp.concatenate([real * factor, imag * factor], axis=1).astype(BF16)
    values = [dot(value, right[1]) for value in values]
    for index in range(2):
        real, imag = halve(values[index])
        put(index, real * cosine - imag * sine, imag * cosine + real * sine, -1)
    even, odd = both((0, 2))
    potential = [even + odd, even - odd]
    results = []
    last = 2 * plan.tiles - 2
    weight = -0.5 * tiles[last : last + 1, plan.tail : plan.tail + 1]
    for index, part in enumerate(parts):
        e, f = halve(potential[index])
        a, b = near[0, part, :], near[1, part, :]
        results.append((part, weight * (a * e - b * f), weight * (a * f + b * e)))
    return results


def scratch_of(plan):
    whole = max(plan.kept, plan.blocks * plan.row_period)
    return [
        pltpu.VMEM((2 * plan.padded_tiles, LANES), F32),
        pltpu.VMEM((2, whole, LANES), F32),
        pltpu.VMEM((2 * plan.kept, 2 * LANES), BF16),
    ]


def first_pair(plan, extra):
    def body(*refs):
        own, near_in, kernel, left, right, twiddle = refs[:6]
        bands = refs[6 : 6 + extra]
        accum, *matrices, tiles, near, fourier = refs[6 + extra :]
        results = exchange(plan, own, near_in[...], tiles, near, fourier, kernel, left, right, twiddle)
        for part, real, imag in results:
            accum[0, part, :] = real
            accum[1, part, :] = imag
        for band, matrix in zip(bands, matrices):
            to_matrix(plan, band[...], tiles, matrix)

    matrix = jax.ShapeDtypeStruct((2, plan.kept, LANES), F32)
    return pl.pallas_call(
        body,
        out_shape=[matrix] * (1 + extra),
        in_specs=[VMEM] * (6 + extra),
        out_specs=[VMEM] * (1 + extra),
        scratch_shapes=scratch_of(plan),
        compiler_params=pltpu.CompilerParams(vmem_limit_bytes=16 * 1024 * 1024),
        name="first_pair",
    )


def overlaps(plan, count, total, bands):
    lane = lax.broadcasted_iota(jnp.int32, (1, count), 1)
    norm = 1.0 / math.sqrt(plan.grid)
    sums = [jnp.zeros((1, count), F32)] * 2
    e, f = total[0], total[1]
    for place, band in bands:
        c, d = band[0], band[1]
        parts = (c * e + d * f, c * f - d * e)
        for part in range(2):
            value = jnp.sum(jnp.sum(parts[part], axis=0, keepdims=True), axis=1, keepdims=True)
            sums[part] = jnp.where(lane == place, value * norm, sums[part])
    return sums


def second_pair(plan, others):
    count = others + 1

    def body(*refs):
        own, accum, far_in, near_in, kernel, left, right, twiddle, pair = refs[:9]
        extra = (others - 1) // 2
        shifted = refs[9 : 9 + extra]
        crossed = refs[9 + extra : 9 + 2 * extra]
        out, gram, tiles, near, fourier, total, flat, small, sent, spare, *matrices = refs[8 + others :]
        here = lax.axis_index("band")
        packed = jnp.where(here % 2 == 1, near_in[...], far_in[...])
        for band, matrix in zip(crossed, matrices):
            to_matrix(plan, band[...], spare, matrix)
        results = exchange(plan, own, packed, tiles, near, fourier, kernel, left, right, twiddle)
        for part, real, imag in results:
            total[0, part, :] = (accum[0, part, :] + real).astype(BF16).astype(F32)
            total[1, part, :] = (accum[1, part, :] + imag).astype(BF16).astype(F32)
        join_halves(plan, total, near)
        from_matrix(plan, near, tiles)
        for q in range(plan.tiles):
            turn, i = divmod(q, plan.tile_period)
            rows = tiles[pl.ds(2 * plan.blocks * i + turn, 2, stride=plan.blocks), :].astype(BF16)
            used = min(LANES, plan.grid - LANES * q)
            if used:
                flat[:, LANES * q : LANES * q + used] = rows[:, :used]
        copies = [
            pltpu.make_async_copy(flat, out, sent.at[0]),
            pltpu.make_async_copy(small, gram, sent.at[1]),
        ]
        copies[0].start()

        @pl.when(here >= 0)
        def _():
            pairs = [(here, own), (here ^ 1, pair)]
            for step in range(1, count // 2):
                for start, matrix in ((here, shifted[step - 1]), (here ^ 1, matrices[step - 1])):
                    source = start - 2 * step
                    pairs.append((jnp.where(source < 0, source + count, source), matrix))
            sums = overlaps(plan, count, total, pairs)
            for part in range(2):
                small[part] = sums[part]

        copies[1].start()
        for copy in copies:
            copy.wait()

    return pl.pallas_call(
        body,
        out_shape=[
            jax.ShapeDtypeStruct((2, plan.grid), BF16),
            jax.ShapeDtypeStruct((2, 1, count), F32),
        ],
        in_specs=[VMEM] * (8 + others),
        out_specs=[ANYWHERE] * 2,
        scratch_shapes=scratch_of(plan)
        + [
            pltpu.VMEM((2, plan.kept, LANES), F32),
            pltpu.VMEM((2, plan.grid), BF16),
            pltpu.VMEM((2, 1, count), F32),
            pltpu.SemaphoreType.DMA((2,)),
            pltpu.VMEM((2 * plan.padded_tiles, LANES), F32),
        ]
        + [pltpu.VMEM((2, plan.kept, LANES), F32)] * ((others - 1) // 2),
        compiler_params=pltpu.CompilerParams(vmem_limit_bytes=16 * 1024 * 1024),
        name="second_pair",
    )


def shards(orbitals, occupation, kernel):
    plan = Plan(orbitals.shape[3])
    pools = lax.axis_size("pool")
    groups = lax.axis_size("band")
    others = groups - 1

    def move(array, target):
        pairs = [
            (p * groups + g, q * groups + h)
            for p in range(pools)
            for g in range(groups)
            for q, h in [target(p, g)]
        ]
        return lax.ppermute(array, ("pool", "band"), pairs)

    own = pack(plan)(orbitals[0, 0], occupation[0])
    near = move(own, lambda p, g: ((p + 1) % pools, g))
    far = move(own, lambda p, g: ((p + 1) % pools, (g + 1) % groups) if g % 2 else (p, g + 1))
    partner = lambda p, g: (p, g ^ 1)
    pair_in = move(own, partner)
    shifted, crossed = [], []
    for step in range(1, groups // 2):
        shifted.append(move(own, lambda p, g: (p, (g + 2 * step) % groups)))
        crossed.append(move(shifted[-1], partner))
    swapped = move(near, partner)
    tables = constants(plan)
    mine, pair, factor = prepare(plan)(own, pair_in, kernel, *tables)
    accum, *matrices = first_pair(plan, len(shifted))(
        mine, near, factor, *tables, *shifted
    )
    exchanged, gram = second_pair(plan, others)(
        mine, accum, far, swapped, factor, *tables, pair, *matrices, *crossed
    )
    return exchanged[None, None], jnp.swapaxes(gram, 1, 2)[None]


def solution(mesh):
    return jax.shard_map(
        shards,
        mesh=mesh,
        in_specs=(P("pool", "band", None, None), P("pool", "band"), P()),
        out_specs=(P("pool", "band", None, None), P("pool", None, None, "band")),
        check_vma=False,
    )
```

time: 23.3 us -> 22.4 us (0.961)
  Pallas kernels: 5.06 us -> 4.47 us
  local copies, waits for them, and re-layouts: 4.63 us -> 4.34 us
    pallas_call x4 -> x3, Pallas kernels: 4.82 us -> 4.22 us  [the longest x1 2.45 us: shards(): second_pair(plan, others)]
    unnamed x14, local copies, waits for them, and re-layouts: 4.63 us -> 4.34 us
  transfers between devices with their start and end apart: 6 -> 6, of which waited for: 1 -> 1; matrix products, arithmetic and copies ran while one was open for 0% -> 0% of each run, Pallas kernels for 14% -> 8%
where the time goes in v5:
time: 22.4 us; the launch traced here: 22.1 us
  waiting for transfers between devices  6.38 us (28%)
  starting transfers between devices  5.56 us (25%)
  Pallas kernels  4.47 us (20%)
  local copies, waits for them, and re-layouts  4.34 us (19%)
  between operations  1.39 us (6%)
    ppermute x6, waiting for transfers between devices, move(): return lax.ppermute(array, ('pool', 'band'), pairs)  6.38 us
    ppermute x6, starting transfers between devices, move(): return lax.ppermute(array, ('pool', 'band'), pairs)  5.56 us
    unnamed x14, local copies, waits for them, and re-layouts  4.34 us
    pallas_call x1, Pallas kernels, shards(): second_pair(plan, others)  2.45 us
    pallas_call x1, Pallas kernels, shards(): first_pair(plan, len(shifted))(mine, near, factor, *tables, *shifted)  1.1 us
    pallas_call x1, Pallas kernels, shards(): mine, pair, factor = prepare(plan)(own, pair_in, kernel, *tables)  0.68 us
  transfers between devices with their start and end apart: 6, of which 1 were waited for; matrix products, arithmetic and copies ran while one was open for 0% of the time, Pallas kernels for 8%

profile of v5, /device:TPU:0, one launch (start us, length us, event | category | flops | bytes accessed | tf_op | source)
XLA Modules:
  0.0 22.1 jit_solution(8933071916120534788)
XLA Ops:
  0.6 0.0 copy-start.2
  1.3 0.0 copy-start.6
  1.3 0.9 %copy-done.6 = bf16[1,1,2,46656]{3,2,1,0:T(2,128)(2,1)S(1)} copy-done((bf16[1,1,2,46656]{3,2,1,0:T(2,128)(2,1)S(1)}, bf16[1,1,2,46656]{3,2,1,0:T(2,128)(2,1)}, u32[]{:S(2)}) %copy-start.6) | copy-done | bytes 186648
  2.3 0.2 %pack.1.own_in = bf16[730,128]{1,0:T(8,128)(2,1)S(1)} custom-call(bf16[2,46656]{1,0:T(2,128)(2,1)S(1)} %bitcast.7, s32[1]{0:T(128)} %bitcast.6.occupation), custom_call_target="tpu_custom_call" | custom-call | tf_op jit(solution)/shard_map/pack/pallas_call | solution.py:404
  2.5 3.0 %collective-permute-start.1 = (bf16[730,128]{1,0:T(8,128)(2,1)S(1)}, bf16[730,128]{1,0:T(8,128)(2,1)S(1)}, u32[]{:S(2)}, u32[]{:S(2)}) collective-permute-start(bf16[730,128]{1,0:T(8,128)(2,1)S(1)} %pack.1.own_in), channel_id=1, source_target_pairs={{0,4},{1,5},{2,6},{3,7},{4,8},{5,9},{6,10},{7,11},{8,12},{9,13},{1... | collective-permute-start | bytes 560648 | tf_op jit(solution)/shard_map/ppermute | solution.py:402
  5.5 1.5 %collective-permute-start.2 = (bf16[730,128]{1,0:T(8,128)(2,1)S(1)}, bf16[730,128]{1,0:T(8,128)(2,1)S(1)}, u32[]{:S(2)}, u32[]{:S(2)}) collective-permute-start(bf16[730,128]{1,0:T(8,128)(2,1)S(1)} %pack.1.own_in), channel_id=1, source_target_pairs={{0,2},{1,3},{2,0},{3,1},{4,6},{5,7},{6,4},{7,5},{8,10},{9,11},{10,... | collective-permute-start | bytes 560648 | tf_op jit(solution)/shard_map/ppermute | solution.py:402
  7.0 0.0 collective-permute-start
  7.0 0.5 %collective-permute-start.3 = (bf16[730,128]{1,0:T(8,128)(2,1)S(1)}, bf16[730,128]{1,0:T(8,128)(2,1)S(1)}, u32[]{:S(2)}, u32[]{:S(2)}) collective-permute-start(bf16[730,128]{1,0:T(8,128)(2,1)S(1)} %pack.1.own_in), channel_id=1, source_target_pairs={{0,1},{1,6},{2,3},{3,4},{4,5},{5,10},{6,7},{7,8},{8,9},{9,14},{10,... | collective-permute-start | bytes 560648 | tf_op jit(solution)/shard_map/ppermute | solution.py:402
  7.6 6.4 %collective-permute-done.1.refs_1_ = bf16[730,128]{1,0:T(8,128)(2,1)S(1)} collective-permute-done((bf16[730,128]{1,0:T(8,128)(2,1)S(1)}, bf16[730,128]{1,0:T(8,128)(2,1)S(1)}, u32[]{:S(2)}, u32[]{:S(2)}) %collective-permute-start.1) | collective-permute-done | bytes 186912 | tf_op jit(solution)/shard_map/ppermute | solution.py:402
  13.9 0.0 collective-permute-start.4
  13.9 0.0 collective-permute-done.2.refs_6_
  13.9 0.5 %collective-permute-start.5 = (bf16[730,128]{1,0:T(8,128)(2,1)S(1)}, bf16[730,128]{1,0:T(8,128)(2,1)S(1)}, u32[]{:S(2)}, u32[]{:S(2)}) collective-permute-start(bf16[730,128]{1,0:T(8,128)(2,1)S(1)} %collective-permute-done.2.refs_6_), channel_id=1, source_target_pairs={{0,1},{1,0},{2,3},{3,2},{4,5},{5,4},{6,7},{7,6},{8,9},{9,8},{10,11... | collective-permute-start | bytes 560648 | tf_op jit(solution)/shard_map/ppermute | solution.py:402
  14.4 0.0 collective-permute-done.pair_in
  14.4 0.0 copy-done.2
  14.4 0.0 copy-start
  14.4 1.1 %copy-done = bf16[3,224,448]{2,1,0:T(8,128)(2,1)S(1)} copy-done((bf16[3,224,448]{2,1,0:T(8,128)(2,1)S(1)}, bf16[3,224,448]{2,1,0:T(8,128)(2,1)}, u32[]{:S(2)}) %copy-start) | copy-done | bytes 602136
  15.5 0.0 copy-start.3
  15.5 0.9 %copy-done.3 = f32[2,224,128]{2,1,0:T(8,128)S(1)} copy-done((f32[2,224,128]{2,1,0:T(8,128)S(1)}, f32[2,224,128]{2,1,0:T(8,128)}, u32[]{:S(2)}) %copy-start.3) | copy-done | bytes 229400
  16.5 0.0 copy-start.5
  16.5 0.9 %copy-done.5 = f32[46656]{0:T(1024)S(1)} copy-done((f32[46656]{0:T(1024)S(1)}, f32[46656]{0:T(1024)}, u32[]{:S(2)}) %copy-start.5) | copy-done | bytes 186648
  17.4 0.0 copy-start.1
  17.4 0.0 copy-start.4
  17.4 0.7 %prepare.1 = (f32[2,448,128]{2,1,0:T(8,128)S(1)}, f32[2,448,128]{2,1,0:T(8,128)S(1)}, f32[448,128]{1,0:T(8,128)S(1)}) custom-call(bf16[730,128]{1,0:T(8,128)(2,1)S(1)} %pack.1.own_in, bf16[730,128]{1,0:T(8,128)(2,1)S(1)} %collective-permute-done.pair_in, f32[46656]{0:T(1024)S(1)} %copy-done.5, bf16[3,224,448]{2,1,0:T(8,128)(2,1)S(1)} %copy-done, ...), custom_call_target="tpu_custom_call" | custom-call | tf_op jit(solution)/shard_map/prepare/pallas_call | solution.py:415
  18.1 0.4 %copy-done.1 = bf16[3,224,448]{2,1,0:T(8,128)(2,1)S(1)} copy-done((bf16[3,224,448]{2,1,0:T(8,128)(2,1)S(1)}, bf16[3,224,448]{2,1,0:T(8,128)(2,1)}, u32[]{:S(2)}) %copy-start.1) | copy-done | bytes 602136
  18.5 0.0 copy-done.4
  18.6 1.1 %first_pair.1 = (f32[2,448,128]{2,1,0:T(8,128)S(1)}, f32[2,448,128]{2,1,0:T(8,128)S(1)}) custom-call(f32[2,448,128]{2,1,0:T(8,128)S(1)} %get-tuple-element.9.refs_0_, bf16[730,128]{1,0:T(8,128)(2,1)S(1)} %collective-permute-done.1.refs_1_, f32[448,128]{1,0:T(8,128)S(1)} %get-tuple-element.10.refs_2_.refs_4_, bf16[3,224,448]{2,1,0:T(8,128)(2,1)S(1)} %copy-done.1, ...), custom_call_target="tpu_custom_call" | custom-call | tf_op jit(solution)/shard_map/first_pair/pallas_call | solution.py:416
  19.7 0.0 collective-permute-done.3.refs_2_
  19.7 0.0 collective-permute-done.4.refs_3_
  19.7 0.0 collective-permute-done.5.refs_10_
  19.7 2.4 %second_pair.1 = (bf16[2,46656]{1,0:T(2,128)(2,1)}, f32[2,1,4]{2,1,0:T(1,128)}) custom-call(f32[2,448,128]{2,1,0:T(8,128)S(1)} %get-tuple-element.9.refs_0_, f32[2,448,128]{2,1,0:T(8,128)S(1)} %get-tuple-element.11.refs_1_, bf16[730,128]{1,0:T(8,128)(2,1)S(1)} %collective-permute-done.3.refs_2_, bf16[730,128]{1,0:T(8,128)(2,1)S(1)} %collective-permute-done.4.refs_3_, ...), custom_call_target="tpu_custom_call" | custom-call | tf_op jit(solution)/shard_map/second_pair/pallas_call | solution.py:419
Async XLA Ops:
  0.6 13.8 %copy-start.2 = (bf16[2,256,256]{2,1,0:T(8,128)(2,1)S(1)}, bf16[2,256,256]{2,1,0:T(8,128)(2,1)}, u32[]{:S(2)}) copy-start(bf16[2,256,256]{2,1,0:T(8,128)(2,1)} %constant.7.clone.right.refs_4_.refs_6_) | copy-start | bytes 786436
  1.3 0.9 %copy-start.6 = (bf16[1,1,2,46656]{3,2,1,0:T(2,128)(2,1)S(1)}, bf16[1,1,2,46656]{3,2,1,0:T(2,128)(2,1)}, u32[]{:S(2)}) copy-start(bf16[1,1,2,46656]{3,2,1,0:T(2,128)(2,1)} %param.6) | copy-start | bytes 559876
  2.5 11.4 %collective-permute-start.1 = (bf16[730,128]{1,0:T(8,128)(2,1)S(1)}, bf16[730,128]{1,0:T(8,128)(2,1)S(1)}, u32[]{:S(2)}, u32[]{:S(2)}) collective-permute-start(bf16[730,128]{1,0:T(8,128)(2,1)S(1)} %pack.1.own_in), channel_id=1, source_target_pairs={{0,4},{1,5},{2,6},{3,7},{4,8},{5,9},{6,10},{7,11},{8,12},{9,13},{1... | collective-permute-start | bytes 560648 | tf_op jit(solution)/shard_map/ppermute | solution.py:402
  5.5 8.4 %collective-permute-start.2 = (bf16[730,128]{1,0:T(8,128)(2,1)S(1)}, bf16[730,128]{1,0:T(8,128)(2,1)S(1)}, u32[]{:S(2)}, u32[]{:S(2)}) collective-permute-start(bf16[730,128]{1,0:T(8,128)(2,1)S(1)} %pack.1.own_in), channel_id=1, source_target_pairs={{0,2},{1,3},{2,0},{3,1},{4,6},{5,7},{6,4},{7,5},{8,10},{9,11},{10,... | collective-permute-start | bytes 560648 | tf_op jit(solution)/shard_map/ppermute | solution.py:402
  7.0 7.4 %collective-permute-start = (bf16[730,128]{1,0:T(8,128)(2,1)S(1)}, bf16[730,128]{1,0:T(8,128)(2,1)S(1)}, u32[]{:S(2)}, u32[]{:S(2)}) collective-permute-start(bf16[730,128]{1,0:T(8,128)(2,1)S(1)} %pack.1.own_in), channel_id=1, source_target_pairs={{0,1},{1,0},{2,3},{3,2},{4,5},{5,4},{6,7},{7,6},{8,9},{9,8},{10,11... | collective-permute-start | bytes 560648 | tf_op jit(solution)/shard_map/ppermute | solution.py:402
  7.0 12.6 %collective-permute-start.3 = (bf16[730,128]{1,0:T(8,128)(2,1)S(1)}, bf16[730,128]{1,0:T(8,128)(2,1)S(1)}, u32[]{:S(2)}, u32[]{:S(2)}) collective-permute-start(bf16[730,128]{1,0:T(8,128)(2,1)S(1)} %pack.1.own_in), channel_id=1, source_target_pairs={{0,1},{1,6},{2,3},{3,4},{4,5},{5,10},{6,7},{7,8},{8,9},{9,14},{10,... | collective-permute-start | bytes 560648 | tf_op jit(solution)/shard_map/ppermute | solution.py:402
  13.9 5.7 %collective-permute-start.4 = (bf16[730,128]{1,0:T(8,128)(2,1)S(1)}, bf16[730,128]{1,0:T(8,128)(2,1)S(1)}, u32[]{:S(2)}, u32[]{:S(2)}) collective-permute-start(bf16[730,128]{1,0:T(8,128)(2,1)S(1)} %collective-permute-done.1.refs_1_), channel_id=1, source_target_pairs={{0,1},{1,0},{2,3},{3,2},{4,5},{5,4},{6,7},{7,6},{8,9},{9,8},{10,11... | collective-permute-start | bytes 560648 | tf_op jit(solution)/shard_map/ppermute | solution.py:402
  13.9 5.8 %collective-permute-start.5 = (bf16[730,128]{1,0:T(8,128)(2,1)S(1)}, bf16[730,128]{1,0:T(8,128)(2,1)S(1)}, u32[]{:S(2)}, u32[]{:S(2)}) collective-permute-start(bf16[730,128]{1,0:T(8,128)(2,1)S(1)} %collective-permute-done.2.refs_6_), channel_id=1, source_target_pairs={{0,1},{1,0},{2,3},{3,2},{4,5},{5,4},{6,7},{7,6},{8,9},{9,8},{10,11... | collective-permute-start | bytes 560648 | tf_op jit(solution)/shard_map/ppermute | solution.py:402
  14.4 1.1 %copy-start = (bf16[3,224,448]{2,1,0:T(8,128)(2,1)S(1)}, bf16[3,224,448]{2,1,0:T(8,128)(2,1)}, u32[]{:S(2)}) copy-start(bf16[3,224,448]{2,1,0:T(8,128)(2,1)} %constant.6.clone.left.refs_3_.refs_5_) | copy-start | bytes 1806340
  15.5 0.9 %copy-start.3 = (f32[2,224,128]{2,1,0:T(8,128)S(1)}, f32[2,224,128]{2,1,0:T(8,128)}, u32[]{:S(2)}) copy-start(f32[2,224,128]{2,1,0:T(8,128)} %constant.8.clone.twiddle.refs_5_.refs_7_) | copy-start | bytes 688132
  16.5 0.9 %copy-start.5 = (f32[46656]{0:T(1024)S(1)}, f32[46656]{0:T(1024)}, u32[]{:S(2)}) copy-start(f32[46656]{0:T(1024)} %kernel_in.1) | copy-start | bytes 559876
  17.4 1.1 %copy-start.1 = (bf16[3,224,448]{2,1,0:T(8,128)(2,1)S(1)}, bf16[3,224,448]{2,1,0:T(8,128)(2,1)}, u32[]{:S(2)}) copy-start(bf16[3,224,448]{2,1,0:T(8,128)(2,1)} %constant.6.clone.left.refs_3_.refs_5_) | copy-start | bytes 1806340
  17.4 1.1 %copy-start.4 = (f32[2,224,128]{2,1,0:T(8,128)S(1)}, f32[2,224,128]{2,1,0:T(8,128)}, u32[]{:S(2)}) copy-start(f32[2,224,128]{2,1,0:T(8,128)} %constant.8.clone.twiddle.refs_5_.refs_7_) | copy-start | bytes 688132

commit v6 on v5

--- a/solution.py
+++ b/solution.py
@@ -305,17 +305,25 @@
 
 
 def overlaps(plan, count, total, bands):
+    step = 56 if plan.kept % 56 == 0 else 8
+    sums = [jnp.zeros((8, LANES), F32)] * (2 * count)
+    for first in range(0, plan.kept, step):
+        rows = slice(first, first + step)
+        e, f = total[0, rows, :], total[1, rows, :]
+        for index, (_, band) in enumerate(bands):
+            c, d = band[0, rows, :], band[1, rows, :]
+            for part, value in enumerate((c * e + d * f, c * f - d * e)):
+                value = jnp.sum(value.reshape(step // 8, 8, LANES), axis=0)
+                sums[2 * index + part] = sums[2 * index + part] + value
     lane = lax.broadcasted_iota(jnp.int32, (1, count), 1)
     norm = 1.0 / math.sqrt(plan.grid)
-    sums = [jnp.zeros((1, count), F32)] * 2
-    e, f = total[0], total[1]
-    for place, band in bands:
-        c, d = band[0], band[1]
-        parts = (c * e + d * f, c * f - d * e)
+    grams = [jnp.zeros((1, count), F32)] * 2
+    for index, (place, _) in enumerate(bands):
         for part in range(2):
-            value = jnp.sum(jnp.sum(parts[part], axis=0, keepdims=True), axis=1, keepdims=True)
-            sums[part] = jnp.where(lane == place, value * norm, sums[part])
-    return sums
+            value = jnp.sum(sums[2 * index + part], axis=0, keepdims=True)
+            value = jnp.sum(value, axis=1, keepdims=True)
+            grams[part] = jnp.where(lane == place, value * norm, grams[part])
+    return grams
 
 
 def second_pair(plan, others):
@@ -335,6 +343,14 @@
         for part, real, imag in results:
             total[0, part, :] = (accum[0, part, :] + real).astype(BF16).astype(F32)
             total[1, part, :] = (accum[1, part, :] + imag).astype(BF16).astype(F32)
+        pairs = [(here, own), (here ^ 1, pair)]
+        for step in range(1, count // 2):
+            for start, matrix in ((here, shifted[step - 1]), (here ^ 1, matrices[step - 1])):
+                source = start - 2 * step
+                pairs.append((jnp.where(source < 0, source + count, source), matrix))
+        sums = overlaps(plan, count, total, pairs)
+        for part in range(2):
+            small[part] = sums[part]
         join_halves(plan, total, near)
         from_matrix(plan, near, tiles)
         for q in range(plan.tiles):
@@ -347,20 +363,8 @@
             pltpu.make_async_copy(flat, out, sent.at[0]),
             pltpu.make_async_copy(small, gram, sent.at[1]),
         ]
-        copies[0].start()
-
-        @pl.when(here >= 0)
-        def _():
-            pairs = [(here, own), (here ^ 1, pair)]
-            for step in range(1, count // 2):
-                for start, matrix in ((here, shifted[step - 1]), (here ^ 1, matrices[step - 1])):
-                    source = start - 2 * step
-                    pairs.append((jnp.where(source < 0, source + count, source), matrix))
-            sums = overlaps(plan, count, total, pairs)
-            for part in range(2):
-                small[part] = sums[part]
-
-        copies[1].start()
+        for copy in copies:
+            copy.start()
         for copy in copies:
             copy.wait()
 

time: 22.4 us -> 22.4 us (level)
  no operation moved by 1% of the time
where the time goes in v6:
time: 22.4 us; the launch traced here: 22.1 us
  waiting for transfers between devices  6.38 us (28%)
  starting transfers between devices  5.56 us (25%)
  Pallas kernels  4.45 us (20%)
  local copies, waits for them, and re-layouts  4.34 us (19%)
  between operations  1.39 us (6%)
    ppermute x6, waiting for transfers between devices, move(): return lax.ppermute(array, ('pool', 'band'), pairs)  6.38 us
    ppermute x6, starting transfers between devices, move(): return lax.ppermute(array, ('pool', 'band'), pairs)  5.56 us
    unnamed x14, local copies, waits for them, and re-layouts  4.34 us
    pallas_call x1, Pallas kernels, shards(): second_pair(plan, others)  2.43 us
    pallas_call x1, Pallas kernels, shards(): first_pair(plan, len(shifted))(mine, near, factor, *tables, *shifted)  1.1 us
    pallas_call x1, Pallas kernels, shards(): mine, pair, factor = prepare(plan)(own, pair_in, kernel, *tables)  0.68 us
  transfers between devices with their start and end apart: 6, of which 1 were waited for; matrix products, arithmetic and copies ran while one was open for 0% of the time, Pallas kernels for 8%

profile of v6, /device:TPU:0, one launch (start us, length us, event | category | flops | bytes accessed | tf_op | source)
XLA Modules:
  0.0 22.1 jit_solution(10929330092271721937)
XLA Ops:
  0.6 0.0 copy-start.2
  1.3 0.0 copy-start.6
  1.3 0.9 %copy-done.6 = bf16[1,1,2,46656]{3,2,1,0:T(2,128)(2,1)S(1)} copy-done((bf16[1,1,2,46656]{3,2,1,0:T(2,128)(2,1)S(1)}, bf16[1,1,2,46656]{3,2,1,0:T(2,128)(2,1)}, u32[]{:S(2)}) %copy-start.6) | copy-done | bytes 186648
  2.3 0.2 %pack.1.own_in = bf16[730,128]{1,0:T(8,128)(2,1)S(1)} custom-call(bf16[2,46656]{1,0:T(2,128)(2,1)S(1)} %bitcast.7, s32[1]{0:T(128)} %bitcast.6.occupation), custom_call_target="tpu_custom_call" | custom-call | tf_op jit(solution)/shard_map/pack/pallas_call | solution.py:408
  2.5 3.0 %collective-permute-start.1 = (bf16[730,128]{1,0:T(8,128)(2,1)S(1)}, bf16[730,128]{1,0:T(8,128)(2,1)S(1)}, u32[]{:S(2)}, u32[]{:S(2)}) collective-permute-start(bf16[730,128]{1,0:T(8,128)(2,1)S(1)} %pack.1.own_in), channel_id=1, source_target_pairs={{0,4},{1,5},{2,6},{3,7},{4,8},{5,9},{6,10},{7,11},{8,12},{9,13},{1... | collective-permute-start | bytes 560648 | tf_op jit(solution)/shard_map/ppermute | solution.py:406
  5.5 1.5 %collective-permute-start.2 = (bf16[730,128]{1,0:T(8,128)(2,1)S(1)}, bf16[730,128]{1,0:T(8,128)(2,1)S(1)}, u32[]{:S(2)}, u32[]{:S(2)}) collective-permute-start(bf16[730,128]{1,0:T(8,128)(2,1)S(1)} %pack.1.own_in), channel_id=1, source_target_pairs={{0,2},{1,3},{2,0},{3,1},{4,6},{5,7},{6,4},{7,5},{8,10},{9,11},{10,... | collective-permute-start | bytes 560648 | tf_op jit(solution)/shard_map/ppermute | solution.py:406
  7.0 0.0 collective-permute-start
  7.0 0.5 %collective-permute-start.3 = (bf16[730,128]{1,0:T(8,128)(2,1)S(1)}, bf16[730,128]{1,0:T(8,128)(2,1)S(1)}, u32[]{:S(2)}, u32[]{:S(2)}) collective-permute-start(bf16[730,128]{1,0:T(8,128)(2,1)S(1)} %pack.1.own_in), channel_id=1, source_target_pairs={{0,1},{1,6},{2,3},{3,4},{4,5},{5,10},{6,7},{7,8},{8,9},{9,14},{10,... | collective-permute-start | bytes 560648 | tf_op jit(solution)/shard_map/ppermute | solution.py:406
  7.6 6.4 %collective-permute-done.1.refs_1_ = bf16[730,128]{1,0:T(8,128)(2,1)S(1)} collective-permute-done((bf16[730,128]{1,0:T(8,128)(2,1)S(1)}, bf16[730,128]{1,0:T(8,128)(2,1)S(1)}, u32[]{:S(2)}, u32[]{:S(2)}) %collective-permute-start.1) | collective-permute-done | bytes 186912 | tf_op jit(solution)/shard_map/ppermute | solution.py:406
  13.9 0.0 collective-permute-start.4
  13.9 0.0 collective-permute-done.2.refs_6_
  13.9 0.5 %collective-permute-start.5 = (bf16[730,128]{1,0:T(8,128)(2,1)S(1)}, bf16[730,128]{1,0:T(8,128)(2,1)S(1)}, u32[]{:S(2)}, u32[]{:S(2)}) collective-permute-start(bf16[730,128]{1,0:T(8,128)(2,1)S(1)} %collective-permute-done.2.refs_6_), channel_id=1, source_target_pairs={{0,1},{1,0},{2,3},{3,2},{4,5},{5,4},{6,7},{7,6},{8,9},{9,8},{10,11... | collective-permute-start | bytes 560648 | tf_op jit(solution)/shard_map/ppermute | solution.py:406
  14.4 0.0 collective-permute-done.pair_in
  14.4 0.0 copy-done.2
  14.4 0.0 copy-start
  14.4 1.1 %copy-done = bf16[3,224,448]{2,1,0:T(8,128)(2,1)S(1)} copy-done((bf16[3,224,448]{2,1,0:T(8,128)(2,1)S(1)}, bf16[3,224,448]{2,1,0:T(8,128)(2,1)}, u32[]{:S(2)}) %copy-start) | copy-done | bytes 602136
  15.5 0.0 copy-start.3
  15.5 0.9 %copy-done.3 = f32[2,224,128]{2,1,0:T(8,128)S(1)} copy-done((f32[2,224,128]{2,1,0:T(8,128)S(1)}, f32[2,224,128]{2,1,0:T(8,128)}, u32[]{:S(2)}) %copy-start.3) | copy-done | bytes 229400
  16.5 0.0 copy-start.5
  16.5 0.9 %copy-done.5 = f32[46656]{0:T(1024)S(1)} copy-done((f32[46656]{0:T(1024)S(1)}, f32[46656]{0:T(1024)}, u32[]{:S(2)}) %copy-start.5) | copy-done | bytes 186648
  17.4 0.0 copy-start.1
  17.4 0.0 copy-start.4
  17.4 0.7 %prepare.1 = (f32[2,448,128]{2,1,0:T(8,128)S(1)}, f32[2,448,128]{2,1,0:T(8,128)S(1)}, f32[448,128]{1,0:T(8,128)S(1)}) custom-call(bf16[730,128]{1,0:T(8,128)(2,1)S(1)} %pack.1.own_in, bf16[730,128]{1,0:T(8,128)(2,1)S(1)} %collective-permute-done.pair_in, f32[46656]{0:T(1024)S(1)} %copy-done.5, bf16[3,224,448]{2,1,0:T(8,128)(2,1)S(1)} %copy-done, ...), custom_call_target="tpu_custom_call" | custom-call | tf_op jit(solution)/shard_map/prepare/pallas_call | solution.py:419
  18.1 0.4 %copy-done.1 = bf16[3,224,448]{2,1,0:T(8,128)(2,1)S(1)} copy-done((bf16[3,224,448]{2,1,0:T(8,128)(2,1)S(1)}, bf16[3,224,448]{2,1,0:T(8,128)(2,1)}, u32[]{:S(2)}) %copy-start.1) | copy-done | bytes 602136
  18.5 0.0 copy-done.4
  18.6 1.1 %first_pair.1 = (f32[2,448,128]{2,1,0:T(8,128)S(1)}, f32[2,448,128]{2,1,0:T(8,128)S(1)}) custom-call(f32[2,448,128]{2,1,0:T(8,128)S(1)} %get-tuple-element.9.refs_0_, bf16[730,128]{1,0:T(8,128)(2,1)S(1)} %collective-permute-done.1.refs_1_, f32[448,128]{1,0:T(8,128)S(1)} %get-tuple-element.10.refs_2_.refs_4_, bf16[3,224,448]{2,1,0:T(8,128)(2,1)S(1)} %copy-done.1, ...), custom_call_target="tpu_custom_call" | custom-call | tf_op jit(solution)/shard_map/first_pair/pallas_call | solution.py:420
  19.7 0.0 collective-permute-done.3.refs_2_
  19.7 0.0 collective-permute-done.4.refs_3_
  19.7 0.0 collective-permute-done.5.refs_10_
  19.7 2.4 %second_pair.1 = (bf16[2,46656]{1,0:T(2,128)(2,1)}, f32[2,1,4]{2,1,0:T(1,128)}) custom-call(f32[2,448,128]{2,1,0:T(8,128)S(1)} %get-tuple-element.9.refs_0_, f32[2,448,128]{2,1,0:T(8,128)S(1)} %get-tuple-element.11.refs_1_, bf16[730,128]{1,0:T(8,128)(2,1)S(1)} %collective-permute-done.3.refs_2_, bf16[730,128]{1,0:T(8,128)(2,1)S(1)} %collective-permute-done.4.refs_3_, ...), custom_call_target="tpu_custom_call" | custom-call | tf_op jit(solution)/shard_map/second_pair/pallas_call | solution.py:423
Async XLA Ops:
  0.6 13.8 %copy-start.2 = (bf16[2,256,256]{2,1,0:T(8,128)(2,1)S(1)}, bf16[2,256,256]{2,1,0:T(8,128)(2,1)}, u32[]{:S(2)}) copy-start(bf16[2,256,256]{2,1,0:T(8,128)(2,1)} %constant.7.clone.right.refs_4_.refs_6_) | copy-start | bytes 786436
  1.3 0.9 %copy-start.6 = (bf16[1,1,2,46656]{3,2,1,0:T(2,128)(2,1)S(1)}, bf16[1,1,2,46656]{3,2,1,0:T(2,128)(2,1)}, u32[]{:S(2)}) copy-start(bf16[1,1,2,46656]{3,2,1,0:T(2,128)(2,1)} %param.6) | copy-start | bytes 559876
  2.5 11.4 %collective-permute-start.1 = (bf16[730,128]{1,0:T(8,128)(2,1)S(1)}, bf16[730,128]{1,0:T(8,128)(2,1)S(1)}, u32[]{:S(2)}, u32[]{:S(2)}) collective-permute-start(bf16[730,128]{1,0:T(8,128)(2,1)S(1)} %pack.1.own_in), channel_id=1, source_target_pairs={{0,4},{1,5},{2,6},{3,7},{4,8},{5,9},{6,10},{7,11},{8,12},{9,13},{1... | collective-permute-start | bytes 560648 | tf_op jit(solution)/shard_map/ppermute | solution.py:406
  5.5 8.4 %collective-permute-start.2 = (bf16[730,128]{1,0:T(8,128)(2,1)S(1)}, bf16[730,128]{1,0:T(8,128)(2,1)S(1)}, u32[]{:S(2)}, u32[]{:S(2)}) collective-permute-start(bf16[730,128]{1,0:T(8,128)(2,1)S(1)} %pack.1.own_in), channel_id=1, source_target_pairs={{0,2},{1,3},{2,0},{3,1},{4,6},{5,7},{6,4},{7,5},{8,10},{9,11},{10,... | collective-permute-start | bytes 560648 | tf_op jit(solution)/shard_map/ppermute | solution.py:406
  7.0 7.4 %collective-permute-start = (bf16[730,128]{1,0:T(8,128)(2,1)S(1)}, bf16[730,128]{1,0:T(8,128)(2,1)S(1)}, u32[]{:S(2)}, u32[]{:S(2)}) collective-permute-start(bf16[730,128]{1,0:T(8,128)(2,1)S(1)} %pack.1.own_in), channel_id=1, source_target_pairs={{0,1},{1,0},{2,3},{3,2},{4,5},{5,4},{6,7},{7,6},{8,9},{9,8},{10,11... | collective-permute-start | bytes 560648 | tf_op jit(solution)/shard_map/ppermute | solution.py:406
  7.0 12.6 %collective-permute-start.3 = (bf16[730,128]{1,0:T(8,128)(2,1)S(1)}, bf16[730,128]{1,0:T(8,128)(2,1)S(1)}, u32[]{:S(2)}, u32[]{:S(2)}) collective-permute-start(bf16[730,128]{1,0:T(8,128)(2,1)S(1)} %pack.1.own_in), channel_id=1, source_target_pairs={{0,1},{1,6},{2,3},{3,4},{4,5},{5,10},{6,7},{7,8},{8,9},{9,14},{10,... | collective-permute-start | bytes 560648 | tf_op jit(solution)/shard_map/ppermute | solution.py:406
  13.9 5.7 %collective-permute-start.4 = (bf16[730,128]{1,0:T(8,128)(2,1)S(1)}, bf16[730,128]{1,0:T(8,128)(2,1)S(1)}, u32[]{:S(2)}, u32[]{:S(2)}) collective-permute-start(bf16[730,128]{1,0:T(8,128)(2,1)S(1)} %collective-permute-done.1.refs_1_), channel_id=1, source_target_pairs={{0,1},{1,0},{2,3},{3,2},{4,5},{5,4},{6,7},{7,6},{8,9},{9,8},{10,11... | collective-permute-start | bytes 560648 | tf_op jit(solution)/shard_map/ppermute | solution.py:406
  13.9 5.8 %collective-permute-start.5 = (bf16[730,128]{1,0:T(8,128)(2,1)S(1)}, bf16[730,128]{1,0:T(8,128)(2,1)S(1)}, u32[]{:S(2)}, u32[]{:S(2)}) collective-permute-start(bf16[730,128]{1,0:T(8,128)(2,1)S(1)} %collective-permute-done.2.refs_6_), channel_id=1, source_target_pairs={{0,1},{1,0},{2,3},{3,2},{4,5},{5,4},{6,7},{7,6},{8,9},{9,8},{10,11... | collective-permute-start | bytes 560648 | tf_op jit(solution)/shard_map/ppermute | solution.py:406
  14.4 1.1 %copy-start = (bf16[3,224,448]{2,1,0:T(8,128)(2,1)S(1)}, bf16[3,224,448]{2,1,0:T(8,128)(2,1)}, u32[]{:S(2)}) copy-start(bf16[3,224,448]{2,1,0:T(8,128)(2,1)} %constant.6.clone.left.refs_3_.refs_5_) | copy-start | bytes 1806340
  15.5 0.9 %copy-start.3 = (f32[2,224,128]{2,1,0:T(8,128)S(1)}, f32[2,224,128]{2,1,0:T(8,128)}, u32[]{:S(2)}) copy-start(f32[2,224,128]{2,1,0:T(8,128)} %constant.8.clone.twiddle.refs_5_.refs_7_) | copy-start | bytes 688132
  16.5 0.9 %copy-start.5 = (f32[46656]{0:T(1024)S(1)}, f32[46656]{0:T(1024)}, u32[]{:S(2)}) copy-start(f32[46656]{0:T(1024)} %kernel_in.1) | copy-start | bytes 559876
  17.4 1.1 %copy-start.1 = (bf16[3,224,448]{2,1,0:T(8,128)(2,1)S(1)}, bf16[3,224,448]{2,1,0:T(8,128)(2,1)}, u32[]{:S(2)}) copy-start(bf16[3,224,448]{2,1,0:T(8,128)(2,1)} %constant.6.clone.left.refs_3_.refs_5_) | copy-start | bytes 1806340
  17.4 1.1 %copy-start.4 = (f32[2,224,128]{2,1,0:T(8,128)S(1)}, f32[2,224,128]{2,1,0:T(8,128)}, u32[]{:S(2)}) copy-start(f32[2,224,128]{2,1,0:T(8,128)} %constant.8.clone.twiddle.refs_5_.refs_7_) | copy-start | bytes 688132

commit v7 on v6

--- a/solution.py
+++ b/solution.py
@@ -74,22 +74,50 @@
 
 
 def pack(plan):
-    def body(orbital, occupation, out):
+    def body(orbital, fill, out):
         last = plan.tiles - 1
         for q in range(last):
             out[2 * q : 2 * q + 2, :] = orbital[:, LANES * q : LANES * (q + 1)]
         if plan.tail:
             out[2 * last :, : plan.tail] = orbital[:, LANES * last :]
-        fill = jnp.full((2, LANES - plan.tail), occupation[0], jnp.int32)
-        out[2 * last :, plan.tail :] = fill.astype(F32).astype(BF16)
+        out[2 * last :, plan.tail :] = fill[:, plan.tail :]
 
     return pl.pallas_call(
         body,
         out_shape=jax.ShapeDtypeStruct((2 * plan.tiles, LANES), BF16),
-        in_specs=[VMEM, SMEM],
+        in_specs=[VMEM, VMEM],
         out_specs=VMEM,
         compiler_params=pltpu.CompilerParams(vmem_limit_bytes=4 * 1024 * 1024),
         name="pack",
+    )
+
+
+def opening(cost):
+    def body(out):
+        out[...] = jnp.zeros((8, LANES), F32)
+
+    return pl.pallas_call(
+        body,
+        out_shape=jax.ShapeDtypeStruct((8, LANES), F32),
+        out_specs=VMEM,
+        cost_estimate=pl.CostEstimate(flops=cost, bytes_accessed=0, transcendentals=0),
+        compiler_params=pltpu.CompilerParams(vmem_limit_bytes=1024 * 1024),
+        name="opening",
+    )
+
+
+def spread():
+    def body(opened, occupation, out):
+        del opened
+        out[...] = jnp.full((2, LANES), occupation[0], jnp.int32).astype(F32).astype(BF16)
+
+    return pl.pallas_call(
+        body,
+        out_shape=jax.ShapeDtypeStruct((2, LANES), BF16),
+        in_specs=[VMEM, SMEM],
+        out_specs=VMEM,
+        compiler_params=pltpu.CompilerParams(vmem_limit_bytes=1024 * 1024),
+        name="spread",
     )
 
 
@@ -405,7 +433,7 @@
         ]
         return lax.ppermute(array, ("pool", "band"), pairs)
 
-    own = pack(plan)(orbitals[0, 0], occupation[0])
+    own = pack(plan)(orbitals[0, 0], spread()(opening(2000000000)(), occupation[0]))
     near = move(own, lambda p, g: ((p + 1) % pools, g))
     far = move(own, lambda p, g: ((p + 1) % pools, (g + 1) % groups) if g % 2 else (p, g + 1))
     partner = lambda p, g: (p, g ^ 1)

time: 22.4 us -> 18.2 us (0.81)
  local copies, waits for them, and re-layouts: 4.34 us -> 0.11 us
    unnamed x14 -> x10, local copies, waits for them, and re-layouts: 4.34 us -> 0.11 us
  transfers between devices with their start and end apart: 6 -> 6, of which waited for: 1 -> 1; matrix products, arithmetic and copies ran while one was open for 0% -> 0% of each run, Pallas kernels for 8% -> 10%
where the time goes in v7:
time: 18.2 us; the launch traced here: 18 us
  waiting for transfers between devices  6.38 us (35%)
  starting transfers between devices  5.56 us (31%)
  Pallas kernels  4.46 us (25%)
  between operations  1.51 us (8%)
    ppermute x6, waiting for transfers between devices, move(): return lax.ppermute(array, ('pool', 'band'), pairs)  6.38 us
    ppermute x6, starting transfers between devices, move(): return lax.ppermute(array, ('pool', 'band'), pairs)  5.56 us
    pallas_call x1, Pallas kernels, shards(): second_pair(plan, others)  2.43 us
    pallas_call x1, Pallas kernels, shards(): first_pair(plan, len(shifted))(mine, near, factor, *tables, *shifted)  1.1 us
    pallas_call x1, Pallas kernels, shards(): mine, pair, factor = prepare(plan)(own, pair_in, kernel, *tables)  0.69 us
  transfers between devices with their start and end apart: 6, of which 1 were waited for; matrix products, arithmetic and copies ran while one was open for 0% of the time, Pallas kernels for 10%

profile of v7, /device:TPU:0, one launch (start us, length us, event | category | flops | bytes accessed | tf_op | source)
XLA Modules:
  0.0 18.0 jit_solution(15659349011960602111)
XLA Ops:
  0.6 0.0 copy-start.4
  0.6 0.0 copy-start
  0.7 0.0 copy-start.2
  0.7 0.0 copy-start.3
  0.7 0.0 copy-start.1
  1.5 0.1 copy-done.4
  1.6 0.2 %pack.1.own_in = bf16[730,128]{1,0:T(8,128)(2,1)S(1)} custom-call(bf16[2,46656]{1,0:T(2,128)(2,1)S(1)} %bitcast.7, bf16[2,128]{1,0:T(2,128)(2,1)S(1)} %spread.1.fill), custom_call_target="tpu_custom_call" | custom-call | tf_op jit(solution)/shard_map/pack/pallas_call | solution.py:436
  1.8 3.0 %collective-permute-start.1 = (bf16[730,128]{1,0:T(8,128)(2,1)S(1)}, bf16[730,128]{1,0:T(8,128)(2,1)S(1)}, u32[]{:S(2)}, u32[]{:S(2)}) collective-permute-start(bf16[730,128]{1,0:T(8,128)(2,1)S(1)} %pack.1.own_in), channel_id=1, source_target_pairs={{0,4},{1,5},{2,6},{3,7},{4,8},{5,9},{6,10},{7,11},{8,12},{9,13},{1... | collective-permute-start | bytes 560648 | tf_op jit(solution)/shard_map/ppermute | solution.py:434
  4.8 1.5 %collective-permute-start.2 = (bf16[730,128]{1,0:T(8,128)(2,1)S(1)}, bf16[730,128]{1,0:T(8,128)(2,1)S(1)}, u32[]{:S(2)}, u32[]{:S(2)}) collective-permute-start(bf16[730,128]{1,0:T(8,128)(2,1)S(1)} %pack.1.own_in), channel_id=1, source_target_pairs={{0,2},{1,3},{2,0},{3,1},{4,6},{5,7},{6,4},{7,5},{8,10},{9,11},{10,... | collective-permute-start | bytes 560648 | tf_op jit(solution)/shard_map/ppermute | solution.py:434
  6.3 0.0 collective-permute-start
  6.3 0.5 %collective-permute-start.3 = (bf16[730,128]{1,0:T(8,128)(2,1)S(1)}, bf16[730,128]{1,0:T(8,128)(2,1)S(1)}, u32[]{:S(2)}, u32[]{:S(2)}) collective-permute-start(bf16[730,128]{1,0:T(8,128)(2,1)S(1)} %pack.1.own_in), channel_id=1, source_target_pairs={{0,1},{1,6},{2,3},{3,4},{4,5},{5,10},{6,7},{7,8},{8,9},{9,14},{10,... | collective-permute-start | bytes 560648 | tf_op jit(solution)/shard_map/ppermute | solution.py:434
  6.8 6.4 %collective-permute-done.1.refs_1_ = bf16[730,128]{1,0:T(8,128)(2,1)S(1)} collective-permute-done((bf16[730,128]{1,0:T(8,128)(2,1)S(1)}, bf16[730,128]{1,0:T(8,128)(2,1)S(1)}, u32[]{:S(2)}, u32[]{:S(2)}) %collective-permute-start.1) | collective-permute-done | bytes 186912 | tf_op jit(solution)/shard_map/ppermute | solution.py:434
  13.2 0.0 collective-permute-start.4
  13.2 0.0 collective-permute-done.2.refs_6_
  13.2 0.5 %collective-permute-start.5 = (bf16[730,128]{1,0:T(8,128)(2,1)S(1)}, bf16[730,128]{1,0:T(8,128)(2,1)S(1)}, u32[]{:S(2)}, u32[]{:S(2)}) collective-permute-start(bf16[730,128]{1,0:T(8,128)(2,1)S(1)} %collective-permute-done.2.refs_6_), channel_id=1, source_target_pairs={{0,1},{1,0},{2,3},{3,2},{4,5},{5,4},{6,7},{7,6},{8,9},{9,8},{10,11... | collective-permute-start | bytes 560648 | tf_op jit(solution)/shard_map/ppermute | solution.py:434
  13.7 0.0 collective-permute-done.pair_in
  13.7 0.0 copy-done
  13.7 0.0 copy-done.2
  13.7 0.0 copy-done.3
  13.8 0.0 copy-done.1
  13.8 0.7 %prepare.1 = (f32[2,448,128]{2,1,0:T(8,128)S(1)}, f32[2,448,128]{2,1,0:T(8,128)S(1)}, f32[448,128]{1,0:T(8,128)S(1)}) custom-call(bf16[730,128]{1,0:T(8,128)(2,1)S(1)} %pack.1.own_in, bf16[730,128]{1,0:T(8,128)(2,1)S(1)} %collective-permute-done.pair_in, f32[46656]{0:T(1024)S(1)} %copy-done.3, bf16[3,224,448]{2,1,0:T(8,128)(2,1)S(1)} %copy-done, ...), custom_call_target="tpu_custom_call" | custom-call | tf_op jit(solution)/shard_map/prepare/pallas_call | solution.py:447
  14.5 1.1 %first_pair.1 = (f32[2,448,128]{2,1,0:T(8,128)S(1)}, f32[2,448,128]{2,1,0:T(8,128)S(1)}) custom-call(f32[2,448,128]{2,1,0:T(8,128)S(1)} %get-tuple-element.9.refs_0_, bf16[730,128]{1,0:T(8,128)(2,1)S(1)} %collective-permute-done.1.refs_1_, f32[448,128]{1,0:T(8,128)S(1)} %get-tuple-element.10.refs_2_.refs_4_, bf16[3,224,448]{2,1,0:T(8,128)(2,1)S(1)} %copy-done, ...), custom_call_target="tpu_custom_call" | custom-call | tf_op jit(solution)/shard_map/first_pair/pallas_call | solution.py:448
  15.6 0.0 collective-permute-done.3.refs_2_
  15.6 0.0 collective-permute-done.4.refs_3_
  15.6 0.0 collective-permute-done.5.refs_10_
  15.6 2.4 %second_pair.1 = (bf16[2,46656]{1,0:T(2,128)(2,1)}, f32[2,1,4]{2,1,0:T(1,128)}) custom-call(f32[2,448,128]{2,1,0:T(8,128)S(1)} %get-tuple-element.9.refs_0_, f32[2,448,128]{2,1,0:T(8,128)S(1)} %get-tuple-element.11.refs_1_, bf16[730,128]{1,0:T(8,128)(2,1)S(1)} %collective-permute-done.3.refs_2_, bf16[730,128]{1,0:T(8,128)(2,1)S(1)} %collective-permute-done.4.refs_3_, ...), custom_call_target="tpu_custom_call" | custom-call | tf_op jit(solution)/shard_map/second_pair/pallas_call | solution.py:451
  (2 shorter events, 0.0 us)
Async XLA Ops:
  0.6 0.9 %copy-start.4 = (bf16[1,1,2,46656]{3,2,1,0:T(2,128)(2,1)S(1)}, bf16[1,1,2,46656]{3,2,1,0:T(2,128)(2,1)}, u32[]{:S(2)}) copy-start(bf16[1,1,2,46656]{3,2,1,0:T(2,128)(2,1)} %param.6) | copy-start | bytes 559876
  0.6 13.1 %copy-start = (bf16[3,224,448]{2,1,0:T(8,128)(2,1)S(1)}, bf16[3,224,448]{2,1,0:T(8,128)(2,1)}, u32[]{:S(2)}) copy-start(bf16[3,224,448]{2,1,0:T(8,128)(2,1)} %constant.6.clone.left.refs_3_.refs_5_) | copy-start | bytes 1806340
  0.7 13.1 %copy-start.2 = (f32[2,224,128]{2,1,0:T(8,128)S(1)}, f32[2,224,128]{2,1,0:T(8,128)}, u32[]{:S(2)}) copy-start(f32[2,224,128]{2,1,0:T(8,128)} %constant.8.clone.twiddle.refs_5_.refs_7_) | copy-start | bytes 688132
  0.7 13.1 %copy-start.3 = (f32[46656]{0:T(1024)S(1)}, f32[46656]{0:T(1024)}, u32[]{:S(2)}) copy-start(f32[46656]{0:T(1024)} %kernel_in.1) | copy-start | bytes 559876
  0.7 13.1 %copy-start.1 = (bf16[2,256,256]{2,1,0:T(8,128)(2,1)S(1)}, bf16[2,256,256]{2,1,0:T(8,128)(2,1)}, u32[]{:S(2)}) copy-start(bf16[2,256,256]{2,1,0:T(8,128)(2,1)} %constant.7.clone.right.refs_4_.refs_6_) | copy-start | bytes 786436
  1.8 11.4 %collective-permute-start.1 = (bf16[730,128]{1,0:T(8,128)(2,1)S(1)}, bf16[730,128]{1,0:T(8,128)(2,1)S(1)}, u32[]{:S(2)}, u32[]{:S(2)}) collective-permute-start(bf16[730,128]{1,0:T(8,128)(2,1)S(1)} %pack.1.own_in), channel_id=1, source_target_pairs={{0,4},{1,5},{2,6},{3,7},{4,8},{5,9},{6,10},{7,11},{8,12},{9,13},{1... | collective-permute-start | bytes 560648 | tf_op jit(solution)/shard_map/ppermute | solution.py:434
  4.8 8.4 %collective-permute-start.2 = (bf16[730,128]{1,0:T(8,128)(2,1)S(1)}, bf16[730,128]{1,0:T(8,128)(2,1)S(1)}, u32[]{:S(2)}, u32[]{:S(2)}) collective-permute-start(bf16[730,128]{1,0:T(8,128)(2,1)S(1)} %pack.1.own_in), channel_id=1, source_target_pairs={{0,2},{1,3},{2,0},{3,1},{4,6},{5,7},{6,4},{7,5},{8,10},{9,11},{10,... | collective-permute-start | bytes 560648 | tf_op jit(solution)/shard_map/ppermute | solution.py:434
  6.3 7.4 %collective-permute-start = (bf16[730,128]{1,0:T(8,128)(2,1)S(1)}, bf16[730,128]{1,0:T(8,128)(2,1)S(1)}, u32[]{:S(2)}, u32[]{:S(2)}) collective-permute-start(bf16[730,128]{1,0:T(8,128)(2,1)S(1)} %pack.1.own_in), channel_id=1, source_target_pairs={{0,1},{1,0},{2,3},{3,2},{4,5},{5,4},{6,7},{7,6},{8,9},{9,8},{10,11... | collective-permute-start | bytes 560648 | tf_op jit(solution)/shard_map/ppermute | solution.py:434
  6.3 9.2 %collective-permute-start.3 = (bf16[730,128]{1,0:T(8,128)(2,1)S(1)}, bf16[730,128]{1,0:T(8,128)(2,1)S(1)}, u32[]{:S(2)}, u32[]{:S(2)}) collective-permute-start(bf16[730,128]{1,0:T(8,128)(2,1)S(1)} %pack.1.own_in), channel_id=1, source_target_pairs={{0,1},{1,6},{2,3},{3,4},{4,5},{5,10},{6,7},{7,8},{8,9},{9,14},{10,... | collective-permute-start | bytes 560648 | tf_op jit(solution)/shard_map/ppermute | solution.py:434
  13.2 2.4 %collective-permute-start.4 = (bf16[730,128]{1,0:T(8,128)(2,1)S(1)}, bf16[730,128]{1,0:T(8,128)(2,1)S(1)}, u32[]{:S(2)}, u32[]{:S(2)}) collective-permute-start(bf16[730,128]{1,0:T(8,128)(2,1)S(1)} %collective-permute-done.1.refs_1_), channel_id=1, source_target_pairs={{0,1},{1,0},{2,3},{3,2},{4,5},{5,4},{6,7},{7,6},{8,9},{9,8},{10,11... | collective-permute-start | bytes 560648 | tf_op jit(solution)/shard_map/ppermute | solution.py:434
  13.2 2.4 %collective-permute-start.5 = (bf16[730,128]{1,0:T(8,128)(2,1)S(1)}, bf16[730,128]{1,0:T(8,128)(2,1)S(1)}, u32[]{:S(2)}, u32[]{:S(2)}) collective-permute-start(bf16[730,128]{1,0:T(8,128)(2,1)S(1)} %collective-permute-done.2.refs_6_), channel_id=1, source_target_pairs={{0,1},{1,0},{2,3},{3,2},{4,5},{5,4},{6,7},{7,6},{8,9},{9,8},{10,11... | collective-permute-start | bytes 560648 | tf_op jit(solution)/shard_map/ppermute | solution.py:434

commit v8 on v7

--- a/solution.py
+++ b/solution.py
@@ -360,12 +360,11 @@
     def body(*refs):
         own, accum, far_in, near_in, kernel, left, right, twiddle, pair = refs[:9]
         extra = (others - 1) // 2
-        shifted = refs[9 : 9 + extra]
-        crossed = refs[9 + extra : 9 + 2 * extra]
+        bands = refs[9 : 9 + 2 * extra]
         out, gram, tiles, near, fourier, total, flat, small, sent, spare, *matrices = refs[8 + others :]
         here = lax.axis_index("band")
         packed = jnp.where(here % 2 == 1, near_in[...], far_in[...])
-        for band, matrix in zip(crossed, matrices):
+        for band, matrix in zip(bands, matrices):
             to_matrix(plan, band[...], spare, matrix)
         results = exchange(plan, own, packed, tiles, near, fourier, kernel, left, right, twiddle)
         for part, real, imag in results:
@@ -373,7 +372,7 @@
             total[1, part, :] = (accum[1, part, :] + imag).astype(BF16).astype(F32)
         pairs = [(here, own), (here ^ 1, pair)]
         for step in range(1, count // 2):
-            for start, matrix in ((here, shifted[step - 1]), (here ^ 1, matrices[step - 1])):
+            for start, matrix in ((here, matrices[step - 1]), (here ^ 1, matrices[extra + step - 1])):
                 source = start - 2 * step
                 pairs.append((jnp.where(source < 0, source + count, source), matrix))
         sums = overlaps(plan, count, total, pairs)
@@ -412,7 +411,7 @@
             pltpu.SemaphoreType.DMA((2,)),
             pltpu.VMEM((2 * plan.padded_tiles, LANES), F32),
         ]
-        + [pltpu.VMEM((2, plan.kept, LANES), F32)] * ((others - 1) // 2),
+        + [pltpu.VMEM((2, plan.kept, LANES), F32)] * (others - 1),
         compiler_params=pltpu.CompilerParams(vmem_limit_bytes=16 * 1024 * 1024),
         name="second_pair",
     )
@@ -445,11 +444,9 @@
     swapped = move(near, partner)
     tables = constants(plan)
     mine, pair, factor = prepare(plan)(own, pair_in, kernel, *tables)
-    accum, *matrices = first_pair(plan, len(shifted))(
-        mine, near, factor, *tables, *shifted
-    )
+    (accum,) = first_pair(plan, 0)(mine, near, factor, *tables)
     exchanged, gram = second_pair(plan, others)(
-        mine, accum, far, swapped, factor, *tables, pair, *matrices, *crossed
+        mine, accum, far, swapped, factor, *tables, pair, *shifted, *crossed
     )
     return exchanged[None, None], jnp.swapaxes(gram, 1, 2)[None]
 

time: 18.2 us -> 18.2 us (level)
  no operation moved by 1% of the time
where the time goes in v8:
time: 18.2 us; the launch traced here: 18 us
  waiting for transfers between devices  6.39 us (35%)
  starting transfers between devices  5.56 us (31%)
  Pallas kernels  4.47 us (25%)
  between operations  1.51 us (8%)
    ppermute x6, waiting for transfers between devices, move(): return lax.ppermute(array, ('pool', 'band'), pairs)  6.39 us
    ppermute x6, starting transfers between devices, move(): return lax.ppermute(array, ('pool', 'band'), pairs)  5.56 us
    pallas_call x1, Pallas kernels, shards(): second_pair(plan, others)  2.45 us
    pallas_call x1, Pallas kernels, shards(): accum, = first_pair(plan, 0)(mine, near, factor, *tables)  1.08 us
    pallas_call x1, Pallas kernels, shards(): mine, pair, factor = prepare(plan)(own, pair_in, kernel, *tables)  0.69 us
  transfers between devices with their start and end apart: 6, of which 1 were waited for; matrix products, arithmetic and copies ran while one was open for 0% of the time, Pallas kernels for 10%

profile of v8, /device:TPU:0, one launch (start us, length us, event | category | flops | bytes accessed | tf_op | source)
XLA Modules:
  0.0 18.0 jit_solution(3976168391730262041)
XLA Ops:
  0.6 0.0 copy-start.4
  0.6 0.0 copy-start
  0.7 0.0 copy-start.2
  0.7 0.0 copy-start.3
  0.7 0.0 copy-start.1
  1.5 0.1 copy-done.4
  1.6 0.2 %pack.1.own_in = bf16[730,128]{1,0:T(8,128)(2,1)S(1)} custom-call(bf16[2,46656]{1,0:T(2,128)(2,1)S(1)} %bitcast.7, bf16[2,128]{1,0:T(2,128)(2,1)S(1)} %spread.1.fill), custom_call_target="tpu_custom_call" | custom-call | tf_op jit(solution)/shard_map/pack/pallas_call | solution.py:435
  1.8 3.0 %collective-permute-start.1 = (bf16[730,128]{1,0:T(8,128)(2,1)S(1)}, bf16[730,128]{1,0:T(8,128)(2,1)S(1)}, u32[]{:S(2)}, u32[]{:S(2)}) collective-permute-start(bf16[730,128]{1,0:T(8,128)(2,1)S(1)} %pack.1.own_in), channel_id=1, source_target_pairs={{0,4},{1,5},{2,6},{3,7},{4,8},{5,9},{6,10},{7,11},{8,12},{9,13},{1... | collective-permute-start | bytes 560648 | tf_op jit(solution)/shard_map/ppermute | solution.py:433
  4.8 1.5 %collective-permute-start.4 = (bf16[730,128]{1,0:T(8,128)(2,1)S(1)}, bf16[730,128]{1,0:T(8,128)(2,1)S(1)}, u32[]{:S(2)}, u32[]{:S(2)}) collective-permute-start(bf16[730,128]{1,0:T(8,128)(2,1)S(1)} %pack.1.own_in), channel_id=1, source_target_pairs={{0,2},{1,3},{2,0},{3,1},{4,6},{5,7},{6,4},{7,5},{8,10},{9,11},{10,... | collective-permute-start | bytes 560648 | tf_op jit(solution)/shard_map/ppermute | solution.py:433
  6.3 0.0 collective-permute-start
  6.3 0.5 %collective-permute-start.2 = (bf16[730,128]{1,0:T(8,128)(2,1)S(1)}, bf16[730,128]{1,0:T(8,128)(2,1)S(1)}, u32[]{:S(2)}, u32[]{:S(2)}) collective-permute-start(bf16[730,128]{1,0:T(8,128)(2,1)S(1)} %pack.1.own_in), channel_id=1, source_target_pairs={{0,1},{1,6},{2,3},{3,4},{4,5},{5,10},{6,7},{7,8},{8,9},{9,14},{10,... | collective-permute-start | bytes 560648 | tf_op jit(solution)/shard_map/ppermute | solution.py:433
  6.8 6.4 %collective-permute-done.1.refs_1_ = bf16[730,128]{1,0:T(8,128)(2,1)S(1)} collective-permute-done((bf16[730,128]{1,0:T(8,128)(2,1)S(1)}, bf16[730,128]{1,0:T(8,128)(2,1)S(1)}, u32[]{:S(2)}, u32[]{:S(2)}) %collective-permute-start.1) | collective-permute-done | bytes 186912 | tf_op jit(solution)/shard_map/ppermute | solution.py:433
  13.2 0.0 collective-permute-start.3
  13.2 0.0 collective-permute-done.4.refs_9_
  13.2 0.5 %collective-permute-start.5 = (bf16[730,128]{1,0:T(8,128)(2,1)S(1)}, bf16[730,128]{1,0:T(8,128)(2,1)S(1)}, u32[]{:S(2)}, u32[]{:S(2)}) collective-permute-start(bf16[730,128]{1,0:T(8,128)(2,1)S(1)} %collective-permute-done.4.refs_9_), channel_id=1, source_target_pairs={{0,1},{1,0},{2,3},{3,2},{4,5},{5,4},{6,7},{7,6},{8,9},{9,8},{10,11... | collective-permute-start | bytes 560648 | tf_op jit(solution)/shard_map/ppermute | solution.py:433
  13.7 0.0 collective-permute-done.pair_in
  13.7 0.0 copy-done
  13.7 0.0 copy-done.2
  13.7 0.0 copy-done.3
  13.8 0.0 copy-done.1
  13.8 0.7 %prepare.1 = (f32[2,448,128]{2,1,0:T(8,128)S(1)}, f32[2,448,128]{2,1,0:T(8,128)S(1)}, f32[448,128]{1,0:T(8,128)S(1)}) custom-call(bf16[730,128]{1,0:T(8,128)(2,1)S(1)} %pack.1.own_in, bf16[730,128]{1,0:T(8,128)(2,1)S(1)} %collective-permute-done.pair_in, f32[46656]{0:T(1024)S(1)} %copy-done.3, bf16[3,224,448]{2,1,0:T(8,128)(2,1)S(1)} %copy-done, ...), custom_call_target="tpu_custom_call" | custom-call | tf_op jit(solution)/shard_map/prepare/pallas_call | solution.py:446
  14.5 1.1 %first_pair.1.refs_1_ = f32[2,448,128]{2,1,0:T(8,128)S(1)} custom-call(f32[2,448,128]{2,1,0:T(8,128)S(1)} %get-tuple-element.7.refs_0_, bf16[730,128]{1,0:T(8,128)(2,1)S(1)} %collective-permute-done.1.refs_1_, f32[448,128]{1,0:T(8,128)S(1)} %get-tuple-element.8.refs_2_.refs_4_, bf16[3,224,448]{2,1,0:T(8,128)(2,1)S(1)} %copy-done, ...), custom_call_target="tpu_custom_call" | custom-call | tf_op jit(solution)/shard_map/first_pair/pallas_call | solution.py:447
  15.6 0.0 collective-permute-done.2.refs_2_
  15.6 0.0 collective-permute-done.3.refs_3_
  15.6 0.0 collective-permute-done.5.refs_10_
  15.6 2.5 %second_pair.1 = (bf16[2,46656]{1,0:T(2,128)(2,1)}, f32[2,1,4]{2,1,0:T(1,128)}) custom-call(f32[2,448,128]{2,1,0:T(8,128)S(1)} %get-tuple-element.7.refs_0_, f32[2,448,128]{2,1,0:T(8,128)S(1)} %first_pair.1.refs_1_, bf16[730,128]{1,0:T(8,128)(2,1)S(1)} %collective-permute-done.2.refs_2_, bf16[730,128]{1,0:T(8,128)(2,1)S(1)} %collective-permute-done.3.refs_3_, ...), custom_call_target="tpu_custom_call" | custom-call | tf_op jit(solution)/shard_map/second_pair/pallas_call | solution.py:448
  (2 shorter events, 0.0 us)
Async XLA Ops:
  0.6 0.9 %copy-start.4 = (bf16[1,1,2,46656]{3,2,1,0:T(2,128)(2,1)S(1)}, bf16[1,1,2,46656]{3,2,1,0:T(2,128)(2,1)}, u32[]{:S(2)}) copy-start(bf16[1,1,2,46656]{3,2,1,0:T(2,128)(2,1)} %param.6) | copy-start | bytes 559876
  0.6 13.1 %copy-start = (bf16[3,224,448]{2,1,0:T(8,128)(2,1)S(1)}, bf16[3,224,448]{2,1,0:T(8,128)(2,1)}, u32[]{:S(2)}) copy-start(bf16[3,224,448]{2,1,0:T(8,128)(2,1)} %constant.6.clone.left.refs_3_.refs_5_) | copy-start | bytes 1806340
  0.7 13.1 %copy-start.2 = (f32[2,224,128]{2,1,0:T(8,128)S(1)}, f32[2,224,128]{2,1,0:T(8,128)}, u32[]{:S(2)}) copy-start(f32[2,224,128]{2,1,0:T(8,128)} %constant.8.clone.twiddle.refs_5_.refs_7_) | copy-start | bytes 688132
  0.7 13.1 %copy-start.3 = (f32[46656]{0:T(1024)S(1)}, f32[46656]{0:T(1024)}, u32[]{:S(2)}) copy-start(f32[46656]{0:T(1024)} %kernel_in.1) | copy-start | bytes 559876
  0.7 13.1 %copy-start.1 = (bf16[2,256,256]{2,1,0:T(8,128)(2,1)S(1)}, bf16[2,256,256]{2,1,0:T(8,128)(2,1)}, u32[]{:S(2)}) copy-start(bf16[2,256,256]{2,1,0:T(8,128)(2,1)} %constant.7.clone.right.refs_4_.refs_6_) | copy-start | bytes 786436
  1.8 11.4 %collective-permute-start.1 = (bf16[730,128]{1,0:T(8,128)(2,1)S(1)}, bf16[730,128]{1,0:T(8,128)(2,1)S(1)}, u32[]{:S(2)}, u32[]{:S(2)}) collective-permute-start(bf16[730,128]{1,0:T(8,128)(2,1)S(1)} %pack.1.own_in), channel_id=1, source_target_pairs={{0,4},{1,5},{2,6},{3,7},{4,8},{5,9},{6,10},{7,11},{8,12},{9,13},{1... | collective-permute-start | bytes 560648 | tf_op jit(solution)/shard_map/ppermute | solution.py:433
  4.8 8.4 %collective-permute-start.4 = (bf16[730,128]{1,0:T(8,128)(2,1)S(1)}, bf16[730,128]{1,0:T(8,128)(2,1)S(1)}, u32[]{:S(2)}, u32[]{:S(2)}) collective-permute-start(bf16[730,128]{1,0:T(8,128)(2,1)S(1)} %pack.1.own_in), channel_id=1, source_target_pairs={{0,2},{1,3},{2,0},{3,1},{4,6},{5,7},{6,4},{7,5},{8,10},{9,11},{10,... | collective-permute-start | bytes 560648 | tf_op jit(solution)/shard_map/ppermute | solution.py:433
  6.3 7.4 %collective-permute-start = (bf16[730,128]{1,0:T(8,128)(2,1)S(1)}, bf16[730,128]{1,0:T(8,128)(2,1)S(1)}, u32[]{:S(2)}, u32[]{:S(2)}) collective-permute-start(bf16[730,128]{1,0:T(8,128)(2,1)S(1)} %pack.1.own_in), channel_id=1, source_target_pairs={{0,1},{1,0},{2,3},{3,2},{4,5},{5,4},{6,7},{7,6},{8,9},{9,8},{10,11... | collective-permute-start | bytes 560648 | tf_op jit(solution)/shard_map/ppermute | solution.py:433
  6.3 9.2 %collective-permute-start.2 = (bf16[730,128]{1,0:T(8,128)(2,1)S(1)}, bf16[730,128]{1,0:T(8,128)(2,1)S(1)}, u32[]{:S(2)}, u32[]{:S(2)}) collective-permute-start(bf16[730,128]{1,0:T(8,128)(2,1)S(1)} %pack.1.own_in), channel_id=1, source_target_pairs={{0,1},{1,6},{2,3},{3,4},{4,5},{5,10},{6,7},{7,8},{8,9},{9,14},{10,... | collective-permute-start | bytes 560648 | tf_op jit(solution)/shard_map/ppermute | solution.py:433
  13.2 2.3 %collective-permute-start.3 = (bf16[730,128]{1,0:T(8,128)(2,1)S(1)}, bf16[730,128]{1,0:T(8,128)(2,1)S(1)}, u32[]{:S(2)}, u32[]{:S(2)}) collective-permute-start(bf16[730,128]{1,0:T(8,128)(2,1)S(1)} %collective-permute-done.1.refs_1_), channel_id=1, source_target_pairs={{0,1},{1,0},{2,3},{3,2},{4,5},{5,4},{6,7},{7,6},{8,9},{9,8},{10,11... | collective-permute-start | bytes 560648 | tf_op jit(solution)/shard_map/ppermute | solution.py:433
  13.2 2.3 %collective-permute-start.5 = (bf16[730,128]{1,0:T(8,128)(2,1)S(1)}, bf16[730,128]{1,0:T(8,128)(2,1)S(1)}, u32[]{:S(2)}, u32[]{:S(2)}) collective-permute-start(bf16[730,128]{1,0:T(8,128)(2,1)S(1)} %collective-permute-done.4.refs_9_), channel_id=1, source_target_pairs={{0,1},{1,0},{2,3},{3,2},{4,5},{5,4},{6,7},{7,6},{8,9},{9,8},{10,11... | collective-permute-start | bytes 560648 | tf_op jit(solution)/shard_map/ppermute | solution.py:433
